TPU v7x, 32 devices: a whole 2x2x4 slice. The times are simulated.
32 devices in a mesh: member: 2 (over x), tensor: 4 (over y, core), answer: 4 (over z).
Axes of the slice: x: 2, y: 2, z: 4, core: 2. Of those that a mesh axis runs over, the one named last changes fastest.
Arguments:
- master: float32 [5120, 13824], P('member', ('tensor', 'answer')), may hold values from -6 to 6
- left_noise: bfloat16 [256, 5120], P(('member', 'answer')), may hold values from -5 to 5
- right_noise: bfloat16 [256, 13824], P(('member', 'answer'), 'tensor'), may hold values from -5 to 5
- returns: float32 [256, 512], P('member', 'answer'), may hold values from -12 to 12
Outputs:
- new_master: float32 [5120, 13824], P('member', ('tensor', 'answer'))
- rollout: bfloat16 [5120, 13824], P(('member', 'answer'), 'tensor')
All inputs are finite; a program needn't handle non-finite values.
Results may differ from a plain program's by a relative error of at most 0.01.
Values may be sent and summed in bfloat16 or wider, within the bound.
A program may use at most 64 MiB of HBM per device.

v0:
```python
import jax
import jax.numpy as jnp
from jax import lax
from jax.experimental import pallas as pl
from jax.experimental.pallas import tpu as pltpu
from jax.sharding import PartitionSpec as P


def contract(left_tile, accum, pieces):
    right_cols, weights = pieces
    weighted = left_tile.astype(jnp.float32) * weights[:, None]
    return accum + lax.dot_general(
        weighted,
        right_cols.astype(jnp.float32),
        (((0,), (0,)), ((), ())),
        precision=lax.Precision.HIGHEST,
    )


def plain_body(master, left_noise, right_noise, returns):
    member_count = lax.axis_size("member")
    answer_count = lax.axis_size("answer")
    partial_value = jnp.sum(returns, axis=1)
    block_len = partial_value.shape[0]
    population = block_len * member_count
    scores = lax.psum(partial_value, "answer")
    score_sum, square_sum = lax.psum((jnp.sum(scores), jnp.sum(scores * scores)), "member")
    average = score_sum / population
    variance = square_sum / population - average * average
    fitness = (scores - average) / jnp.sqrt(variance + 1e-05)
    tile_rows = master.shape[0]
    local_members = left_noise.shape[0]
    restricted = lax.all_to_all(left_noise, "member", split_axis=1, concat_axis=0, tiled=True)
    gathered_rows = lax.all_gather(restricted, "answer", axis=0, tiled=True)
    width = gathered_rows.shape[1]
    left_tile = gathered_rows.reshape(answer_count, member_count, local_members, width)
    left_tile = jnp.transpose(left_tile, (1, 0, 2, 3)).reshape(
        answer_count * member_count * local_members, width
    )
    right_block = lax.all_to_all(right_noise, "answer", split_axis=1, concat_axis=0, tiled=True)
    initial = jnp.zeros((tile_rows, right_block.shape[1]), jnp.float32)
    update = contract(
        left_tile,
        initial,
        (
            lax.all_gather(right_block, "member", axis=0, tiled=True),
            lax.all_gather(fitness.astype(jnp.bfloat16), "member", axis=0, tiled=True).astype(
                jnp.float32
            ),
        ),
    )
    new_master = master + update / jnp.sqrt(jnp.float32(population))
    rollout = lax.all_to_all(
        new_master.astype(jnp.bfloat16), "answer", split_axis=0, concat_axis=1, tiled=True
    )
    return (new_master, rollout)


def exchange_kernel(members, chunks, left_ref, right_ref, returns_ref, master_ref, *refs):
    sides = 3
    l_ref, r_ref, s_ref, p_ref, e_ref, *refs = refs
    blocks, refs = refs[:sides * len(chunks)], refs[sides * len(chunks):]
    (wide, narrow, part, own_sem, pull_sem, push_sem, s_send, s_recv, x_send, x_recv, f_send, f_recv,
     z_send, z_recv, q_send, q_recv, y_send, y_recv, e_send, e_recv) = refs
    me, te, an = lax.axis_index("member"), lax.axis_index("tensor"), lax.axis_index("answer")
    answers = 4
    local = left_ref.shape[0]
    slab = local * members
    tile = l_ref.shape[1]
    piece = tile // 4
    rows = tile // answers
    beside = lambda i: i + 1 - 2 * lax.rem(i, 2)
    other, core, across = 1 - me, beside(te), lax.rem(te + 2, 4)
    near, far = beside(an), 2 - lax.div(an, 2)
    beyond = 2 * (1 - lax.div(an, 2))
    inner = lax.div(an + 1, 2) == 1
    pair = {1: near, 2: lax.rem(an + 2, answers), 3: answers - 1 - an}

    def l_at(start, count, t):
        return l_ref.at[pl.ds(pl.multiple_of(start, local), count), pl.ds(pl.multiple_of(t * piece, piece), piece)]

    def l_slab(a, t):
        return l_at(a * slab, slab, t)

    def r_at(a, m):
        return r_ref.at[pl.ds(pl.multiple_of((a * members + m) * local, local), local), :]

    def remote(src, dst, send, recv, where):
        return pltpu.make_async_remote_copy(src_ref=src, dst_ref=dst, send_sem=send, recv_sem=recv,
                                            device_id=where, device_id_type=pl.DeviceIdType.MESH)

    def pull(x):
        return pltpu.make_async_copy(
            master_ref.at[:, pl.ds(pl.multiple_of(pair[x] * rows, rows), rows)], wide.at[x % 2], pull_sem.at[x - 1])

    def push(x, c):
        at = sum(chunks[:c])
        return pltpu.make_async_copy(
            narrow.at[x % 2, :, at:at + chunks[c]], blocks[(x - 1) * len(chunks) + c], push_sem.at[x - 1, c])

    def cast(x):
        pull(x).wait()
        step = 96

        def one(i, _):
            at = pl.ds(pl.multiple_of(i * step, step), step)
            narrow[x % 2, at, :] = wide[x % 2, at, :].astype(narrow.dtype)
            return 0

        lax.fori_loop(0, narrow.shape[1] // step, one, 0)
        for c in range(len(chunks)):
            push(x, c).start()

    pull(3).start()
    pull(2).start()
    own_l = pltpu.make_async_copy(
        left_ref.at[:, pl.ds(pl.multiple_of(me * tile + te * piece, piece), piece)],
        l_at((an * members + me) * local, local, te), own_sem.at[0])
    own_r = pltpu.make_async_copy(right_ref, r_at(an, me), own_sem.at[1])
    own_l.start()
    own_r.start()
    part[...] = jnp.sum(returns_ref[...].T, axis=0, keepdims=True)
    own_p = pltpu.make_async_copy(part, p_ref, own_sem.at[2])
    own_s = pltpu.make_async_copy(part, s_ref.at[an * members + me], own_sem.at[3])
    own_p.start()
    own_s.start()

    barrier = pltpu.get_barrier_semaphore()
    peers = [(dm, da) for dm in range(members) for da in range(answers) if (dm, da) != (0, 0)]
    place = lambda dm, da: {"member": lax.rem(me + dm, members), "answer": lax.rem(an + da, answers)}
    for dm, da in peers:
        pl.semaphore_signal(barrier, inc=1, device_id=place(dm, da), device_id_type=pl.DeviceIdType.MESH)
    for t in (core, across):
        pl.semaphore_signal(barrier, inc=1, device_id={"tensor": t}, device_id_type=pl.DeviceIdType.MESH)
    pl.semaphore_wait(barrier, len(peers) + 2)

    mine = lax.rem(an, 2)
    r_near = remote(right_ref, r_at(an, me), z_send.at[0], z_recv.at[0], {"answer": near})
    r_far = remote(right_ref, r_at(an, me), z_send.at[1], z_recv.at[1 + mine], {"answer": far})
    l_over = remote(left_ref.at[:, pl.ds(pl.multiple_of(other * tile + te * piece, piece), piece)],
                    l_at((an * members + me) * local, local, te), x_send.at[0], x_recv.at[0], {"member": other})
    forward = {0: remote(right_ref, r_at(an, me), f_send.at[0], f_recv.at[0], {"member": other})}
    l_over.start()
    r_far.start()
    r_near.start()
    forward[0].start()
    own_p.wait()
    scores = []
    for i, (dm, da) in enumerate(peers):
        copy = remote(p_ref, s_ref.at[an * members + me], s_send.at[i], s_recv.at[i], place(dm, da))
        copy.start()
        scores.append(copy)
    own_l.wait()
    l_over.wait_recv()
    l_near = remote(l_slab(an, te), l_slab(an, te), q_send.at[0], q_recv.at[0], {"answer": near})
    l_far = remote(l_slab(an, te), l_slab(an, te), q_send.at[1], q_recv.at[1 + mine], {"answer": far})
    l_far.start()
    l_near.start()
    cast(3)
    push(3, 0).wait()
    early = remote(blocks[2 * len(chunks)], e_ref, e_send, e_recv, {"answer": pair[3]})
    early.start()
    for c in range(1, len(chunks)):
        push(3, c).wait()
    pull(1).start()
    cast(2)
    cast(1)

    sources = (near, beyond, beyond + 1)
    r_relays, l_relays = {}, {}
    for k, source in enumerate(sources):
        block = r_at(source, me)
        remote(block, block, z_send.at[0], z_recv.at[k], {"answer": near}).wait_recv()
        forward[k + 1] = remote(block, block, f_send.at[k + 1], f_recv.at[k + 1], {"member": other})
        forward[k + 1].start()
        if k:
            r_relays[k] = remote(block, block, z_send.at[1 + k], z_recv.at[k], {"answer": near})
            pl.when(inner)(r_relays[k].start)
        block = l_slab(source, te)
        remote(block, block, q_send.at[0], q_recv.at[k], {"answer": near}).wait_recv()
        if k:
            l_relays[k] = remote(block, block, q_send.at[1 + k], q_recv.at[k], {"answer": near})
            pl.when(inner)(l_relays[k].start)
    total = slab * answers
    l_y = remote(l_at(0, total, te), l_at(0, total, te), y_send.at[0], y_recv.at[0], {"tensor": across})
    l_c = remote(l_at(0, total, te), l_at(0, total, te), y_send.at[1], y_recv.at[1], {"tensor": core})
    l_y.start()
    l_c.start()
    block = l_at(0, total, across)
    remote(block, block, y_send.at[0], y_recv.at[0], {"tensor": across}).wait_recv()
    l_d = remote(block, block, y_send.at[2], y_recv.at[2], {"tensor": core})
    l_d.start()
    for i, (dm, da) in enumerate(peers):
        block = s_ref.at[lax.rem(an + answers - da, answers) * members + lax.rem(me + members - dm, members)]
        remote(block, block, s_send.at[i], s_recv.at[i], {"member": other}).wait_recv()
    for k, source in enumerate((an,) + sources):
        block = r_at(source, other)
        remote(block, block, f_send.at[k], f_recv.at[k], {"member": other}).wait_recv()
    for k, t in ((1, core), (2, 3 - te)):
        block = l_at(0, total, t)
        remote(block, block, y_send.at[k], y_recv.at[k], {"tensor": core}).wait_recv()
    own_r.wait()
    own_s.wait()
    for x in (2, 1):
        for c in range(len(chunks)):
            push(x, c).wait()
    for copy in [r_near, r_far, l_over, l_near, l_far, l_y, l_c, l_d] + scores + list(forward.values()):
        copy.wait_send()
    for copy in list(r_relays.values()) + list(l_relays.values()):
        pl.when(inner)(copy.wait_send)
    early.wait_recv()
    early.wait_send()


def exchange(left_noise, right_noise, returns, transposed, members, chunks):
    answers, sides = 4, 3
    local, width = right_noise.shape
    cols, tile = transposed.shape
    total = local * members * answers
    count = members * answers
    block = returns.shape[0]
    half = left_noise.dtype
    dma = pltpu.SemaphoreType.DMA
    vmem, anywhere = pl.BlockSpec(memory_space=pltpu.VMEM), pl.BlockSpec(memory_space=pl.ANY)
    shape = jax.ShapeDtypeStruct
    return pl.pallas_call(
        lambda *refs: exchange_kernel(members, chunks, *refs),
        out_shape=(
            shape((total, tile), half),
            shape((total, width), half),
            shape((count, 1, block), jnp.float32),
            shape((1, block), jnp.float32),
            shape((cols, chunks[0]), half),
        ) + tuple(shape((cols, size), half) for _ in range(sides) for size in chunks),
        in_specs=[vmem] * 3 + [anywhere],
        out_specs=(anywhere,) * (5 + sides * len(chunks)),
        scratch_shapes=[
            pltpu.VMEM((2, cols, tile // answers), jnp.float32), pltpu.VMEM((2, cols, tile // answers), half),
            pltpu.VMEM((1, block), jnp.float32),
            dma((4,)), dma((sides,)), dma((sides, len(chunks))), dma((count - 1,)), dma((count - 1,)),
            dma((1,)), dma((1,)), dma((answers,)), dma((answers,)),
            dma((4,)), dma((3,)), dma((4,)), dma((3,)), dma((3,)), dma((3,)), dma, dma,
        ],
        compiler_params=pltpu.CompilerParams(collective_id=0, has_side_effects=True),
        name="exchange",
    )(left_noise, right_noise, returns, transposed)


def divisor(size, least, most):
    fits = [n for n in range(least, most + 1, least) if size % n == 0]
    return fits[-1] if fits else size


def final_kernel(where_ref, master_ref, one_ref, two_ref, three_ref, left_ref, right_ref, *refs):
    out_ref, stack = refs[-2:]
    an = lax.axis_index("answer")
    width, rows = master_ref.shape
    near = an + 1 - 2 * lax.rem(an, 2)
    parts = ((an, master_ref), (near, one_ref), (lax.rem(an + 2, 4), two_ref), (3 - an, three_ref))
    for a, ref in parts:
        stack[pl.ds(pl.multiple_of(a * width, 16), width), :] = ref[...].astype(stack.dtype)
    row = lax.broadcasted_iota(jnp.int32, (rows, rows), 0)
    col = lax.broadcasted_iota(jnp.int32, (rows, rows), 1)
    unit = jnp.where(row == col, 1.0, 0.0).astype(stack.dtype)
    step = divisor(out_ref.shape[1], 128, 512)
    for at in range(0, out_ref.shape[1], step):
        cols = slice(at, at + step)
        new = jnp.dot(left_ref[...], right_ref[:, cols], preferred_element_type=jnp.float32)
        old = lax.dot_general(unit, stack[cols, :], (((1,), (1,)), ((), ())), preferred_element_type=jnp.float32)
        out_ref[:, cols] = (new + old).astype(out_ref.dtype)


def finalize(where, transposed, sides, left, right, first, size, so_far):
    rows, members = left.shape
    width = transposed.shape[0]
    total = right.shape[1]
    chunk = 128
    start, steps = first // chunk, size // chunk
    per = rows // chunk
    side = pl.BlockSpec((width, chunk), lambda i, w: (0, i))
    more = [] if so_far is None else [so_far]
    return pl.pallas_call(
        final_kernel,
        grid_spec=pltpu.PrefetchScalarGridSpec(
            num_scalar_prefetch=1,
            grid=(steps,),
            in_specs=[
                pl.BlockSpec((width, chunk), lambda i, w: (0, w[0] * per + start + i)),
                side, side, side,
                pl.BlockSpec((chunk, members), lambda i, w: (start + i, 0)),
                pl.BlockSpec((members, total), lambda i, w: (0, 0)),
            ] + [pl.BlockSpec(memory_space=pl.ANY)] * len(more),
            out_specs=pl.BlockSpec((chunk, total), lambda i, w: (start + i, 0)),
            scratch_shapes=[pltpu.VMEM((total, chunk), jnp.bfloat16)],
        ),
        out_shape=jax.ShapeDtypeStruct((rows, total), jnp.bfloat16),
        input_output_aliases={7: 0} if more else {},
        cost_estimate=pl.CostEstimate(
            flops=2 * size * total * (members + chunk), bytes_accessed=6 * size * total, transcendentals=0),
        name="final",
    )(where, transposed, *sides, left, right, *more)


def update_kernel(master_ref, right_ref, left_ref, new_ref):
    new_ref[...] = master_ref[...] + jnp.dot(right_ref[...], left_ref[...], preferred_element_type=jnp.float32)


def update(transposed, right, left):
    width, tile = transposed.shape
    members = right.shape[1]
    chunk = divisor(width, 16, 150)
    return pl.pallas_call(
        update_kernel,
        grid=(width // chunk,),
        in_specs=[
            pl.BlockSpec((chunk, tile), lambda i: (i, 0)),
            pl.BlockSpec((chunk, members), lambda i: (i, 0)),
            pl.BlockSpec((members, tile), lambda i: (0, 0)),
        ],
        out_specs=pl.BlockSpec((chunk, tile), lambda i: (i, 0)),
        out_shape=jax.ShapeDtypeStruct(transposed.shape, jnp.float32),
        cost_estimate=pl.CostEstimate(
            flops=2 * width * tile * members, bytes_accessed=8 * width * tile, transcendentals=0),
        name="update",
    )(transposed, right, left)


def weigh_kernel(members, l_ref, r_ref, s_ref, w_ref, o_ref, t_ref, turned):
    answers, block = s_ref.shape[0] // members, s_ref.shape[2]
    population = members * block
    local = block // answers
    an = lax.axis_index("answer")
    scores = []
    for m in range(members):
        total = s_ref[m]
        for a in range(1, answers):
            total = total + s_ref[a * members + m]
        scores.append(total)
    average = sum(jnp.sum(x, axis=1, keepdims=True) for x in scores) / population
    squares = sum(jnp.sum(x * x, axis=1, keepdims=True) for x in scores) / population
    spread = jnp.sqrt(squares - average * average + 1e-05) * jnp.sqrt(jnp.float32(population))
    for m in range(members):
        scale = jnp.broadcast_to((scores[m] - average) / spread, (block, block)).T[:, :1]
        for a in range(answers):
            at = (a * members + m) * local
            rows = slice(at, at + local)
            w_ref[rows, :] = (l_ref[rows, :].astype(jnp.float32) * scale[a * local:(a + 1) * local]).astype(w_ref.dtype)
    rows = o_ref.shape[0]
    o_ref[...] = w_ref[:, pl.ds(pl.multiple_of(an * rows, 128), rows)].T
    turned[...] = r_ref[...].T
    width = t_ref.shape[0]
    t_ref[...] = turned[pl.ds(pl.multiple_of(an * width, 16), width), :]


def weigh(left_tile, right, parts, members, rows, width):
    vmem = pl.BlockSpec(memory_space=pltpu.VMEM)
    total = left_tile.shape[0]
    half = left_tile.dtype
    return pl.pallas_call(
        lambda *refs: weigh_kernel(members, *refs),
        out_shape=(
            jax.ShapeDtypeStruct(left_tile.shape, half),
            jax.ShapeDtypeStruct((rows, total), half),
            jax.ShapeDtypeStruct((width, total), half),
        ),
        in_specs=[vmem] * 3,
        out_specs=(vmem,) * 3,
        scratch_shapes=[pltpu.VMEM(right.shape[::-1], half)],
        cost_estimate=pl.CostEstimate(flops=total * right.shape[1] * 256, bytes_accessed=1 << 23, transcendentals=0),
        name="weigh",
    )(left_tile, right, parts)


def split(rows):
    steps = rows // 128
    last = 1 if steps > 1 else 0
    first = (steps - last + 1) // 2
    return [n * 128 for n in (first, steps - last - first, last) if n]


def order_of(chunks):
    return [(c, x) for c in range(len(chunks)) for x in (2, 1, 3) if (c, x) != (0, 3)]


def fast_body(master, left_noise, right_noise, returns):
    members, answers = lax.axis_size("member"), lax.axis_size("answer")
    where = lax.axis_index("answer").astype(jnp.int32)[None]
    transposed = master.T
    width, tile = transposed.shape
    rows = tile // answers
    chunks = split(rows)
    left_tile, right, parts, _, early, *blocks = exchange(left_noise, right_noise, returns, transposed, members, chunks)
    blocks = [blocks[i:i + len(chunks)] for i in range(0, len(blocks), len(chunks))]
    got = {(0, 3): early}
    for c, x in order_of(chunks):
        got[c, x] = lax.ppermute(blocks[x - 1][c], "answer", [(i, i ^ x) for i in range(answers)])
    weighted, own, turned = weigh(left_tile, right, parts, members, rows, width)
    new_master = update(transposed, turned, weighted)
    rollout, at = None, 0
    for c, size in enumerate(chunks):
        rollout = finalize(where, transposed, [got[c, x] for x in (1, 2, 3)], own, right, at, size, rollout)
        at += size
    return (new_master.T, rollout)


def fits(members, tensors, answers, tile, local):
    return (members, tensors, answers) == (2, 4, 4) and tile % 512 == 0 and local % 32 == 0


def body(master, left_noise, right_noise, returns):
    sizes = [lax.axis_size(n) for n in ("member", "tensor", "answer")]
    fast = fits(*sizes, master.shape[0], left_noise.shape[0])
    return (fast_body if fast else plain_body)(master, left_noise, right_noise, returns)


def solution(mesh):
    return jax.shard_map(
        body,
        mesh=mesh,
        in_specs=(
            P("member", ("tensor", "answer")),
            P(("member", "answer"), None),
            P(("member", "answer"), "tensor"),
            P("member", "answer"),
        ),
        out_specs=(P("member", ("tensor", "answer")), P(("member", "answer"), "tensor")),
        check_vma=False,
    )
```

profile of v0, /device:TPU:8, one launch (start us, length us, event | category | flops | bytes accessed | tf_op | source)
XLA Modules:
  0.0 139.9 jit_solution(14288058161923535329)
XLA Ops:
  0.6 41.0 %exchange.1 = (bf16[256,2560]{1,0:T(8,128)(2,1)}, bf16[256,3456]{1,0:T(8,128)(2,1)}, f32[8,1,128]{2,1,0:T(1,128)}, f32[1,128]{1,0:T(1,128)}, bf16[864,256]{1,0:T...) custom-call(bf16[32,5120]{1,0:T(8,128)(2,1)} %refs_0_.1, ...), custom_call_target="tpu_custom_call" | custom-call | tf_op jit(solution)/shard_map/exchange/pallas_call | solution.py:226
  41.7 13.8 %collective-permute-start.3 = (bf16[864,256]{1,0:T(8,128)(2,1)}, bf16[864,256]{1,0:T(8,128)(2,1)S(1)}, u32[]{:S(2)}, u32[]{:S(2)}) collective-permute-start(bf16[864,256]{1,0:T(8,128)(2,1)} %get-tuple-element.26), channel_id=1, source_target_pairs={{0,1},{1,0},{2,3},{3,2},{4,5},{5,4},{6,7},{7,6},{8,9},{9,8},{10,11... | collective-permute-start | bytes 1327112 | tf_op jit(solution)/shard_map/ppermute | solution.py:396
  55.5 0.1 collective-permute-start.6
  55.6 1.7 %collective-permute-start.7 = (bf16[864,256]{1,0:T(8,128)(2,1)}, bf16[864,256]{1,0:T(8,128)(2,1)S(1)}, u32[]{:S(2)}, u32[]{:S(2)}) collective-permute-start(bf16[864,256]{1,0:T(8,128)(2,1)} %get-tuple-element.30), channel_id=1, source_target_pairs={{0,2},{1,3},{2,0},{3,1},{4,6},{5,7},{6,4},{7,5},{8,10},{9,11},{10,... | collective-permute-start | bytes 1327112 | tf_op jit(solution)/shard_map/ppermute | solution.py:396
  57.3 1.2 collective-permute-start.4
  58.5 0.5 collective-permute-start.5
  59.0 3.6 %weigh.1 = (bf16[256,2560]{1,0:T(8,128)(2,1)}, bf16[640,256]{1,0:T(8,128)(2,1)}, bf16[864,256]{1,0:T(8,128)(2,1)}) custom-call(bf16[256,2560]{1,0:T(8,128)(2,1)} %get-tuple-element.17.refs_0_, bf16[256,3456]{1,0:T(8,128)(2,1)} %get-tuple-element.18.refs_1_.right_ref, f32[8,1,128]{2,1,0:T(1,128)} %get-tuple-element.19.refs_2_), custom_call_target="tpu_custom_call" | custom-call | flops 226492416 | bytes 8388608 | tf_op jit(solution)/shard_map/weigh/pallas_call | solution.py:359
  62.7 19.8 %collective-permute-done.3.one_ref = bf16[864,256]{1,0:T(8,128)(2,1)S(1)} collective-permute-done((bf16[864,256]{1,0:T(8,128)(2,1)}, bf16[864,256]{1,0:T(8,128)(2,1)S(1)}, u32[]{:S(2)}, u32[]{:S(2)}) %collective-permute-start.3) | collective-permute-done | bytes 442400 | tf_op jit(solution)/shard_map/ppermute | solution.py:396
  82.5 0.0 copy-start
  82.5 2.4 %collective-permute-start = (bf16[864,128]{1,0:T(8,128)(2,1)}, bf16[864,128]{1,0:T(8,128)(2,1)S(1)}, u32[]{:S(2)}, u32[]{:S(2)}) collective-permute-start(bf16[864,128]{1,0:T(8,128)(2,1)} %get-tuple-element.22), channel_id=1, source_target_pairs={{0,1},{1,0},{2,3},{3,2},{4,5},{5,4},{6,7},{7,6},{8,9},{9,8},{10,11... | collective-permute-start | bytes 663560 | tf_op jit(solution)/shard_map/ppermute | solution.py:396
  84.9 7.1 %collective-permute-done.6.one_ref = bf16[864,256]{1,0:T(8,128)(2,1)S(1)} collective-permute-done((bf16[864,256]{1,0:T(8,128)(2,1)}, bf16[864,256]{1,0:T(8,128)(2,1)S(1)}, u32[]{:S(2)}, u32[]{:S(2)}) %collective-permute-start.6) | collective-permute-done | bytes 442400 | tf_op jit(solution)/shard_map/ppermute | solution.py:396
  92.0 0.0 copy-start.3
  92.0 3.5 %collective-permute-start.1 = (bf16[864,128]{1,0:T(8,128)(2,1)}, bf16[864,128]{1,0:T(8,128)(2,1)S(1)}, u32[]{:S(2)}, u32[]{:S(2)}) collective-permute-start(bf16[864,128]{1,0:T(8,128)(2,1)} %get-tuple-element.23), channel_id=1, source_target_pairs={{0,2},{1,3},{2,0},{3,1},{4,6},{5,7},{6,4},{7,5},{8,10},{9,11},{10,... | collective-permute-start | bytes 663560 | tf_op jit(solution)/shard_map/ppermute | solution.py:396
  95.5 0.0 collective-permute-done.7.two_ref
  95.5 0.0 copy-start.4
  95.5 0.3 collective-permute-start.2
  95.8 9.8 %update.1 = f32[864,2560]{1,0:T(8,128)} custom-call(f32[864,2560]{1,0:T(8,128)} %bitcast.4, bf16[864,256]{1,0:T(8,128)(2,1)} %get-tuple-element.20.right_ref, bf16[256,2560]{1,0:T(8,128)(2,1)} %get-tuple-element.21.left_ref), custom_call_target="tpu_custom_call" | custom-call | flops 1132462080 | bytes 17694720 | tf_op jit(solution)/shard_map/update/pallas_call | solution.py:312
  105.7 0.0 copy-done
  105.7 0.0 copy-done.3
  105.7 0.0 copy-done.4
  105.7 4.7 %final.3.refs_0_ = bf16[640,3456]{1,0:T(8,128)(2,1)} custom-call(s32[1]{0:T(128)} %bitcast.2.where_ref, f32[864,2560]{1,0:T(8,128)} %bitcast.5, bf16[864,256]{1,0:T(8,128)(2,1)} %copy-done.3, bf16[864,256]{1,0:T(8,128)(2,1)} %copy-done.4, bf16[864,256]{1,0:T(8,128)(2,1)} %get-tuple-element.31.three_ref, bf16[640,256]{1,0:T(8,128)(2,1)} %get-tuple-element.25.left_ref, ...), custom_call_target="tpu_custom_call" | custom-call | flops 679477248 | bytes 5308416 | tf_op jit(solution)/shard_map/final/pallas_call | solution.py:282
  110.3 0.0 collective-permute-done.4.two_ref
  110.3 0.0 copy-start.1
  110.4 16.8 %collective-permute-done.5.three_ref = bf16[864,256]{1,0:T(8,128)(2,1)S(1)} collective-permute-done((bf16[864,256]{1,0:T(8,128)(2,1)}, bf16[864,256]{1,0:T(8,128)(2,1)S(1)}, u32[]{:S(2)}, u32[]{:S(2)}) %collective-permute-start.5) | collective-permute-done | bytes 442400 | tf_op jit(solution)/shard_map/ppermute | solution.py:396
  127.1 0.0 copy-done.1
  127.1 0.0 copy-start.2
  127.1 0.8 copy-done.2
  127.9 4.6 %final.4.refs_0_ = bf16[640,3456]{1,0:T(8,128)(2,1)} custom-call(s32[1]{0:T(128)} %bitcast.2.where_ref, f32[864,2560]{1,0:T(8,128)} %bitcast.6, bf16[864,256]{1,0:T(8,128)(2,1)} %copy-done, bf16[864,256]{1,0:T(8,128)(2,1)} %copy-done.1, bf16[864,256]{1,0:T(8,128)(2,1)} %copy-done.2, ...), custom_call_target="tpu_custom_call", output_to_operand_aliasing={{}: (7, {})} | custom-call | flops 679477248 | bytes 5308416 | tf_op jit(solution)/shard_map/final/pallas_call | solution.py:282
  132.5 0.0 collective-permute-done.one_ref
  132.5 0.0 copy-start.5
  132.6 0.0 collective-permute-done.1.two_ref
  132.6 0.0 copy-start.6
  132.6 3.0 %collective-permute-done.2.three_ref = bf16[864,128]{1,0:T(8,128)(2,1)S(1)} collective-permute-done((bf16[864,128]{1,0:T(8,128)(2,1)}, bf16[864,128]{1,0:T(8,128)(2,1)S(1)}, u32[]{:S(2)}, u32[]{:S(2)}) %collective-permute-start.2) | collective-permute-done | bytes 221216 | tf_op jit(solution)/shard_map/ppermute | solution.py:396
  135.5 0.0 copy-done.5
  135.5 0.0 copy-done.6
  135.5 0.0 copy-start.7
  135.5 0.7 copy-done.7
  136.2 3.7 %final.5 = bf16[640,3456]{1,0:T(8,128)(2,1)} custom-call(s32[1]{0:T(128)} %bitcast.2.where_ref, f32[864,2560]{1,0:T(8,128)} %bitcast.7, bf16[864,128]{1,0:T(8,128)(2,1)} %copy-done.5, bf16[864,128]{1,0:T(8,128)(2,1)} %copy-done.6, bf16[864,128]{1,0:T(8,128)(2,1)} %copy-done.7, ...), custom_call_target="tpu_custom_call", output_to_operand_aliasing={{}: (7, {})} | custom-call | flops 339738624 | bytes 2654208 | tf_op jit(solution)/shard_map/final/pallas_call | solution.py:282
Async XLA Ops:
  41.7 40.8 %collective-permute-start.3 = (bf16[864,256]{1,0:T(8,128)(2,1)}, bf16[864,256]{1,0:T(8,128)(2,1)S(1)}, u32[]{:S(2)}, u32[]{:S(2)}) collective-permute-start(bf16[864,256]{1,0:T(8,128)(2,1)} %get-tuple-element.26), channel_id=1, source_target_pairs={{0,1},{1,0},{2,3},{3,2},{4,5},{5,4},{6,7},{7,6},{8,9},{9,8},{10,11... | collective-permute-start | bytes 1327112 | tf_op jit(solution)/shard_map/ppermute | solution.py:396
  55.5 36.5 %collective-permute-start.6 = (bf16[864,256]{1,0:T(8,128)(2,1)}, bf16[864,256]{1,0:T(8,128)(2,1)S(1)}, u32[]{:S(2)}, u32[]{:S(2)}) collective-permute-start(bf16[864,256]{1,0:T(8,128)(2,1)} %get-tuple-element.29), channel_id=1, source_target_pairs={{0,1},{1,0},{2,3},{3,2},{4,5},{5,4},{6,7},{7,6},{8,9},{9,8},{10,11... | collective-permute-start | bytes 1327112 | tf_op jit(solution)/shard_map/ppermute | solution.py:396
  55.6 39.9 %collective-permute-start.7 = (bf16[864,256]{1,0:T(8,128)(2,1)}, bf16[864,256]{1,0:T(8,128)(2,1)S(1)}, u32[]{:S(2)}, u32[]{:S(2)}) collective-permute-start(bf16[864,256]{1,0:T(8,128)(2,1)} %get-tuple-element.30), channel_id=1, source_target_pairs={{0,2},{1,3},{2,0},{3,1},{4,6},{5,7},{6,4},{7,5},{8,10},{9,11},{10,... | collective-permute-start | bytes 1327112 | tf_op jit(solution)/shard_map/ppermute | solution.py:396
  57.3 53.1 %collective-permute-start.4 = (bf16[864,256]{1,0:T(8,128)(2,1)}, bf16[864,256]{1,0:T(8,128)(2,1)S(1)}, u32[]{:S(2)}, u32[]{:S(2)}) collective-permute-start(bf16[864,256]{1,0:T(8,128)(2,1)} %get-tuple-element.27), channel_id=1, source_target_pairs={{0,2},{1,3},{2,0},{3,1},{4,6},{5,7},{6,4},{7,5},{8,10},{9,11},{10,... | collective-permute-start | bytes 1327112 | tf_op jit(solution)/shard_map/ppermute | solution.py:396
  58.5 68.6 %collective-permute-start.5 = (bf16[864,256]{1,0:T(8,128)(2,1)}, bf16[864,256]{1,0:T(8,128)(2,1)S(1)}, u32[]{:S(2)}, u32[]{:S(2)}) collective-permute-start(bf16[864,256]{1,0:T(8,128)(2,1)} %get-tuple-element.28), channel_id=1, source_target_pairs={{0,3},{1,2},{2,1},{3,0},{4,7},{5,6},{6,5},{7,4},{8,11},{9,10},{10,... | collective-permute-start | bytes 1327112 | tf_op jit(solution)/shard_map/ppermute | solution.py:396
  82.5 23.2 %copy-start = (bf16[864,256]{1,0:T(8,128)(2,1)}, bf16[864,256]{1,0:T(8,128)(2,1)S(1)}, u32[]{:S(2)}) copy-start(bf16[864,256]{1,0:T(8,128)(2,1)S(1)} %collective-permute-done.3.one_ref) | copy-start | bytes 1327108
  82.5 50.0 %collective-permute-start = (bf16[864,128]{1,0:T(8,128)(2,1)}, bf16[864,128]{1,0:T(8,128)(2,1)S(1)}, u32[]{:S(2)}, u32[]{:S(2)}) collective-permute-start(bf16[864,128]{1,0:T(8,128)(2,1)} %get-tuple-element.22), channel_id=1, source_target_pairs={{0,1},{1,0},{2,3},{3,2},{4,5},{5,4},{6,7},{7,6},{8,9},{9,8},{10,11... | collective-permute-start | bytes 663560 | tf_op jit(solution)/shard_map/ppermute | solution.py:396
  92.0 13.7 %copy-start.3 = (bf16[864,256]{1,0:T(8,128)(2,1)}, bf16[864,256]{1,0:T(8,128)(2,1)S(1)}, u32[]{:S(2)}) copy-start(bf16[864,256]{1,0:T(8,128)(2,1)S(1)} %collective-permute-done.6.one_ref) | copy-start | bytes 1327108
  92.0 40.6 %collective-permute-start.1 = (bf16[864,128]{1,0:T(8,128)(2,1)}, bf16[864,128]{1,0:T(8,128)(2,1)S(1)}, u32[]{:S(2)}, u32[]{:S(2)}) collective-permute-start(bf16[864,128]{1,0:T(8,128)(2,1)} %get-tuple-element.23), channel_id=1, source_target_pairs={{0,2},{1,3},{2,0},{3,1},{4,6},{5,7},{6,4},{7,5},{8,10},{9,11},{10,... | collective-permute-start | bytes 663560 | tf_op jit(solution)/shard_map/ppermute | solution.py:396
  95.5 10.2 %copy-start.4 = (bf16[864,256]{1,0:T(8,128)(2,1)}, bf16[864,256]{1,0:T(8,128)(2,1)S(1)}, u32[]{:S(2)}) copy-start(bf16[864,256]{1,0:T(8,128)(2,1)S(1)} %collective-permute-done.7.two_ref) | copy-start | bytes 1327108
  95.5 40.0 %collective-permute-start.2 = (bf16[864,128]{1,0:T(8,128)(2,1)}, bf16[864,128]{1,0:T(8,128)(2,1)S(1)}, u32[]{:S(2)}, u32[]{:S(2)}) collective-permute-start(bf16[864,128]{1,0:T(8,128)(2,1)} %get-tuple-element.24), channel_id=1, source_target_pairs={{0,3},{1,2},{2,1},{3,0},{4,7},{5,6},{6,5},{7,4},{8,11},{9,10},{10,... | collective-permute-start | bytes 663560 | tf_op jit(solution)/shard_map/ppermute | solution.py:396
  110.3 16.8 %copy-start.1 = (bf16[864,256]{1,0:T(8,128)(2,1)}, bf16[864,256]{1,0:T(8,128)(2,1)S(1)}, u32[]{:S(2)}) copy-start(bf16[864,256]{1,0:T(8,128)(2,1)S(1)} %collective-permute-done.4.two_ref) | copy-start | bytes 1327108
  127.1 0.8 copy-start.2
  132.5 3.0 %copy-start.5 = (bf16[864,128]{1,0:T(8,128)(2,1)}, bf16[864,128]{1,0:T(8,128)(2,1)S(1)}, u32[]{:S(2)}) copy-start(bf16[864,128]{1,0:T(8,128)(2,1)S(1)} %collective-permute-done.one_ref) | copy-start | bytes 663556
  132.6 3.0 %copy-start.6 = (bf16[864,128]{1,0:T(8,128)(2,1)}, bf16[864,128]{1,0:T(8,128)(2,1)S(1)}, u32[]{:S(2)}) copy-start(bf16[864,128]{1,0:T(8,128)(2,1)S(1)} %collective-permute-done.1.two_ref) | copy-start | bytes 663556
  135.5 0.7 copy-start.7
where the time goes:
time: 140 us
  Pallas kernels  67.5 us (48%)
  waiting for transfers between devices  46.7 us (33%)
  starting transfers between devices  23.5 us (17%)
  local copies, waits for them, and re-layouts  1.5 us (1%)
    ppermute x8, waiting for transfers between devices, fast_body(): lax.ppermute(blocks[x - 1][c], 'answer', [(i, i ^ x) for i in range(answe...  46.7 us
    pallas_call x1, Pallas kernels, exchange(): pl.pallas_call(lambda *refs: exchange_kernel(members, chunks, *refs), out...  41 us
    ppermute x8, starting transfers between devices, fast_body(): lax.ppermute(blocks[x - 1][c], 'answer', [(i, i ^ x) for i in range(answe...  23.5 us
    pallas_call x3, Pallas kernels, finalize(): pl.pallas_call(final_kernel, grid_spec=pltpu.PrefetchScalarGridSpec(num_s...  12.9 us
    pallas_call x1, Pallas kernels, update(): pl.pallas_call(update_kernel, grid=(width // chunk,), in_specs=[pl.BlockS...  9.84 us
    pallas_call x1, Pallas kernels, weigh(): pl.pallas_call(lambda *refs: weigh_kernel(members, *refs), out_shape=(jax...  3.64 us
  transfers between devices with their start and end apart: 8, of which 4 were waited for; matrix products, arithmetic and copies ran while one was open for 0% of the time, Pallas kernels for 16%

commit v1 on v0

--- a/solution.py
+++ b/solution.py
@@ -111,6 +111,13 @@
         for c in range(len(chunks)):
             push(x, c).start()
 
+    barrier = pltpu.get_barrier_semaphore()
+    peers = [(dm, da) for dm in range(members) for da in range(answers) if (dm, da) != (0, 0)]
+    place = lambda dm, da: {"member": lax.rem(me + dm, members), "answer": lax.rem(an + da, answers)}
+    for dm, da in peers:
+        pl.semaphore_signal(barrier, inc=1, device_id=place(dm, da), device_id_type=pl.DeviceIdType.MESH)
+    for t in (core, across):
+        pl.semaphore_signal(barrier, inc=1, device_id={"tensor": t}, device_id_type=pl.DeviceIdType.MESH)
     pull(3).start()
     pull(2).start()
     own_l = pltpu.make_async_copy(
@@ -125,91 +132,116 @@
     own_p.start()
     own_s.start()
 
-    barrier = pltpu.get_barrier_semaphore()
-    peers = [(dm, da) for dm in range(members) for da in range(answers) if (dm, da) != (0, 0)]
-    place = lambda dm, da: {"member": lax.rem(me + dm, members), "answer": lax.rem(an + da, answers)}
-    for dm, da in peers:
-        pl.semaphore_signal(barrier, inc=1, device_id=place(dm, da), device_id_type=pl.DeviceIdType.MESH)
-    for t in (core, across):
-        pl.semaphore_signal(barrier, inc=1, device_id={"tensor": t}, device_id_type=pl.DeviceIdType.MESH)
     pl.semaphore_wait(barrier, len(peers) + 2)
 
     mine = lax.rem(an, 2)
-    r_near = remote(right_ref, r_at(an, me), z_send.at[0], z_recv.at[0], {"answer": near})
-    r_far = remote(right_ref, r_at(an, me), z_send.at[1], z_recv.at[1 + mine], {"answer": far})
-    l_over = remote(left_ref.at[:, pl.ds(pl.multiple_of(other * tile + te * piece, piece), piece)],
-                    l_at((an * members + me) * local, local, te), x_send.at[0], x_recv.at[0], {"member": other})
-    forward = {0: remote(right_ref, r_at(an, me), f_send.at[0], f_recv.at[0], {"member": other})}
-    l_over.start()
-    r_far.start()
-    r_near.start()
-    forward[0].start()
+    halves = 2
+    count = local // halves
+    sources = (an, near, beyond, beyond + 1)
+    started = []
+
+    def start(copy):
+        copy.start()
+        started.append(copy)
+        return copy
+
+    def landed(block, sem):
+        remote(block, block, x_send.at[0], sem, {"member": other}).wait_recv()
+
+    def r_half(a, m, h):
+        return r_ref.at[pl.ds(pl.multiple_of((a * members + m) * local + h * count, count), count), :]
+
+    def forward(k, h):
+        block = r_half(sources[k], me, h)
+        src = right_ref.at[h * count:(h + 1) * count, :] if k == 0 else block
+        start(remote(src, block, f_send.at[k, h], f_recv.at[k, h], {"member": other}))
+
+    def spread(k):
+        block = l_slab(sources[k], te)
+        start(remote(block, block, y_send.at[k, 0], y_recv.at[k, 0], {"tensor": across}))
+        start(remote(block, block, y_send.at[k, 1], y_recv.at[k, 1], {"tensor": core}))
+
+    start(remote(left_ref.at[:, pl.ds(pl.multiple_of(other * tile + te * piece, piece), piece)],
+                 l_at((an * members + me) * local, local, te), x_send.at[0], x_recv.at[0], {"member": other}))
+
+    def part_of(h):
+        src = right_ref.at[h * count:(h + 1) * count, :]
+        start(remote(src, r_half(an, me, h), z_send.at[0, h], z_recv.at[1 + mine, h], {"answer": far}))
+        start(remote(src, r_half(an, me, h), z_send.at[1, h], z_recv.at[0, h], {"answer": near}))
+
+    part_of(0)
     own_p.wait()
-    scores = []
     for i, (dm, da) in enumerate(peers):
-        copy = remote(p_ref, s_ref.at[an * members + me], s_send.at[i], s_recv.at[i], place(dm, da))
-        copy.start()
-        scores.append(copy)
+        start(remote(p_ref, s_ref.at[an * members + me], s_send.at[i], s_recv.at[i], place(dm, da)))
     own_l.wait()
-    l_over.wait_recv()
-    l_near = remote(l_slab(an, te), l_slab(an, te), q_send.at[0], q_recv.at[0], {"answer": near})
-    l_far = remote(l_slab(an, te), l_slab(an, te), q_send.at[1], q_recv.at[1 + mine], {"answer": far})
-    l_far.start()
-    l_near.start()
+    landed(l_at((an * members + other) * local, local, te), x_recv.at[0])
+    block = l_slab(an, te)
+    start(remote(block, block, q_send.at[0], q_recv.at[1 + mine], {"answer": far}))
+    start(remote(block, block, q_send.at[1], q_recv.at[0], {"answer": near}))
+    part_of(1)
+    spread(0)
+    for h in range(halves):
+        forward(0, h)
     cast(3)
-    push(3, 0).wait()
-    early = remote(blocks[2 * len(chunks)], e_ref, e_send, e_recv, {"answer": pair[3]})
-    early.start()
-    for c in range(1, len(chunks)):
+    early = []
+    for c, size in enumerate(chunks):
         push(3, c).wait()
+        at = sum(chunks[:c])
+        copy = remote(blocks[2 * len(chunks) + c], e_ref.at[:, at:at + size], e_send.at[c], e_recv.at[c], {"answer": pair[3]})
+        pl.when(inner)(copy.start)
+        early.append(copy)
     pull(1).start()
+    for h in range(halves):
+        landed(r_half(near, me, h), z_recv.at[0, h])
+        forward(1, h)
+    landed(l_slab(near, te), q_recv.at[0])
+    spread(1)
     cast(2)
+    relays = []
+
+    def relay(block, send, recv):
+        copy = remote(block, block, send, recv, {"answer": near})
+        pl.when(inner)(copy.start)
+        relays.append(copy)
+
+    def pass_on(h):
+        for k in (2, 3):
+            block = r_half(sources[k], me, h)
+            landed(block, z_recv.at[k - 1, h])
+            relay(block, z_send.at[k, h], z_recv.at[k - 1, h])
+            forward(k, h)
+
+    pass_on(0)
+    for k in (2, 3):
+        block = l_slab(sources[k], te)
+        landed(block, q_recv.at[k - 1])
+        relay(block, q_send.at[k], q_recv.at[k - 1])
+        spread(k)
+    pass_on(1)
+    for k in range(answers):
+        block = l_slab(sources[k], across)
+        landed(block, y_recv.at[k, 0])
+        start(remote(block, block, y_send.at[k, 2], y_recv.at[k, 2], {"tensor": core}))
     cast(1)
-
-    sources = (near, beyond, beyond + 1)
-    r_relays, l_relays = {}, {}
-    for k, source in enumerate(sources):
-        block = r_at(source, me)
-        remote(block, block, z_send.at[0], z_recv.at[k], {"answer": near}).wait_recv()
-        forward[k + 1] = remote(block, block, f_send.at[k + 1], f_recv.at[k + 1], {"member": other})
-        forward[k + 1].start()
-        if k:
-            r_relays[k] = remote(block, block, z_send.at[1 + k], z_recv.at[k], {"answer": near})
-            pl.when(inner)(r_relays[k].start)
-        block = l_slab(source, te)
-        remote(block, block, q_send.at[0], q_recv.at[k], {"answer": near}).wait_recv()
-        if k:
-            l_relays[k] = remote(block, block, q_send.at[1 + k], q_recv.at[k], {"answer": near})
-            pl.when(inner)(l_relays[k].start)
-    total = slab * answers
-    l_y = remote(l_at(0, total, te), l_at(0, total, te), y_send.at[0], y_recv.at[0], {"tensor": across})
-    l_c = remote(l_at(0, total, te), l_at(0, total, te), y_send.at[1], y_recv.at[1], {"tensor": core})
-    l_y.start()
-    l_c.start()
-    block = l_at(0, total, across)
-    remote(block, block, y_send.at[0], y_recv.at[0], {"tensor": across}).wait_recv()
-    l_d = remote(block, block, y_send.at[2], y_recv.at[2], {"tensor": core})
-    l_d.start()
     for i, (dm, da) in enumerate(peers):
-        block = s_ref.at[lax.rem(an + answers - da, answers) * members + lax.rem(me + members - dm, members)]
-        remote(block, block, s_send.at[i], s_recv.at[i], {"member": other}).wait_recv()
-    for k, source in enumerate((an,) + sources):
-        block = r_at(source, other)
-        remote(block, block, f_send.at[k], f_recv.at[k], {"member": other}).wait_recv()
-    for k, t in ((1, core), (2, 3 - te)):
-        block = l_at(0, total, t)
-        remote(block, block, y_send.at[k], y_recv.at[k], {"tensor": core}).wait_recv()
+        landed(s_ref.at[lax.rem(an + answers - da, answers) * members + lax.rem(me + members - dm, members)], s_recv.at[i])
+    for k in range(answers):
+        for h in range(halves):
+            landed(r_half(sources[k], other, h), f_recv.at[k, h])
+    for k in range(answers):
+        landed(l_slab(sources[k], core), y_recv.at[k, 1])
+        landed(l_slab(sources[k], 3 - te), y_recv.at[k, 2])
     own_r.wait()
     own_s.wait()
     for x in (2, 1):
         for c in range(len(chunks)):
             push(x, c).wait()
-    for copy in [r_near, r_far, l_over, l_near, l_far, l_y, l_c, l_d] + scores + list(forward.values()):
+    for copy in started:
         copy.wait_send()
-    for copy in list(r_relays.values()) + list(l_relays.values()):
+    for copy in relays + early:
         pl.when(inner)(copy.wait_send)
-    early.wait_recv()
-    early.wait_send()
+    for copy in early:
+        pl.when(inner)(copy.wait_recv)
 
 
 def exchange(left_noise, right_noise, returns, transposed, members, chunks):
@@ -230,7 +262,7 @@
             shape((total, width), half),
             shape((count, 1, block), jnp.float32),
             shape((1, block), jnp.float32),
-            shape((cols, chunks[0]), half),
+            shape((cols, tile // answers), half),
         ) + tuple(shape((cols, size), half) for _ in range(sides) for size in chunks),
         in_specs=[vmem] * 3 + [anywhere],
         out_specs=(anywhere,) * (5 + sides * len(chunks)),
@@ -238,8 +270,9 @@
             pltpu.VMEM((2, cols, tile // answers), jnp.float32), pltpu.VMEM((2, cols, tile // answers), half),
             pltpu.VMEM((1, block), jnp.float32),
             dma((4,)), dma((sides,)), dma((sides, len(chunks))), dma((count - 1,)), dma((count - 1,)),
-            dma((1,)), dma((1,)), dma((answers,)), dma((answers,)),
-            dma((4,)), dma((3,)), dma((4,)), dma((3,)), dma((3,)), dma((3,)), dma, dma,
+            dma((1,)), dma((1,)), dma((answers, 2)), dma((answers, 2)),
+            dma((4, 2)), dma((3, 2)), dma((4,)), dma((3,)), dma((answers, 3)), dma((answers, 3)),
+            dma((len(chunks),)), dma((len(chunks),)),
         ],
         compiler_params=pltpu.CompilerParams(collective_id=0, has_side_effects=True),
         name="exchange",
@@ -251,14 +284,21 @@
     return fits[-1] if fits else size
 
 
-def final_kernel(where_ref, master_ref, one_ref, two_ref, three_ref, left_ref, right_ref, *refs):
+def final_kernel(where_ref, master_ref, one_ref, two_ref, three_ref, early_ref, left_ref, right_ref, *refs):
     out_ref, stack = refs[-2:]
     an = lax.axis_index("answer")
     width, rows = master_ref.shape
     near = an + 1 - 2 * lax.rem(an, 2)
-    parts = ((an, master_ref), (near, one_ref), (lax.rem(an + 2, 4), two_ref), (3 - an, three_ref))
-    for a, ref in parts:
+    inner = lax.div(an + 1, 2) == 1
+
+    def place(a, ref):
         stack[pl.ds(pl.multiple_of(a * width, 16), width), :] = ref[...].astype(stack.dtype)
+
+    place(an, master_ref)
+    place(near, one_ref)
+    place(lax.rem(an + 2, 4), two_ref)
+    pl.when(inner)(lambda: place(3 - an, early_ref))
+    pl.when(jnp.logical_not(inner))(lambda: place(3 - an, three_ref))
     row = lax.broadcasted_iota(jnp.int32, (rows, rows), 0)
     col = lax.broadcasted_iota(jnp.int32, (rows, rows), 1)
     unit = jnp.where(row == col, 1.0, 0.0).astype(stack.dtype)
@@ -270,7 +310,7 @@
         out_ref[:, cols] = (new + old).astype(out_ref.dtype)
 
 
-def finalize(where, transposed, sides, left, right, first, size, so_far):
+def finalize(where, transposed, sides, early, left, right, first, size, so_far):
     rows, members = left.shape
     width = transposed.shape[0]
     total = right.shape[1]
@@ -287,6 +327,7 @@
             in_specs=[
                 pl.BlockSpec((width, chunk), lambda i, w: (0, w[0] * per + start + i)),
                 side, side, side,
+                pl.BlockSpec((width, chunk), lambda i, w: (0, start + i)),
                 pl.BlockSpec((chunk, members), lambda i, w: (start + i, 0)),
                 pl.BlockSpec((members, total), lambda i, w: (0, 0)),
             ] + [pl.BlockSpec(memory_space=pl.ANY)] * len(more),
@@ -294,11 +335,12 @@
             scratch_shapes=[pltpu.VMEM((total, chunk), jnp.bfloat16)],
         ),
         out_shape=jax.ShapeDtypeStruct((rows, total), jnp.bfloat16),
-        input_output_aliases={7: 0} if more else {},
+        input_output_aliases={8: 0} if more else {},
         cost_estimate=pl.CostEstimate(
             flops=2 * size * total * (members + chunk), bytes_accessed=6 * size * total, transcendentals=0),
+        compiler_params=pltpu.CompilerParams(vmem_limit_bytes=24 << 20),
         name="final",
-    )(where, transposed, *sides, left, right, *more)
+    )(where, transposed, *sides, early, left, right, *more)
 
 
 def update_kernel(master_ref, right_ref, left_ref, new_ref):
@@ -321,6 +363,7 @@
         out_shape=jax.ShapeDtypeStruct(transposed.shape, jnp.float32),
         cost_estimate=pl.CostEstimate(
             flops=2 * width * tile * members, bytes_accessed=8 * width * tile, transcendentals=0),
+        compiler_params=pltpu.CompilerParams(vmem_limit_bytes=24 << 20),
         name="update",
     )(transposed, right, left)
 
@@ -367,6 +410,7 @@
         out_specs=(vmem,) * 3,
         scratch_shapes=[pltpu.VMEM(right.shape[::-1], half)],
         cost_estimate=pl.CostEstimate(flops=total * right.shape[1] * 256, bytes_accessed=1 << 23, transcendentals=0),
+        compiler_params=pltpu.CompilerParams(vmem_limit_bytes=24 << 20),
         name="weigh",
     )(left_tile, right, parts)
 
@@ -378,8 +422,8 @@
     return [n * 128 for n in (first, steps - last - first, last) if n]
 
 
-def order_of(chunks):
-    return [(c, x) for c in range(len(chunks)) for x in (2, 1, 3) if (c, x) != (0, 3)]
+def order_of(count):
+    return [(c, x) for c in range(count) for x in (3, 2, 1)]
 
 
 def fast_body(master, left_noise, right_noise, returns):
@@ -391,14 +435,14 @@
     chunks = split(rows)
     left_tile, right, parts, _, early, *blocks = exchange(left_noise, right_noise, returns, transposed, members, chunks)
     blocks = [blocks[i:i + len(chunks)] for i in range(0, len(blocks), len(chunks))]
-    got = {(0, 3): early}
-    for c, x in order_of(chunks):
-        got[c, x] = lax.ppermute(blocks[x - 1][c], "answer", [(i, i ^ x) for i in range(answers)])
+    got = {}
+    for c, x in order_of(len(chunks)):
+        got[c, x] = lax.ppermute(blocks[x - 1][c], "answer", [(i, i ^ x) for i in range(answers) if x < 3 or i in (0, 3)])
     weighted, own, turned = weigh(left_tile, right, parts, members, rows, width)
     new_master = update(transposed, turned, weighted)
     rollout, at = None, 0
     for c, size in enumerate(chunks):
-        rollout = finalize(where, transposed, [got[c, x] for x in (1, 2, 3)], own, right, at, size, rollout)
+        rollout = finalize(where, transposed, [got[c, x] for x in (1, 2, 3)], early, own, right, at, size, rollout)
         at += size
     return (new_master.T, rollout)
 

time: 140 us -> 124 us (0.89)
  the two profiles are of different devices: /device:TPU:8 before, /device:TPU:0 now
where the time goes in v1:
time: 124 us
  Pallas kernels  54.7 us (44%)
  waiting for transfers between devices  37.9 us (31%)
  starting transfers between devices  23.4 us (19%)
  local copies, waits for them, and re-layouts  6.98 us (6%)
    pallas_call x1, Pallas kernels, exchange(): pl.pallas_call(lambda *refs: exchange_kernel(members, chunks, *refs), out...  40.8 us
    ppermute x9, waiting for transfers between devices, fast_body(): lax.ppermute(blocks[x - 1][c], 'answer', [(i, i ^ x) for i in range(answe...  37.9 us
    ppermute x9, starting transfers between devices, fast_body(): lax.ppermute(blocks[x - 1][c], 'answer', [(i, i ^ x) for i in range(answe...  23.4 us
    pallas_call x3, Pallas kernels, finalize(): pl.pallas_call(final_kernel, grid_spec=pltpu.PrefetchScalarGridSpec(num_s...  7.96 us
    unnamed x12, local copies, waits for them, and re-layouts  6.98 us
    pallas_call x1, Pallas kernels, update(): pl.pallas_call(update_kernel, grid=(width // chunk,), in_specs=[pl.BlockS...  4.91 us
  transfers between devices with their start and end apart: 9, of which 4 were waited for; matrix products, arithmetic and copies ran while one was open for 0% of the time, Pallas kernels for 10%

profile of v1, /device:TPU:0, one launch (start us, length us, event | category | flops | bytes accessed | tf_op | source)
XLA Modules:
  0.0 123.7 jit_solution(2662482898691173812)
XLA Ops:
  0.6 40.8 %exchange.1 = (bf16[256,2560]{1,0:T(8,128)(2,1)}, bf16[256,3456]{1,0:T(8,128)(2,1)}, f32[8,1,128]{2,1,0:T(1,128)}, f32[1,128]{1,0:T(1,128)}, bf16[864,640]{1,0:T...) custom-call(bf16[32,5120]{1,0:T(8,128)(2,1)} %refs_0_.1, ...), custom_call_target="tpu_custom_call" | custom-call | tf_op jit(solution)/shard_map/exchange/pallas_call | solution.py:258
  41.5 5.7 %collective-permute-start.3 = (bf16[864,256]{1,0:T(8,128)(2,1)}, bf16[864,256]{1,0:T(8,128)(2,1)S(1)}, u32[]{:S(2)}, u32[]{:S(2)}) collective-permute-start(bf16[864,256]{1,0:T(8,128)(2,1)} %get-tuple-element.28), channel_id=1, source_target_pairs={{0,1},{1,0},{2,3},{3,2},{4,5},{5,4},{6,7},{7,6},{8,9},{9,8},{10,11... | collective-permute-start | bytes 1327112 | tf_op jit(solution)/shard_map/ppermute | solution.py:440
  47.2 0.1 collective-permute-start.6
  47.2 2.8 %collective-permute-start.7 = (bf16[864,256]{1,0:T(8,128)(2,1)}, bf16[864,256]{1,0:T(8,128)(2,1)S(1)}, u32[]{:S(2)}, u32[]{:S(2)}) collective-permute-start(bf16[864,256]{1,0:T(8,128)(2,1)} %get-tuple-element.32), channel_id=1, source_target_pairs={{0,2},{1,3},{2,0},{3,1},{4,6},{5,7},{6,4},{7,5},{8,10},{9,11},{10,... | collective-permute-start | bytes 1327112 | tf_op jit(solution)/shard_map/ppermute | solution.py:440
  50.1 3.4 %collective-permute-start.8 = (bf16[864,256]{1,0:T(8,128)(2,1)}, bf16[864,256]{1,0:T(8,128)(2,1)S(1)}, u32[]{:S(2)}, u32[]{:S(2)}) collective-permute-start(bf16[864,256]{1,0:T(8,128)(2,1)} %get-tuple-element.33), channel_id=1, source_target_pairs={{0,3},{3,0},{4,7},{7,4},{8,11},{11,8},{12,15},{15,12},{16,19},{19,... | collective-permute-start | bytes 1327112 | tf_op jit(solution)/shard_map/ppermute | solution.py:440
  53.5 0.1 collective-permute-start.4
  53.5 22.7 %collective-permute-done.3.one_ref = bf16[864,256]{1,0:T(8,128)(2,1)S(1)} collective-permute-done((bf16[864,256]{1,0:T(8,128)(2,1)}, bf16[864,256]{1,0:T(8,128)(2,1)S(1)}, u32[]{:S(2)}, u32[]{:S(2)}) %collective-permute-start.3) | collective-permute-done | bytes 442400 | tf_op jit(solution)/shard_map/ppermute | solution.py:440
  76.2 5.1 %collective-permute-start.5 = (bf16[864,256]{1,0:T(8,128)(2,1)}, bf16[864,256]{1,0:T(8,128)(2,1)S(1)}, u32[]{:S(2)}, u32[]{:S(2)}) collective-permute-start(bf16[864,256]{1,0:T(8,128)(2,1)} %get-tuple-element.30), channel_id=1, source_target_pairs={{0,3},{3,0},{4,7},{7,4},{8,11},{11,8},{12,15},{15,12},{16,19},{19,... | collective-permute-start | bytes 1327112 | tf_op jit(solution)/shard_map/ppermute | solution.py:440
  81.3 0.0 copy-start.1
  81.4 1.5 %copy-done.1 = bf16[256,3456]{1,0:T(8,128)(2,1)S(1)} copy-done((bf16[256,3456]{1,0:T(8,128)(2,1)S(1)}, bf16[256,3456]{1,0:T(8,128)(2,1)}, u32[]{:S(2)}) %copy-start.1) | copy-done | bytes 1769496
  82.8 0.0 copy-start.4
  82.8 1.3 %copy-done.4 = bf16[256,2560]{1,0:T(8,128)(2,1)S(1)} copy-done((bf16[256,2560]{1,0:T(8,128)(2,1)S(1)}, bf16[256,2560]{1,0:T(8,128)(2,1)}, u32[]{:S(2)}) %copy-start.4) | copy-done | bytes 1310744
  84.1 0.0 copy-start.5
  84.1 0.7 copy-done.5
  84.8 1.0 weigh.1
  85.8 8.6 %collective-permute-done.6.one_ref = bf16[864,256]{1,0:T(8,128)(2,1)S(1)} collective-permute-done((bf16[864,256]{1,0:T(8,128)(2,1)}, bf16[864,256]{1,0:T(8,128)(2,1)S(1)}, u32[]{:S(2)}, u32[]{:S(2)}) %collective-permute-start.6) | collective-permute-done | bytes 442400 | tf_op jit(solution)/shard_map/ppermute | solution.py:440
  94.4 0.0 collective-permute-start
  94.4 0.0 collective-permute-done.7.two_ref
  94.4 2.9 %collective-permute-start.1 = (bf16[864,128]{1,0:T(8,128)(2,1)}, bf16[864,128]{1,0:T(8,128)(2,1)S(1)}, u32[]{:S(2)}, u32[]{:S(2)}) collective-permute-start(bf16[864,128]{1,0:T(8,128)(2,1)} %get-tuple-element.24), channel_id=1, source_target_pairs={{0,2},{1,3},{2,0},{3,1},{4,6},{5,7},{6,4},{7,5},{8,10},{9,11},{10,... | collective-permute-start | bytes 663560 | tf_op jit(solution)/shard_map/ppermute | solution.py:440
  97.3 0.0 collective-permute-done.8.three_ref
  97.3 3.4 %collective-permute-start.2 = (bf16[864,128]{1,0:T(8,128)(2,1)}, bf16[864,128]{1,0:T(8,128)(2,1)S(1)}, u32[]{:S(2)}, u32[]{:S(2)}) collective-permute-start(bf16[864,128]{1,0:T(8,128)(2,1)} %get-tuple-element.25), channel_id=1, source_target_pairs={{0,3},{3,0},{4,7},{7,4},{8,11},{11,8},{12,15},{15,12},{16,19},{19,... | collective-permute-start | bytes 663560 | tf_op jit(solution)/shard_map/ppermute | solution.py:440
  100.7 0.0 copy-start
  100.8 3.5 %copy-done = f32[2560,864]{0,1:T(8,128)S(1)} copy-done((f32[2560,864]{0,1:T(8,128)S(1)}, f32[2560,864]{0,1:T(8,128)}, u32[]{:S(2)}) %copy-start) | copy-done | bytes 8847384
  104.3 0.0 copy-start.2
  104.3 0.0 copy-start.3
  104.3 4.9 %update.1 = f32[864,2560]{1,0:T(8,128)} custom-call(f32[864,2560]{1,0:T(8,128)S(1)} %bitcast.4, bf16[864,256]{1,0:T(8,128)(2,1)S(1)} %get-tuple-element.21.right_ref, bf16[256,2560]{1,0:T(8,128)(2,1)S(1)} %get-tuple-element.22.left_ref), custom_call_target="tpu_custom_call" | custom-call | flops 1132462080 | bytes 17694720 | tf_op jit(solution)/shard_map/update/pallas_call | solution.py:354
  109.2 0.0 copy-done.2
  109.2 0.0 copy-done.3
  109.2 3.1 %final.3.refs_0_ = bf16[640,3456]{1,0:T(8,128)(2,1)} custom-call(s32[1]{0:T(128)} %bitcast.2.where_ref, f32[864,2560]{1,0:T(8,128)S(1)} %bitcast.5, bf16[864,256]{1,0:T(8,128)(2,1)S(1)} %collective-permute-done.6.one_ref, bf16[864,256]{1,0:T(8,128)(2,1)S(1)} %collective-permute-done.7.two_ref, bf16[864,256]{1,0:T(8,128)(2,1)S(1)} %collective-permute-done.8.three_ref, ...), custom_call_target="tpu_custom_call" | custom-call | flops 679477248 | bytes 5308416 | tf_op jit(solution)/shard_map/final/pallas_call | solution.py:322
  112.2 0.0 collective-permute-done.4.two_ref
  112.2 0.0 collective-permute-done.5.three_ref
  112.2 3.1 %final.4.refs_0_ = bf16[640,3456]{1,0:T(8,128)(2,1)} custom-call(s32[1]{0:T(128)} %bitcast.2.where_ref, f32[864,2560]{1,0:T(8,128)S(1)} %bitcast.6, bf16[864,256]{1,0:T(8,128)(2,1)S(1)} %collective-permute-done.3.one_ref, bf16[864,256]{1,0:T(8,128)(2,1)S(1)} %collective-permute-done.4.two_ref, ...), custom_call_target="tpu_custom_call", output_to_operand_aliasing={{}: (8, {})} | custom-call | flops 679477248 | bytes 5308416 | tf_op jit(solution)/shard_map/final/pallas_call | solution.py:322
  115.3 0.3 collective-permute-done.one_ref
  115.6 6.3 %collective-permute-done.1.two_ref = bf16[864,128]{1,0:T(8,128)(2,1)S(1)} collective-permute-done((bf16[864,128]{1,0:T(8,128)(2,1)}, bf16[864,128]{1,0:T(8,128)(2,1)S(1)}, u32[]{:S(2)}, u32[]{:S(2)}) %collective-permute-start.1) | collective-permute-done | bytes 221216 | tf_op jit(solution)/shard_map/ppermute | solution.py:440
  121.9 0.0 collective-permute-done.2.three_ref
  121.9 1.8 %final.5 = bf16[640,3456]{1,0:T(8,128)(2,1)} custom-call(s32[1]{0:T(128)} %bitcast.2.where_ref, f32[864,2560]{1,0:T(8,128)S(1)} %bitcast.7, bf16[864,128]{1,0:T(8,128)(2,1)S(1)} %collective-permute-done.one_ref, bf16[864,128]{1,0:T(8,128)(2,1)S(1)} %collective-permute-done.1.two_ref, ...), custom_call_target="tpu_custom_call", output_to_operand_aliasing={{}: (8, {})} | custom-call | flops 339738624 | bytes 2654208 | tf_op jit(solution)/shard_map/final/pallas_call | solution.py:322
Async XLA Ops:
  41.5 34.8 %collective-permute-start.3 = (bf16[864,256]{1,0:T(8,128)(2,1)}, bf16[864,256]{1,0:T(8,128)(2,1)S(1)}, u32[]{:S(2)}, u32[]{:S(2)}) collective-permute-start(bf16[864,256]{1,0:T(8,128)(2,1)} %get-tuple-element.28), channel_id=1, source_target_pairs={{0,1},{1,0},{2,3},{3,2},{4,5},{5,4},{6,7},{7,6},{8,9},{9,8},{10,11... | collective-permute-start | bytes 1327112 | tf_op jit(solution)/shard_map/ppermute | solution.py:440
  47.2 47.3 %collective-permute-start.6 = (bf16[864,256]{1,0:T(8,128)(2,1)}, bf16[864,256]{1,0:T(8,128)(2,1)S(1)}, u32[]{:S(2)}, u32[]{:S(2)}) collective-permute-start(bf16[864,256]{1,0:T(8,128)(2,1)} %get-tuple-element.31), channel_id=1, source_target_pairs={{0,1},{1,0},{2,3},{3,2},{4,5},{5,4},{6,7},{7,6},{8,9},{9,8},{10,11... | collective-permute-start | bytes 1327112 | tf_op jit(solution)/shard_map/ppermute | solution.py:440
  47.2 47.2 %collective-permute-start.7 = (bf16[864,256]{1,0:T(8,128)(2,1)}, bf16[864,256]{1,0:T(8,128)(2,1)S(1)}, u32[]{:S(2)}, u32[]{:S(2)}) collective-permute-start(bf16[864,256]{1,0:T(8,128)(2,1)} %get-tuple-element.32), channel_id=1, source_target_pairs={{0,2},{1,3},{2,0},{3,1},{4,6},{5,7},{6,4},{7,5},{8,10},{9,11},{10,... | collective-permute-start | bytes 1327112 | tf_op jit(solution)/shard_map/ppermute | solution.py:440
  50.1 47.2 %collective-permute-start.8 = (bf16[864,256]{1,0:T(8,128)(2,1)}, bf16[864,256]{1,0:T(8,128)(2,1)S(1)}, u32[]{:S(2)}, u32[]{:S(2)}) collective-permute-start(bf16[864,256]{1,0:T(8,128)(2,1)} %get-tuple-element.33), channel_id=1, source_target_pairs={{0,3},{3,0},{4,7},{7,4},{8,11},{11,8},{12,15},{15,12},{16,19},{19,... | collective-permute-start | bytes 1327112 | tf_op jit(solution)/shard_map/ppermute | solution.py:440
  53.5 58.8 %collective-permute-start.4 = (bf16[864,256]{1,0:T(8,128)(2,1)}, bf16[864,256]{1,0:T(8,128)(2,1)S(1)}, u32[]{:S(2)}, u32[]{:S(2)}) collective-permute-start(bf16[864,256]{1,0:T(8,128)(2,1)} %get-tuple-element.29), channel_id=1, source_target_pairs={{0,2},{1,3},{2,0},{3,1},{4,6},{5,7},{6,4},{7,5},{8,10},{9,11},{10,... | collective-permute-start | bytes 1327112 | tf_op jit(solution)/shard_map/ppermute | solution.py:440
  76.2 36.0 %collective-permute-start.5 = (bf16[864,256]{1,0:T(8,128)(2,1)}, bf16[864,256]{1,0:T(8,128)(2,1)S(1)}, u32[]{:S(2)}, u32[]{:S(2)}) collective-permute-start(bf16[864,256]{1,0:T(8,128)(2,1)} %get-tuple-element.30), channel_id=1, source_target_pairs={{0,3},{3,0},{4,7},{7,4},{8,11},{11,8},{12,15},{15,12},{16,19},{19,... | collective-permute-start | bytes 1327112 | tf_op jit(solution)/shard_map/ppermute | solution.py:440
  81.3 1.5 %copy-start.1 = (bf16[256,3456]{1,0:T(8,128)(2,1)S(1)}, bf16[256,3456]{1,0:T(8,128)(2,1)}, u32[]{:S(2)}) copy-start(bf16[256,3456]{1,0:T(8,128)(2,1)} %get-tuple-element.19.refs_1_.right_ref) | copy-start | bytes 5308420
  82.8 1.3 %copy-start.4 = (bf16[256,2560]{1,0:T(8,128)(2,1)S(1)}, bf16[256,2560]{1,0:T(8,128)(2,1)}, u32[]{:S(2)}) copy-start(bf16[256,2560]{1,0:T(8,128)(2,1)} %get-tuple-element.18.refs_0_) | copy-start | bytes 3932164
  84.1 0.7 copy-start.5
  94.4 21.2 %collective-permute-start = (bf16[864,128]{1,0:T(8,128)(2,1)}, bf16[864,128]{1,0:T(8,128)(2,1)S(1)}, u32[]{:S(2)}, u32[]{:S(2)}) collective-permute-start(bf16[864,128]{1,0:T(8,128)(2,1)} %get-tuple-element.23), channel_id=1, source_target_pairs={{0,1},{1,0},{2,3},{3,2},{4,5},{5,4},{6,7},{7,6},{8,9},{9,8},{10,11... | collective-permute-start | bytes 663560 | tf_op jit(solution)/shard_map/ppermute | solution.py:440
  94.4 27.4 %collective-permute-start.1 = (bf16[864,128]{1,0:T(8,128)(2,1)}, bf16[864,128]{1,0:T(8,128)(2,1)S(1)}, u32[]{:S(2)}, u32[]{:S(2)}) collective-permute-start(bf16[864,128]{1,0:T(8,128)(2,1)} %get-tuple-element.24), channel_id=1, source_target_pairs={{0,2},{1,3},{2,0},{3,1},{4,6},{5,7},{6,4},{7,5},{8,10},{9,11},{10,... | collective-permute-start | bytes 663560 | tf_op jit(solution)/shard_map/ppermute | solution.py:440
  97.3 24.6 %collective-permute-start.2 = (bf16[864,128]{1,0:T(8,128)(2,1)}, bf16[864,128]{1,0:T(8,128)(2,1)S(1)}, u32[]{:S(2)}, u32[]{:S(2)}) collective-permute-start(bf16[864,128]{1,0:T(8,128)(2,1)} %get-tuple-element.25), channel_id=1, source_target_pairs={{0,3},{3,0},{4,7},{7,4},{8,11},{11,8},{12,15},{15,12},{16,19},{19,... | collective-permute-start | bytes 663560 | tf_op jit(solution)/shard_map/ppermute | solution.py:440
  100.7 3.5 %copy-start = (f32[2560,864]{0,1:T(8,128)S(1)}, f32[2560,864]{0,1:T(8,128)}, u32[]{:S(2)}) copy-start(f32[2560,864]{0,1:T(8,128)} %param.4) | copy-start | bytes 26542084
  104.3 4.9 %copy-start.2 = (bf16[256,3456]{1,0:T(8,128)(2,1)S(1)}, bf16[256,3456]{1,0:T(8,128)(2,1)}, u32[]{:S(2)}) copy-start(bf16[256,3456]{1,0:T(8,128)(2,1)} %get-tuple-element.19.refs_1_.right_ref) | copy-start | bytes 5308420
  104.3 4.9 %copy-start.3 = (bf16[864,640]{1,0:T(8,128)(2,1)S(1)}, bf16[864,640]{1,0:T(8,128)(2,1)}, u32[]{:S(2)}) copy-start(bf16[864,640]{1,0:T(8,128)(2,1)} %get-tuple-element.26.early_ref) | copy-start | bytes 3317764

commit v2 on v1

--- a/solution.py
+++ b/solution.py
@@ -58,10 +58,10 @@
 
 def exchange_kernel(members, chunks, left_ref, right_ref, returns_ref, master_ref, *refs):
     sides = 3
-    l_ref, r_ref, s_ref, p_ref, e_ref, *refs = refs
+    l_ref, r_ref, s_ref, p_ref, e_ref, n_ref, b_ref, *refs = refs
     blocks, refs = refs[:sides * len(chunks)], refs[sides * len(chunks):]
-    (wide, narrow, part, own_sem, pull_sem, push_sem, s_send, s_recv, x_send, x_recv, f_send, f_recv,
-     z_send, z_recv, q_send, q_recv, y_send, y_recv, e_send, e_recv) = refs
+    (wide, narrow, part, own_sem, pull_sem, push_sem, s_send, s_recv, t_send, t_recv, x_send, x_recv, f_send, f_recv,
+     z_send, z_recv, q_send, q_recv, y_send, y_recv, e_send, e_recv, n_send, n_recv, b_send, b_recv) = refs
     me, te, an = lax.axis_index("member"), lax.axis_index("tensor"), lax.axis_index("answer")
     answers = 4
     local = left_ref.shape[0]
@@ -74,6 +74,7 @@
     near, far = beside(an), 2 - lax.div(an, 2)
     beyond = 2 * (1 - lax.div(an, 2))
     inner = lax.div(an + 1, 2) == 1
+    outer = jnp.logical_not(inner)
     pair = {1: near, 2: lax.rem(an + 2, answers), 3: answers - 1 - an}
 
     def l_at(start, count, t):
@@ -112,13 +113,19 @@
             push(x, c).start()
 
     barrier = pltpu.get_barrier_semaphore()
-    peers = [(dm, da) for dm in range(members) for da in range(answers) if (dm, da) != (0, 0)]
-    place = lambda dm, da: {"member": lax.rem(me + dm, members), "answer": lax.rem(an + da, answers)}
-    for dm, da in peers:
-        pl.semaphore_signal(barrier, inc=1, device_id=place(dm, da), device_id_type=pl.DeviceIdType.MESH)
-    for t in (core, across):
-        pl.semaphore_signal(barrier, inc=1, device_id={"tensor": t}, device_id_type=pl.DeviceIdType.MESH)
-    pull(3).start()
+
+    def greet(where):
+        pl.semaphore_signal(barrier, inc=1, device_id=where, device_id_type=pl.DeviceIdType.MESH)
+
+    for where in ({"answer": near}, {"member": other}, {"tensor": core}, {"tensor": across}):
+        greet(where)
+
+    @pl.when(inner)
+    def _():
+        greet({"answer": beyond})
+        greet({"answer": beyond + 1})
+
+    pull(1).start()
     pull(2).start()
     own_l = pltpu.make_async_copy(
         left_ref.at[:, pl.ds(pl.multiple_of(me * tile + te * piece, piece), piece)],
@@ -132,7 +139,7 @@
     own_p.start()
     own_s.start()
 
-    pl.semaphore_wait(barrier, len(peers) + 2)
+    pl.semaphore_wait(barrier, 5)
 
     mine = lax.rem(an, 2)
     halves = 2
@@ -171,8 +178,10 @@
 
     part_of(0)
     own_p.wait()
-    for i, (dm, da) in enumerate(peers):
-        start(remote(p_ref, s_ref.at[an * members + me], s_send.at[i], s_recv.at[i], place(dm, da)))
+    score = lambda a, m: s_ref.at[a * members + m]
+    start(remote(p_ref, score(an, me), s_send.at[0], s_recv.at[mine + 1], {"answer": far}))
+    start(remote(p_ref, score(an, me), s_send.at[1], s_recv.at[0], {"answer": near}))
+    start(remote(p_ref, score(an, me), t_send.at[0], t_recv.at[0], {"member": other}))
     own_l.wait()
     landed(l_at((an * members + other) * local, local, te), x_recv.at[0])
     block = l_slab(an, te)
@@ -182,21 +191,32 @@
     spread(0)
     for h in range(halves):
         forward(0, h)
+    last = len(chunks) - 1
+    cast(1)
+    push(1, last).wait()
+    aside = remote(blocks[last], b_ref, b_send, b_recv, {"answer": near})
+    pl.when(inner)(aside.start)
+    for c in range(last):
+        push(1, c).wait()
+    pull(3).start()
+    cast(2)
+    push(2, last).wait()
+    cross = remote(blocks[len(chunks) + last], n_ref, n_send, n_recv, {"answer": far})
+    pl.when(outer)(cross.start)
     cast(3)
     early = []
-    for c, size in enumerate(chunks):
+    push(3, last).wait()
+    for c, size in enumerate(chunks[:last]):
         push(3, c).wait()
         at = sum(chunks[:c])
         copy = remote(blocks[2 * len(chunks) + c], e_ref.at[:, at:at + size], e_send.at[c], e_recv.at[c], {"answer": pair[3]})
         pl.when(inner)(copy.start)
         early.append(copy)
-    pull(1).start()
     for h in range(halves):
         landed(r_half(near, me, h), z_recv.at[0, h])
         forward(1, h)
     landed(l_slab(near, te), q_recv.at[0])
     spread(1)
-    cast(2)
     relays = []
 
     def relay(block, send, recv):
@@ -222,9 +242,14 @@
         block = l_slab(sources[k], across)
         landed(block, y_recv.at[k, 0])
         start(remote(block, block, y_send.at[k, 2], y_recv.at[k, 2], {"tensor": core}))
-    cast(1)
-    for i, (dm, da) in enumerate(peers):
-        landed(s_ref.at[lax.rem(an + answers - da, answers) * members + lax.rem(me + members - dm, members)], s_recv.at[i])
+    for k in range(1, answers):
+        block = score(sources[k], me)
+        landed(block, s_recv.at[k - 1])
+        if k > 1:
+            relay(block, s_send.at[k], s_recv.at[k - 1])
+        start(remote(block, block, t_send.at[k], t_recv.at[k], {"member": other}))
+    for k in range(answers):
+        landed(score(sources[k], other), t_recv.at[k])
     for k in range(answers):
         for h in range(halves):
             landed(r_half(sources[k], other, h), f_recv.at[k, h])
@@ -233,15 +258,18 @@
         landed(l_slab(sources[k], 3 - te), y_recv.at[k, 2])
     own_r.wait()
     own_s.wait()
-    for x in (2, 1):
-        for c in range(len(chunks)):
-            push(x, c).wait()
+    for c in range(last):
+        push(2, c).wait()
     for copy in started:
         copy.wait_send()
     for copy in relays + early:
         pl.when(inner)(copy.wait_send)
     for copy in early:
         pl.when(inner)(copy.wait_recv)
+    pl.when(outer)(cross.wait_send)
+    pl.when(inner)(cross.wait_recv)
+    pl.when(inner)(aside.wait_send)
+    pl.when(outer)(aside.wait_recv)
 
 
 def exchange(left_noise, right_noise, returns, transposed, members, chunks):
@@ -262,17 +290,19 @@
             shape((total, width), half),
             shape((count, 1, block), jnp.float32),
             shape((1, block), jnp.float32),
-            shape((cols, tile // answers), half),
+            shape((cols, sum(chunks[:-1])), half),
+            shape((cols, chunks[-1]), half),
+            shape((cols, chunks[-1]), half),
         ) + tuple(shape((cols, size), half) for _ in range(sides) for size in chunks),
         in_specs=[vmem] * 3 + [anywhere],
-        out_specs=(anywhere,) * (5 + sides * len(chunks)),
+        out_specs=(anywhere,) * (7 + sides * len(chunks)),
         scratch_shapes=[
             pltpu.VMEM((2, cols, tile // answers), jnp.float32), pltpu.VMEM((2, cols, tile // answers), half),
             pltpu.VMEM((1, block), jnp.float32),
-            dma((4,)), dma((sides,)), dma((sides, len(chunks))), dma((count - 1,)), dma((count - 1,)),
+            dma((4,)), dma((sides,)), dma((sides, len(chunks))), dma((4,)), dma((3,)), dma((4,)), dma((4,)),
             dma((1,)), dma((1,)), dma((answers, 2)), dma((answers, 2)),
             dma((4, 2)), dma((3, 2)), dma((4,)), dma((3,)), dma((answers, 3)), dma((answers, 3)),
-            dma((len(chunks),)), dma((len(chunks),)),
+            dma((len(chunks) - 1,)), dma((len(chunks) - 1,)), dma, dma, dma, dma,
         ],
         compiler_params=pltpu.CompilerParams(collective_id=0, has_side_effects=True),
         name="exchange",
@@ -284,21 +314,25 @@
     return fits[-1] if fits else size
 
 
-def final_kernel(where_ref, master_ref, one_ref, two_ref, three_ref, early_ref, left_ref, right_ref, *refs):
-    out_ref, stack = refs[-2:]
+def final_kernel(picks, where_ref, master_ref, *refs):
+    sides, refs = refs[:len(picks)], refs[len(picks):]
+    left_ref, right_ref, out_ref, stack = refs[0], refs[1], refs[-2], refs[-1]
     an = lax.axis_index("answer")
     width, rows = master_ref.shape
     near = an + 1 - 2 * lax.rem(an, 2)
     inner = lax.div(an + 1, 2) == 1
+    places = {1: near, 2: lax.rem(an + 2, 4), 3: 3 - an}
+    within = {True: inner, False: jnp.logical_not(inner)}
 
     def place(a, ref):
         stack[pl.ds(pl.multiple_of(a * width, 16), width), :] = ref[...].astype(stack.dtype)
 
     place(an, master_ref)
-    place(near, one_ref)
-    place(lax.rem(an + 2, 4), two_ref)
-    pl.when(inner)(lambda: place(3 - an, early_ref))
-    pl.when(jnp.logical_not(inner))(lambda: place(3 - an, three_ref))
+    for (x, which), ref in zip(picks, sides):
+        if which is None:
+            place(places[x], ref)
+        else:
+            pl.when(within[which])(lambda x=x, ref=ref: place(places[x], ref))
     row = lax.broadcasted_iota(jnp.int32, (rows, rows), 0)
     col = lax.broadcasted_iota(jnp.int32, (rows, rows), 1)
     unit = jnp.where(row == col, 1.0, 0.0).astype(stack.dtype)
@@ -310,24 +344,22 @@
         out_ref[:, cols] = (new + old).astype(out_ref.dtype)
 
 
-def finalize(where, transposed, sides, early, left, right, first, size, so_far):
+def finalize(where, transposed, sides, left, right, first, size, so_far):
     rows, members = left.shape
     width = transposed.shape[0]
     total = right.shape[1]
     chunk = 128
     start, steps = first // chunk, size // chunk
     per = rows // chunk
-    side = pl.BlockSpec((width, chunk), lambda i, w: (0, i))
     more = [] if so_far is None else [so_far]
+    picks = tuple(key for key, _, _ in sides)
+    blocks = [pl.BlockSpec((width, chunk), lambda i, w, at=at: (0, at + i)) for _, _, at in sides]
     return pl.pallas_call(
-        final_kernel,
+        lambda *refs: final_kernel(picks, *refs),
         grid_spec=pltpu.PrefetchScalarGridSpec(
             num_scalar_prefetch=1,
             grid=(steps,),
-            in_specs=[
-                pl.BlockSpec((width, chunk), lambda i, w: (0, w[0] * per + start + i)),
-                side, side, side,
-                pl.BlockSpec((width, chunk), lambda i, w: (0, start + i)),
+            in_specs=[pl.BlockSpec((width, chunk), lambda i, w: (0, w[0] * per + start + i))] + blocks + [
                 pl.BlockSpec((chunk, members), lambda i, w: (start + i, 0)),
                 pl.BlockSpec((members, total), lambda i, w: (0, 0)),
             ] + [pl.BlockSpec(memory_space=pl.ANY)] * len(more),
@@ -335,12 +367,12 @@
             scratch_shapes=[pltpu.VMEM((total, chunk), jnp.bfloat16)],
         ),
         out_shape=jax.ShapeDtypeStruct((rows, total), jnp.bfloat16),
-        input_output_aliases={8: 0} if more else {},
+        input_output_aliases={4 + len(sides): 0} if more else {},
         cost_estimate=pl.CostEstimate(
             flops=2 * size * total * (members + chunk), bytes_accessed=6 * size * total, transcendentals=0),
         compiler_params=pltpu.CompilerParams(vmem_limit_bytes=24 << 20),
         name="final",
-    )(where, transposed, *sides, early, left, right, *more)
+    )(where, transposed, *[block for _, block, _ in sides], left, right, *more)
 
 
 def update_kernel(master_ref, right_ref, left_ref, new_ref):
@@ -423,7 +455,7 @@
 
 
 def order_of(count):
-    return [(c, x) for c in range(count) for x in (3, 2, 1)]
+    return [(c, x) for c in range(count) for x in (3, 2, 1)] + [(count - 1, 4)]
 
 
 def fast_body(master, left_noise, right_noise, returns):
@@ -433,22 +465,30 @@
     width, tile = transposed.shape
     rows = tile // answers
     chunks = split(rows)
-    left_tile, right, parts, _, early, *blocks = exchange(left_noise, right_noise, returns, transposed, members, chunks)
+    last = len(chunks) - 1
+    left_tile, right, parts, _, early, cross, aside, *blocks = exchange(left_noise, right_noise, returns, transposed, members, chunks)
     blocks = [blocks[i:i + len(chunks)] for i in range(0, len(blocks), len(chunks))]
+    pairs = {1: [(0, 1), (1, 0), (2, 3), (3, 2)], 2: [(1, 3), (2, 0), (0, 2), (3, 1)], 3: [(0, 3), (3, 0)], 4: [(1, 2), (2, 1)]}
     got = {}
     for c, x in order_of(len(chunks)):
-        got[c, x] = lax.ppermute(blocks[x - 1][c], "answer", [(i, i ^ x) for i in range(answers) if x < 3 or i in (0, 3)])
+        some = {(last, 2): pairs[2][:2], (last, 1): pairs[1][::3]}.get((c, x), pairs[x])
+        got[c, x] = lax.ppermute(blocks[min(x, 3) - 1][c], "answer", some)
     weighted, own, turned = weigh(left_tile, right, parts, members, rows, width)
     new_master = update(transposed, turned, weighted)
     rollout, at = None, 0
     for c, size in enumerate(chunks):
-        rollout = finalize(where, transposed, [got[c, x] for x in (1, 2, 3)], early, own, right, at, size, rollout)
+        sides = [((1, True if c == last else None), got[c, 1], 0), ((3, False), got[c, 3], 0)]
+        if c == last:
+            sides += [((1, False), aside, 0), ((2, True), cross, 0), ((2, False), got[c, 2], 0), ((3, True), got[c, 4], 0)]
+        else:
+            sides += [((2, None), got[c, 2], 0), ((3, True), early, at // 128)]
+        rollout = finalize(where, transposed, sides, own, right, at, size, rollout)
         at += size
     return (new_master.T, rollout)
 
 
 def fits(members, tensors, answers, tile, local):
-    return (members, tensors, answers) == (2, 4, 4) and tile % 512 == 0 and local % 32 == 0
+    return (members, tensors, answers) == (2, 4, 4) and tile % 512 == 0 and tile >= 1024 and local % 32 == 0
 
 
 def body(master, left_noise, right_noise, returns):

time: 124 us -> 125 us (level)
  waiting for transfers between devices: 37.9 us -> 40.6 us
    ppermute x9 -> x10, waiting for transfers between devices: 37.9 us -> 40.6 us  [fast_body(): got[c, x] = lax.ppermute(blocks[min(x, 3) - 1][c], 'answer', some)]
    ppermute x9 -> x10, starting transfers between devices: 23.4 us -> 22.3 us  [fast_body(): got[c, x] = lax.ppermute(blocks[min(x, 3) - 1][c], 'answer', some)]
    unnamed x12 -> x16, local copies, waits for them, and re-layouts: 6.98 us -> 7 us
  transfers between devices with their start and end apart: 9 -> 10, of which waited for: 4 -> 5; matrix products, arithmetic and copies ran while one was open for 0% -> 0% of each run, Pallas kernels for 10% -> 10%
where the time goes in v2:
time: 125 us
  Pallas kernels  54.1 us (43%)
  waiting for transfers between devices  40.6 us (32%)
  starting transfers between devices  22.3 us (18%)
  local copies, waits for them, and re-layouts  7 us (6%)
    ppermute x10, waiting for transfers between devices, fast_body(): got[c, x] = lax.ppermute(blocks[min(x, 3) - 1][c], 'answer', some)  40.6 us
    pallas_call x1, Pallas kernels, exchange(): pl.pallas_call(lambda *refs: exchange_kernel(members, chunks, *refs), out...  40.3 us
    ppermute x10, starting transfers between devices, fast_body(): got[c, x] = lax.ppermute(blocks[min(x, 3) - 1][c], 'answer', some)  22.3 us
    pallas_call x3, Pallas kernels, finalize(): pl.pallas_call(lambda *refs: final_kernel(picks, *refs), grid_spec=pltpu....  7.93 us
    unnamed x16, local copies, waits for them, and re-layouts  7 us
    pallas_call x1, Pallas kernels, update(): pl.pallas_call(update_kernel, grid=(width // chunk,), in_specs=[pl.BlockS...  4.91 us
  transfers between devices with their start and end apart: 10, of which 5 were waited for; matrix products, arithmetic and copies ran while one was open for 0% of the time, Pallas kernels for 10%

profile of v2, /device:TPU:0, one launch (start us, length us, event | category | flops | bytes accessed | tf_op | source)
XLA Modules:
  0.0 124.7 jit_solution(5346570893573792130)
XLA Ops:
  0.6 40.3 %exchange.1 = (bf16[256,2560]{1,0:T(8,128)(2,1)}, bf16[256,3456]{1,0:T(8,128)(2,1)}, f32[8,1,128]{2,1,0:T(1,128)}, f32[1,128]{1,0:T(1,128)}, bf16[864,512]{1,0:T...) custom-call(bf16[32,5120]{1,0:T(8,128)(2,1)} %refs_0_.1, ...), custom_call_target="tpu_custom_call" | custom-call | tf_op jit(solution)/shard_map/exchange/pallas_call | solution.py:286
  40.9 5.2 %collective-permute-start.7 = (bf16[864,256]{1,0:T(8,128)(2,1)}, bf16[864,256]{1,0:T(8,128)(2,1)S(1)}, u32[]{:S(2)}, u32[]{:S(2)}) collective-permute-start(bf16[864,256]{1,0:T(8,128)(2,1)} %get-tuple-element.35), channel_id=1, source_target_pairs={{0,1},{1,0},{2,3},{3,2},{4,5},{5,4},{6,7},{7,6},{8,9},{9,8},{10,11... | collective-permute-start | bytes 1327112 | tf_op jit(solution)/shard_map/ppermute | solution.py:475
  46.2 3.2 %collective-permute-start.8 = (bf16[864,256]{1,0:T(8,128)(2,1)}, bf16[864,256]{1,0:T(8,128)(2,1)S(1)}, u32[]{:S(2)}, u32[]{:S(2)}) collective-permute-start(bf16[864,256]{1,0:T(8,128)(2,1)} %get-tuple-element.36), channel_id=1, source_target_pairs={{0,3},{3,0},{4,7},{7,4},{8,11},{11,8},{12,15},{15,12},{16,19},{19,... | collective-permute-start | bytes 1327112 | tf_op jit(solution)/shard_map/ppermute | solution.py:475
  49.4 0.1 collective-permute-start.9
  49.5 3.0 %collective-permute-start.4 = (bf16[864,256]{1,0:T(8,128)(2,1)}, bf16[864,256]{1,0:T(8,128)(2,1)S(1)}, u32[]{:S(2)}, u32[]{:S(2)}) collective-permute-start(bf16[864,256]{1,0:T(8,128)(2,1)} %get-tuple-element.31), channel_id=1, source_target_pairs={{0,1},{1,0},{2,3},{3,2},{4,5},{5,4},{6,7},{7,6},{8,9},{9,8},{10,11... | collective-permute-start | bytes 1327112 | tf_op jit(solution)/shard_map/ppermute | solution.py:475
  52.5 3.2 %collective-permute-start.5 = (bf16[864,256]{1,0:T(8,128)(2,1)}, bf16[864,256]{1,0:T(8,128)(2,1)S(1)}, u32[]{:S(2)}, u32[]{:S(2)}) collective-permute-start(bf16[864,256]{1,0:T(8,128)(2,1)} %get-tuple-element.32), channel_id=1, source_target_pairs={{0,3},{3,0},{4,7},{7,4},{8,11},{11,8},{12,15},{15,12},{16,19},{19,... | collective-permute-start | bytes 1327112 | tf_op jit(solution)/shard_map/ppermute | solution.py:475
  55.8 16.3 %collective-permute-done.7.refs_2_ = bf16[864,256]{1,0:T(8,128)(2,1)S(1)} collective-permute-done((bf16[864,256]{1,0:T(8,128)(2,1)}, bf16[864,256]{1,0:T(8,128)(2,1)S(1)}, u32[]{:S(2)}, u32[]{:S(2)}) %collective-permute-start.7) | collective-permute-done | bytes 442400 | tf_op jit(solution)/shard_map/ppermute | solution.py:475
  72.1 0.0 collective-permute-start.6
  72.1 0.0 copy-start.1
  72.1 1.5 %copy-done.1 = bf16[256,3456]{1,0:T(8,128)(2,1)S(1)} copy-done((bf16[256,3456]{1,0:T(8,128)(2,1)S(1)}, bf16[256,3456]{1,0:T(8,128)(2,1)}, u32[]{:S(2)}) %copy-start.1) | copy-done | bytes 1769496
  73.6 0.0 copy-start.4
  73.6 1.3 %copy-done.4 = bf16[256,2560]{1,0:T(8,128)(2,1)S(1)} copy-done((bf16[256,2560]{1,0:T(8,128)(2,1)S(1)}, bf16[256,2560]{1,0:T(8,128)(2,1)}, u32[]{:S(2)}) %copy-start.4) | copy-done | bytes 1310744
  74.9 0.0 copy-start.7
  74.9 0.7 copy-done.7
  75.6 1.0 weigh.1
  76.6 0.0 collective-permute-done.8.refs_3_
  76.6 3.9 %collective-permute-start.1 = (bf16[864,128]{1,0:T(8,128)(2,1)}, bf16[864,128]{1,0:T(8,128)(2,1)S(1)}, u32[]{:S(2)}, u32[]{:S(2)}) collective-permute-start(bf16[864,128]{1,0:T(8,128)(2,1)} %get-tuple-element.26), channel_id=1, source_target_pairs={{0,3},{3,0},{4,7},{7,4},{8,11},{11,8},{12,15},{15,12},{16,19},{19,... | collective-permute-start | bytes 663560 | tf_op jit(solution)/shard_map/ppermute | solution.py:475
  80.5 2.2 %collective-permute-done.9.refs_4_ = bf16[864,256]{1,0:T(8,128)(2,1)S(1)} collective-permute-done((bf16[864,256]{1,0:T(8,128)(2,1)}, bf16[864,256]{1,0:T(8,128)(2,1)S(1)}, u32[]{:S(2)}, u32[]{:S(2)}) %collective-permute-start.9) | collective-permute-done | bytes 442400 | tf_op jit(solution)/shard_map/ppermute | solution.py:475
  82.7 0.7 collective-permute-start.3
  83.4 15.5 %collective-permute-done.4.refs_2_ = bf16[864,256]{1,0:T(8,128)(2,1)S(1)} collective-permute-done((bf16[864,256]{1,0:T(8,128)(2,1)}, bf16[864,256]{1,0:T(8,128)(2,1)S(1)}, u32[]{:S(2)}, u32[]{:S(2)}) %collective-permute-start.4) | collective-permute-done | bytes 442400 | tf_op jit(solution)/shard_map/ppermute | solution.py:475
  98.9 1.6 %collective-permute-start = (bf16[864,128]{1,0:T(8,128)(2,1)}, bf16[864,128]{1,0:T(8,128)(2,1)S(1)}, u32[]{:S(2)}, u32[]{:S(2)}) collective-permute-start(bf16[864,128]{1,0:T(8,128)(2,1)} %get-tuple-element.25), channel_id=1, source_target_pairs={{0,1},{3,2},{4,5},{7,6},{8,9},{11,10},{12,13},{15,14},{16,17},{19,... | collective-permute-start | bytes 663560 | tf_op jit(solution)/shard_map/ppermute | solution.py:475
  100.5 0.0 collective-permute-done.5.refs_3_
  100.5 1.3 %collective-permute-start.2 = (bf16[864,128]{1,0:T(8,128)(2,1)}, bf16[864,128]{1,0:T(8,128)(2,1)S(1)}, u32[]{:S(2)}, u32[]{:S(2)}) collective-permute-start(bf16[864,128]{1,0:T(8,128)(2,1)} %get-tuple-element.29), channel_id=1, source_target_pairs={{1,3},{2,0},{5,7},{6,4},{9,11},{10,8},{13,15},{14,12},{17,19},{18,... | collective-permute-start | bytes 663560 | tf_op jit(solution)/shard_map/ppermute | solution.py:475
  101.8 0.0 copy-start
  101.8 3.5 %copy-done = f32[2560,864]{0,1:T(8,128)S(1)} copy-done((f32[2560,864]{0,1:T(8,128)S(1)}, f32[2560,864]{0,1:T(8,128)}, u32[]{:S(2)}) %copy-start) | copy-done | bytes 8847384
  105.3 0.0 copy-start.2
  105.3 0.0 copy-start.3
  105.3 4.9 %update.1 = f32[864,2560]{1,0:T(8,128)} custom-call(f32[864,2560]{1,0:T(8,128)S(1)} %bitcast.4, bf16[864,256]{1,0:T(8,128)(2,1)S(1)} %get-tuple-element.23.right_ref, bf16[256,2560]{1,0:T(8,128)(2,1)S(1)} %get-tuple-element.24.left_ref), custom_call_target="tpu_custom_call" | custom-call | flops 1132462080 | bytes 17694720 | tf_op jit(solution)/shard_map/update/pallas_call | solution.py:386
  110.2 0.0 copy-done.2
  110.2 0.0 copy-done.3
  110.2 3.1 %final.3.refs_8_ = bf16[640,3456]{1,0:T(8,128)(2,1)} custom-call(s32[1]{0:T(128)} %bitcast.2.refs_0_, f32[864,2560]{1,0:T(8,128)S(1)} %bitcast.5, bf16[864,256]{1,0:T(8,128)(2,1)S(1)} %collective-permute-done.7.refs_2_, bf16[864,256]{1,0:T(8,128)(2,1)S(1)} %collective-permute-done.8.refs_3_, bf16[864,256]{1,0:T(8,128)(2,1)S(1)} %collective-permute-done.9.refs_4_, ...), custom_call_target="tpu_custom_call" | custom-call | flops 679477248 | bytes 5308416 | tf_op jit(solution)/shard_map/final/pallas_call | solution.py:357
  113.3 0.0 copy-start.5
  113.3 0.0 copy-start.6
  113.3 2.6 %collective-permute-done.6.refs_4_ = bf16[864,256]{1,0:T(8,128)(2,1)S(1)} collective-permute-done((bf16[864,256]{1,0:T(8,128)(2,1)}, bf16[864,256]{1,0:T(8,128)(2,1)S(1)}, u32[]{:S(2)}, u32[]{:S(2)}) %collective-permute-start.6) | collective-permute-done | bytes 442400 | tf_op jit(solution)/shard_map/ppermute | solution.py:475
  115.8 3.1 %final.4.refs_10_ = bf16[640,3456]{1,0:T(8,128)(2,1)} custom-call(s32[1]{0:T(128)} %bitcast.2.refs_0_, f32[864,2560]{1,0:T(8,128)S(1)} %bitcast.6, bf16[864,256]{1,0:T(8,128)(2,1)S(1)} %collective-permute-done.4.refs_2_, bf16[864,256]{1,0:T(8,128)(2,1)S(1)} %collective-permute-done.5.refs_3_, ...), custom_call_target="tpu_custom_call", output_to_operand_aliasing={{}: (8, {})} | custom-call | flops 679477248 | bytes 5308416 | tf_op jit(solution)/shard_map/final/pallas_call | solution.py:357
  118.9 0.0 collective-permute-done.1.refs_3_
  118.9 0.0 collective-permute-done.3.refs_7_
  118.9 0.0 collective-permute-done.refs_2_
  118.9 4.0 %collective-permute-done.2.refs_6_ = bf16[864,128]{1,0:T(8,128)(2,1)S(1)} collective-permute-done((bf16[864,128]{1,0:T(8,128)(2,1)}, bf16[864,128]{1,0:T(8,128)(2,1)S(1)}, u32[]{:S(2)}, u32[]{:S(2)}) %collective-permute-start.2) | collective-permute-done | bytes 221216 | tf_op jit(solution)/shard_map/ppermute | solution.py:475
  122.9 0.0 copy-done.5
  122.9 0.0 copy-done.6
  122.9 1.8 %final.5 = bf16[640,3456]{1,0:T(8,128)(2,1)} custom-call(s32[1]{0:T(128)} %bitcast.2.refs_0_, f32[864,2560]{1,0:T(8,128)S(1)} %bitcast.7, bf16[864,128]{1,0:T(8,128)(2,1)S(1)} %collective-permute-done.refs_2_, bf16[864,128]{1,0:T(8,128)(2,1)S(1)} %collective-permute-done.1.refs_3_, bf16[864,128]{1,0:T(8,128)(2,1)S(1)} %copy-done.6, ...), custom_call_target="tpu_custom_call", output_to_operand_aliasing={{}: (10, {})} | custom-call | flops 339738624 | bytes 2654208 | tf_op jit(solution)/shard_map/final/pallas_call | solution.py:357
Async XLA Ops:
  40.9 31.1 %collective-permute-start.7 = (bf16[864,256]{1,0:T(8,128)(2,1)}, bf16[864,256]{1,0:T(8,128)(2,1)S(1)}, u32[]{:S(2)}, u32[]{:S(2)}) collective-permute-start(bf16[864,256]{1,0:T(8,128)(2,1)} %get-tuple-element.35), channel_id=1, source_target_pairs={{0,1},{1,0},{2,3},{3,2},{4,5},{5,4},{6,7},{7,6},{8,9},{9,8},{10,11... | collective-permute-start | bytes 1327112 | tf_op jit(solution)/shard_map/ppermute | solution.py:475
  46.2 30.4 %collective-permute-start.8 = (bf16[864,256]{1,0:T(8,128)(2,1)}, bf16[864,256]{1,0:T(8,128)(2,1)S(1)}, u32[]{:S(2)}, u32[]{:S(2)}) collective-permute-start(bf16[864,256]{1,0:T(8,128)(2,1)} %get-tuple-element.36), channel_id=1, source_target_pairs={{0,3},{3,0},{4,7},{7,4},{8,11},{11,8},{12,15},{15,12},{16,19},{19,... | collective-permute-start | bytes 1327112 | tf_op jit(solution)/shard_map/ppermute | solution.py:475
  49.4 33.3 %collective-permute-start.9 = (bf16[864,256]{1,0:T(8,128)(2,1)}, bf16[864,256]{1,0:T(8,128)(2,1)S(1)}, u32[]{:S(2)}, u32[]{:S(2)}) collective-permute-start(bf16[864,256]{1,0:T(8,128)(2,1)} %get-tuple-element.37), channel_id=1, source_target_pairs={{1,3},{2,0},{0,2},{3,1},{5,7},{6,4},{4,6},{7,5},{9,11},{10,8},{8,1... | collective-permute-start | bytes 1327112 | tf_op jit(solution)/shard_map/ppermute | solution.py:475
  49.5 49.4 %collective-permute-start.4 = (bf16[864,256]{1,0:T(8,128)(2,1)}, bf16[864,256]{1,0:T(8,128)(2,1)S(1)}, u32[]{:S(2)}, u32[]{:S(2)}) collective-permute-start(bf16[864,256]{1,0:T(8,128)(2,1)} %get-tuple-element.31), channel_id=1, source_target_pairs={{0,1},{1,0},{2,3},{3,2},{4,5},{5,4},{6,7},{7,6},{8,9},{9,8},{10,11... | collective-permute-start | bytes 1327112 | tf_op jit(solution)/shard_map/ppermute | solution.py:475
  52.5 47.9 %collective-permute-start.5 = (bf16[864,256]{1,0:T(8,128)(2,1)}, bf16[864,256]{1,0:T(8,128)(2,1)S(1)}, u32[]{:S(2)}, u32[]{:S(2)}) collective-permute-start(bf16[864,256]{1,0:T(8,128)(2,1)} %get-tuple-element.32), channel_id=1, source_target_pairs={{0,3},{3,0},{4,7},{7,4},{8,11},{11,8},{12,15},{15,12},{16,19},{19,... | collective-permute-start | bytes 1327112 | tf_op jit(solution)/shard_map/ppermute | solution.py:475
  72.1 43.7 %collective-permute-start.6 = (bf16[864,256]{1,0:T(8,128)(2,1)}, bf16[864,256]{1,0:T(8,128)(2,1)S(1)}, u32[]{:S(2)}, u32[]{:S(2)}) collective-permute-start(bf16[864,256]{1,0:T(8,128)(2,1)} %get-tuple-element.33), channel_id=1, source_target_pairs={{1,3},{2,0},{0,2},{3,1},{5,7},{6,4},{4,6},{7,5},{9,11},{10,8},{8,1... | collective-permute-start | bytes 1327112 | tf_op jit(solution)/shard_map/ppermute | solution.py:475
  72.1 1.5 %copy-start.1 = (bf16[256,3456]{1,0:T(8,128)(2,1)S(1)}, bf16[256,3456]{1,0:T(8,128)(2,1)}, u32[]{:S(2)}) copy-start(bf16[256,3456]{1,0:T(8,128)(2,1)} %get-tuple-element.21.refs_1_.refs_7_.refs_9_) | copy-start | bytes 5308420
  73.6 1.3 %copy-start.4 = (bf16[256,2560]{1,0:T(8,128)(2,1)S(1)}, bf16[256,2560]{1,0:T(8,128)(2,1)}, u32[]{:S(2)}) copy-start(bf16[256,2560]{1,0:T(8,128)(2,1)} %get-tuple-element.20.refs_0_) | copy-start | bytes 3932164
  74.9 0.7 copy-start.7
  76.6 42.3 %collective-permute-start.1 = (bf16[864,128]{1,0:T(8,128)(2,1)}, bf16[864,128]{1,0:T(8,128)(2,1)S(1)}, u32[]{:S(2)}, u32[]{:S(2)}) collective-permute-start(bf16[864,128]{1,0:T(8,128)(2,1)} %get-tuple-element.26), channel_id=1, source_target_pairs={{0,3},{3,0},{4,7},{7,4},{8,11},{11,8},{12,15},{15,12},{16,19},{19,... | collective-permute-start | bytes 663560 | tf_op jit(solution)/shard_map/ppermute | solution.py:475
  82.7 36.2 %collective-permute-start.3 = (bf16[864,128]{1,0:T(8,128)(2,1)}, bf16[864,128]{1,0:T(8,128)(2,1)S(1)}, u32[]{:S(2)}, u32[]{:S(2)}) collective-permute-start(bf16[864,128]{1,0:T(8,128)(2,1)} %get-tuple-element.26), channel_id=1, source_target_pairs={{1,2},{2,1},{5,6},{6,5},{9,10},{10,9},{13,14},{14,13},{17,18},{18,... | collective-permute-start | bytes 663560 | tf_op jit(solution)/shard_map/ppermute | solution.py:475
  98.9 20.0 %collective-permute-start = (bf16[864,128]{1,0:T(8,128)(2,1)}, bf16[864,128]{1,0:T(8,128)(2,1)S(1)}, u32[]{:S(2)}, u32[]{:S(2)}) collective-permute-start(bf16[864,128]{1,0:T(8,128)(2,1)} %get-tuple-element.25), channel_id=1, source_target_pairs={{0,1},{3,2},{4,5},{7,6},{8,9},{11,10},{12,13},{15,14},{16,17},{19,... | collective-permute-start | bytes 663560 | tf_op jit(solution)/shard_map/ppermute | solution.py:475
  100.5 22.5 %collective-permute-start.2 = (bf16[864,128]{1,0:T(8,128)(2,1)}, bf16[864,128]{1,0:T(8,128)(2,1)S(1)}, u32[]{:S(2)}, u32[]{:S(2)}) collective-permute-start(bf16[864,128]{1,0:T(8,128)(2,1)} %get-tuple-element.29), channel_id=1, source_target_pairs={{1,3},{2,0},{5,7},{6,4},{9,11},{10,8},{13,15},{14,12},{17,19},{18,... | collective-permute-start | bytes 663560 | tf_op jit(solution)/shard_map/ppermute | solution.py:475
  101.8 3.5 %copy-start = (f32[2560,864]{0,1:T(8,128)S(1)}, f32[2560,864]{0,1:T(8,128)}, u32[]{:S(2)}) copy-start(f32[2560,864]{0,1:T(8,128)} %param.4) | copy-start | bytes 26542084
  105.3 4.9 %copy-start.2 = (bf16[256,3456]{1,0:T(8,128)(2,1)S(1)}, bf16[256,3456]{1,0:T(8,128)(2,1)}, u32[]{:S(2)}) copy-start(bf16[256,3456]{1,0:T(8,128)(2,1)} %get-tuple-element.21.refs_1_.refs_7_.refs_9_) | copy-start | bytes 5308420
  105.3 4.9 %copy-start.3 = (bf16[864,512]{1,0:T(8,128)(2,1)S(1)}, bf16[864,512]{1,0:T(8,128)(2,1)}, u32[]{:S(2)}) copy-start(bf16[864,512]{1,0:T(8,128)(2,1)} %get-tuple-element.34.refs_5_) | copy-start | bytes 2654212
  113.3 9.7 %copy-start.5 = (bf16[864,128]{1,0:T(8,128)(2,1)S(1)}, bf16[864,128]{1,0:T(8,128)(2,1)}, u32[]{:S(2)}) copy-start(bf16[864,128]{1,0:T(8,128)(2,1)} %get-tuple-element.28.refs_5_) | copy-start | bytes 663556
  113.3 9.7 %copy-start.6 = (bf16[864,128]{1,0:T(8,128)(2,1)S(1)}, bf16[864,128]{1,0:T(8,128)(2,1)}, u32[]{:S(2)}) copy-start(bf16[864,128]{1,0:T(8,128)(2,1)} %get-tuple-element.27.refs_4_) | copy-start | bytes 663556

commit v3 on v2

--- a/solution.py
+++ b/solution.py
@@ -56,11 +56,11 @@
     return (new_master, rollout)
 
 
-def exchange_kernel(members, chunks, left_ref, right_ref, returns_ref, master_ref, *refs):
+def exchange_kernel(members, chunks, left_hbm, right_hbm, returns_hbm, master_ref, *refs):
     sides = 3
     l_ref, r_ref, s_ref, p_ref, e_ref, n_ref, b_ref, *refs = refs
     blocks, refs = refs[:sides * len(chunks)], refs[sides * len(chunks):]
-    (wide, narrow, part, own_sem, pull_sem, push_sem, s_send, s_recv, t_send, t_recv, x_send, x_recv, f_send, f_recv,
+    (left_ref, right_ref, returns_ref, load_sem, wide, narrow, part, own_sem, pull_sem, push_sem, s_send, s_recv, t_send, t_recv, x_send, x_recv, f_send, f_recv,
      z_send, z_recv, q_send, q_recv, y_send, y_recv, e_send, e_recv, n_send, n_recv, b_send, b_recv) = refs
     me, te, an = lax.axis_index("member"), lax.axis_index("tensor"), lax.axis_index("answer")
     answers = 4
@@ -125,58 +125,63 @@
         greet({"answer": beyond})
         greet({"answer": beyond + 1})
 
+    loads = [pltpu.make_async_copy(src, dst, load_sem.at[i]) for i, (src, dst) in enumerate(
+        ((right_hbm, right_ref), (left_hbm, left_ref), (returns_hbm, returns_ref)))]
+    for load in loads:
+        load.start()
     pull(1).start()
     pull(2).start()
+    loads[0].wait()
+    own_r = pltpu.make_async_copy(right_ref, r_at(an, me), own_sem.at[1])
+    own_r.start()
+    pl.semaphore_wait(barrier, 5)
+
+    mine = lax.rem(an, 2)
+    halves = 2
+    count = local // halves
+    sources = (an, near, beyond, beyond + 1)
+    started = []
+
+    def start(copy):
+        copy.start()
+        started.append(copy)
+        return copy
+
+    def landed(block, sem):
+        remote(block, block, x_send.at[0], sem, {"member": other}).wait_recv()
+
+    def r_half(a, m, h):
+        return r_ref.at[pl.ds(pl.multiple_of((a * members + m) * local + h * count, count), count), :]
+
+    def forward(k, h):
+        block = r_half(sources[k], me, h)
+        src = right_ref.at[h * count:(h + 1) * count, :] if k == 0 else block
+        start(remote(src, block, f_send.at[k, h], f_recv.at[k, h], {"member": other}))
+
+    def spread(k):
+        block = l_slab(sources[k], te)
+        start(remote(block, block, y_send.at[k, 0], y_recv.at[k, 0], {"tensor": across}))
+        start(remote(block, block, y_send.at[k, 1], y_recv.at[k, 1], {"tensor": core}))
+
+    def part_of(h):
+        src = right_ref.at[h * count:(h + 1) * count, :]
+        start(remote(src, r_half(an, me, h), z_send.at[0, h], z_recv.at[1 + mine, h], {"answer": far}))
+        start(remote(src, r_half(an, me, h), z_send.at[1, h], z_recv.at[0, h], {"answer": near}))
+
+    part_of(0)
+    loads[1].wait()
+    start(remote(left_ref.at[:, pl.ds(pl.multiple_of(other * tile + te * piece, piece), piece)],
+                 l_at((an * members + me) * local, local, te), x_send.at[0], x_recv.at[0], {"member": other}))
     own_l = pltpu.make_async_copy(
         left_ref.at[:, pl.ds(pl.multiple_of(me * tile + te * piece, piece), piece)],
         l_at((an * members + me) * local, local, te), own_sem.at[0])
-    own_r = pltpu.make_async_copy(right_ref, r_at(an, me), own_sem.at[1])
     own_l.start()
-    own_r.start()
+    loads[2].wait()
     part[...] = jnp.sum(returns_ref[...].T, axis=0, keepdims=True)
     own_p = pltpu.make_async_copy(part, p_ref, own_sem.at[2])
     own_s = pltpu.make_async_copy(part, s_ref.at[an * members + me], own_sem.at[3])
     own_p.start()
     own_s.start()
-
-    pl.semaphore_wait(barrier, 5)
-
-    mine = lax.rem(an, 2)
-    halves = 2
-    count = local // halves
-    sources = (an, near, beyond, beyond + 1)
-    started = []
-
-    def start(copy):
-        copy.start()
-        started.append(copy)
-        return copy
-
-    def landed(block, sem):
-        remote(block, block, x_send.at[0], sem, {"member": other}).wait_recv()
-
-    def r_half(a, m, h):
-        return r_ref.at[pl.ds(pl.multiple_of((a * members + m) * local + h * count, count), count), :]
-
-    def forward(k, h):
-        block = r_half(sources[k], me, h)
-        src = right_ref.at[h * count:(h + 1) * count, :] if k == 0 else block
-        start(remote(src, block, f_send.at[k, h], f_recv.at[k, h], {"member": other}))
-
-    def spread(k):
-        block = l_slab(sources[k], te)
-        start(remote(block, block, y_send.at[k, 0], y_recv.at[k, 0], {"tensor": across}))
-        start(remote(block, block, y_send.at[k, 1], y_recv.at[k, 1], {"tensor": core}))
-
-    start(remote(left_ref.at[:, pl.ds(pl.multiple_of(other * tile + te * piece, piece), piece)],
-                 l_at((an * members + me) * local, local, te), x_send.at[0], x_recv.at[0], {"member": other}))
-
-    def part_of(h):
-        src = right_ref.at[h * count:(h + 1) * count, :]
-        start(remote(src, r_half(an, me, h), z_send.at[0, h], z_recv.at[1 + mine, h], {"answer": far}))
-        start(remote(src, r_half(an, me, h), z_send.at[1, h], z_recv.at[0, h], {"answer": near}))
-
-    part_of(0)
     own_p.wait()
     score = lambda a, m: s_ref.at[a * members + m]
     start(remote(p_ref, score(an, me), s_send.at[0], s_recv.at[mine + 1], {"answer": far}))
@@ -281,7 +286,7 @@
     block = returns.shape[0]
     half = left_noise.dtype
     dma = pltpu.SemaphoreType.DMA
-    vmem, anywhere = pl.BlockSpec(memory_space=pltpu.VMEM), pl.BlockSpec(memory_space=pl.ANY)
+    anywhere = pl.BlockSpec(memory_space=pl.ANY)
     shape = jax.ShapeDtypeStruct
     return pl.pallas_call(
         lambda *refs: exchange_kernel(members, chunks, *refs),
@@ -294,9 +299,11 @@
             shape((cols, chunks[-1]), half),
             shape((cols, chunks[-1]), half),
         ) + tuple(shape((cols, size), half) for _ in range(sides) for size in chunks),
-        in_specs=[vmem] * 3 + [anywhere],
+        in_specs=[anywhere] * 4,
         out_specs=(anywhere,) * (7 + sides * len(chunks)),
         scratch_shapes=[
+            pltpu.VMEM(left_noise.shape, half), pltpu.VMEM(right_noise.shape, half),
+            pltpu.VMEM(returns.shape, returns.dtype), dma((3,)),
             pltpu.VMEM((2, cols, tile // answers), jnp.float32), pltpu.VMEM((2, cols, tile // answers), half),
             pltpu.VMEM((1, block), jnp.float32),
             dma((4,)), dma((sides,)), dma((sides, len(chunks))), dma((4,)), dma((3,)), dma((4,)), dma((4,)),
@@ -375,6 +382,60 @@
     )(where, transposed, *[block for _, block, _ in sides], left, right, *more)
 
 
+def last_kernel(picks, first, master_ref, *refs):
+    sides, refs = refs[:len(picks)], refs[len(picks):]
+    base_ref, _, out_ref, stack, block, sem = refs
+    an = lax.axis_index("answer")
+    width, tile = master_ref.shape
+    rows = block.shape[0]
+    places = {0: an, 1: an + 1 - 2 * lax.rem(an, 2), 2: lax.rem(an + 2, 4), 3: 3 - an}
+    inner = lax.div(an + 1, 2) == 1
+    within = {True: inner, False: jnp.logical_not(inner)}
+
+    def place(x, value):
+        stack[pl.ds(pl.multiple_of(places[x] * width, 16), width), :] = value.astype(stack.dtype)
+
+    place(0, master_ref[:, pl.ds(pl.multiple_of(an * (tile // 4) + first, 128), rows)])
+    for (x, which), ref in zip(picks, sides):
+        pl.when(within[which])(lambda x=x, ref=ref: place(x, ref[...]))
+    row = lax.broadcasted_iota(jnp.int32, (rows, rows), 0)
+    col = lax.broadcasted_iota(jnp.int32, (rows, rows), 1)
+    unit = jnp.where(row == col, 1.0, 0.0).astype(stack.dtype)
+    total = out_ref.shape[1]
+    step = divisor(total, 128, 512)
+    copies = []
+    for i, at in enumerate(range(0, total, step)):
+        cols = slice(at, at + step)
+        old = lax.dot_general(unit, stack[cols, :], (((1,), (1,)), ((), ())), preferred_element_type=jnp.float32)
+        block[:, cols] = (base_ref[:, cols] + old).astype(block.dtype)
+        copy = pltpu.make_async_copy(block.at[:, cols], out_ref.at[first:first + rows, cols], sem.at[i])
+        copy.start()
+        copies.append(copy)
+    for copy in copies:
+        copy.wait()
+
+
+def finish(transposed, sides, base, first, so_far):
+    size, total = base.shape
+    vmem, anywhere = pl.BlockSpec(memory_space=pltpu.VMEM), pl.BlockSpec(memory_space=pl.ANY)
+    picks = tuple(key for key, _, _ in sides)
+    return pl.pallas_call(
+        lambda *refs: last_kernel(picks, first, *refs),
+        in_specs=[vmem] * (2 + len(sides)) + [anywhere],
+        out_specs=anywhere,
+        scratch_shapes=[
+            pltpu.VMEM((total, size), so_far.dtype), pltpu.VMEM((size, total), so_far.dtype),
+            pltpu.SemaphoreType.DMA((total // divisor(total, 128, 512),)),
+        ],
+        out_shape=jax.ShapeDtypeStruct(so_far.shape, so_far.dtype),
+        input_output_aliases={2 + len(sides): 0},
+        cost_estimate=pl.CostEstimate(
+            flops=2 * size * total * size, bytes_accessed=6 * size * total, transcendentals=0),
+        compiler_params=pltpu.CompilerParams(vmem_limit_bytes=24 << 20),
+        name="last",
+    )(transposed, *[block for _, block, _ in sides], base, so_far)
+
+
 def update_kernel(master_ref, right_ref, left_ref, new_ref):
     new_ref[...] = master_ref[...] + jnp.dot(right_ref[...], left_ref[...], preferred_element_type=jnp.float32)
 
@@ -400,7 +461,7 @@
     )(transposed, right, left)
 
 
-def weigh_kernel(members, l_ref, r_ref, s_ref, w_ref, o_ref, t_ref, turned):
+def weigh_kernel(members, l_ref, r_ref, s_ref, w_ref, o_ref, t_ref, b_ref, turned):
     answers, block = s_ref.shape[0] // members, s_ref.shape[2]
     population = members * block
     local = block // answers
@@ -425,9 +486,13 @@
     turned[...] = r_ref[...].T
     width = t_ref.shape[0]
     t_ref[...] = turned[pl.ds(pl.multiple_of(an * width, 16), width), :]
-
-
-def weigh(left_tile, right, parts, members, rows, width):
+    step = divisor(b_ref.shape[1], 128, 512)
+    for at in range(0, b_ref.shape[1], step):
+        b_ref[:, at:at + step] = jnp.dot(
+            o_ref[rows - b_ref.shape[0]:, :], r_ref[:, at:at + step], preferred_element_type=jnp.float32)
+
+
+def weigh(left_tile, right, parts, members, rows, width, size):
     vmem = pl.BlockSpec(memory_space=pltpu.VMEM)
     total = left_tile.shape[0]
     half = left_tile.dtype
@@ -437,9 +502,10 @@
             jax.ShapeDtypeStruct(left_tile.shape, half),
             jax.ShapeDtypeStruct((rows, total), half),
             jax.ShapeDtypeStruct((width, total), half),
+            jax.ShapeDtypeStruct((size, right.shape[1]), jnp.float32),
         ),
         in_specs=[vmem] * 3,
-        out_specs=(vmem,) * 3,
+        out_specs=(vmem,) * 4,
         scratch_shapes=[pltpu.VMEM(right.shape[::-1], half)],
         cost_estimate=pl.CostEstimate(flops=total * right.shape[1] * 256, bytes_accessed=1 << 23, transcendentals=0),
         compiler_params=pltpu.CompilerParams(vmem_limit_bytes=24 << 20),
@@ -473,7 +539,7 @@
     for c, x in order_of(len(chunks)):
         some = {(last, 2): pairs[2][:2], (last, 1): pairs[1][::3]}.get((c, x), pairs[x])
         got[c, x] = lax.ppermute(blocks[min(x, 3) - 1][c], "answer", some)
-    weighted, own, turned = weigh(left_tile, right, parts, members, rows, width)
+    weighted, own, turned, base = weigh(left_tile, right, parts, members, rows, width, chunks[-1])
     new_master = update(transposed, turned, weighted)
     rollout, at = None, 0
     for c, size in enumerate(chunks):
@@ -482,7 +548,10 @@
             sides += [((1, False), aside, 0), ((2, True), cross, 0), ((2, False), got[c, 2], 0), ((3, True), got[c, 4], 0)]
         else:
             sides += [((2, None), got[c, 2], 0), ((3, True), early, at // 128)]
-        rollout = finalize(where, transposed, sides, own, right, at, size, rollout)
+        if c == last:
+            rollout = finish(transposed, sides, base, at, rollout)
+        else:
+            rollout = finalize(where, transposed, sides, own, right, at, size, rollout)
         at += size
     return (new_master.T, rollout)
 

time: 125 us -> 124 us (level)
  Pallas kernels: 54.1 us -> 52.8 us
    pallas_call x3 -> x2, Pallas kernels: 7.93 us -> 6.15 us  [finalize(): pl.pallas_call(lambda *refs: final_kernel(picks, *refs), grid_spec=pltpu....]
    pallas_call x0 -> x1, Pallas kernels: none -> 1.35 us  [finish(): pl.pallas_call(lambda *refs: last_kernel(picks, first, *refs), in_specs=[...]
where the time goes in v3:
time: 124 us; the launch traced here: 123 us
  Pallas kernels  52.8 us (43%)
  waiting for transfers between devices  40.5 us (33%)
  starting transfers between devices  22.3 us (18%)
  local copies, waits for them, and re-layouts  7 us (6%)
    ppermute x10, waiting for transfers between devices, fast_body(): got[c, x] = lax.ppermute(blocks[min(x, 3) - 1][c], 'answer', some)  40.5 us
    pallas_call x1, Pallas kernels, exchange(): pl.pallas_call(lambda *refs: exchange_kernel(members, chunks, *refs), out...  39.3 us
    ppermute x10, starting transfers between devices, fast_body(): got[c, x] = lax.ppermute(blocks[min(x, 3) - 1][c], 'answer', some)  22.3 us
    unnamed x16, local copies, waits for them, and re-layouts  7 us
    pallas_call x2, Pallas kernels, finalize(): pl.pallas_call(lambda *refs: final_kernel(picks, *refs), grid_spec=pltpu....  6.15 us
    pallas_call x1, Pallas kernels, update(): pl.pallas_call(update_kernel, grid=(width // chunk,), in_specs=[pl.BlockS...  4.91 us
  transfers between devices with their start and end apart: 10, of which 5 were waited for; matrix products, arithmetic and copies ran while one was open for 0% of the time, Pallas kernels for 10%

profile of v3, /device:TPU:0, one launch (start us, length us, event | category | flops | bytes accessed | tf_op | source)
XLA Modules:
  0.0 123.3 jit_solution(3459476321001912016)
XLA Ops:
  0.6 39.3 %exchange.1 = (bf16[256,2560]{1,0:T(8,128)(2,1)}, bf16[256,3456]{1,0:T(8,128)(2,1)}, f32[8,1,128]{2,1,0:T(1,128)}, f32[1,128]{1,0:T(1,128)}, bf16[864,512]{1,0:T...) custom-call(bf16[32,5120]{1,0:T(8,128)(2,1)} %refs_0_.1, ...), custom_call_target="tpu_custom_call" | custom-call | tf_op jit(solution)/shard_map/exchange/pallas_call | solution.py:291
  39.9 5.2 %collective-permute-start.7 = (bf16[864,256]{1,0:T(8,128)(2,1)}, bf16[864,256]{1,0:T(8,128)(2,1)S(1)}, u32[]{:S(2)}, u32[]{:S(2)}) collective-permute-start(bf16[864,256]{1,0:T(8,128)(2,1)} %get-tuple-element.37), channel_id=1, source_target_pairs={{0,1},{1,0},{2,3},{3,2},{4,5},{5,4},{6,7},{7,6},{8,9},{9,8},{10,11... | collective-permute-start | bytes 1327112 | tf_op jit(solution)/shard_map/ppermute | solution.py:541
  45.1 3.3 %collective-permute-start.8 = (bf16[864,256]{1,0:T(8,128)(2,1)}, bf16[864,256]{1,0:T(8,128)(2,1)S(1)}, u32[]{:S(2)}, u32[]{:S(2)}) collective-permute-start(bf16[864,256]{1,0:T(8,128)(2,1)} %get-tuple-element.38), channel_id=1, source_target_pairs={{0,3},{3,0},{4,7},{7,4},{8,11},{11,8},{12,15},{15,12},{16,19},{19,... | collective-permute-start | bytes 1327112 | tf_op jit(solution)/shard_map/ppermute | solution.py:541
  48.4 0.1 collective-permute-start.9
  48.5 3.0 %collective-permute-start.4 = (bf16[864,256]{1,0:T(8,128)(2,1)}, bf16[864,256]{1,0:T(8,128)(2,1)S(1)}, u32[]{:S(2)}, u32[]{:S(2)}) collective-permute-start(bf16[864,256]{1,0:T(8,128)(2,1)} %get-tuple-element.32), channel_id=1, source_target_pairs={{0,1},{1,0},{2,3},{3,2},{4,5},{5,4},{6,7},{7,6},{8,9},{9,8},{10,11... | collective-permute-start | bytes 1327112 | tf_op jit(solution)/shard_map/ppermute | solution.py:541
  51.5 3.3 %collective-permute-start.5 = (bf16[864,256]{1,0:T(8,128)(2,1)}, bf16[864,256]{1,0:T(8,128)(2,1)S(1)}, u32[]{:S(2)}, u32[]{:S(2)}) collective-permute-start(bf16[864,256]{1,0:T(8,128)(2,1)} %get-tuple-element.33), channel_id=1, source_target_pairs={{0,3},{3,0},{4,7},{7,4},{8,11},{11,8},{12,15},{15,12},{16,19},{19,... | collective-permute-start | bytes 1327112 | tf_op jit(solution)/shard_map/ppermute | solution.py:541
  54.8 16.3 %collective-permute-done.7.refs_2_ = bf16[864,256]{1,0:T(8,128)(2,1)S(1)} collective-permute-done((bf16[864,256]{1,0:T(8,128)(2,1)}, bf16[864,256]{1,0:T(8,128)(2,1)S(1)}, u32[]{:S(2)}, u32[]{:S(2)}) %collective-permute-start.7) | collective-permute-done | bytes 442400 | tf_op jit(solution)/shard_map/ppermute | solution.py:541
  71.0 0.0 collective-permute-start.6
  71.0 0.0 copy-start.1
  71.0 1.5 %copy-done.1 = bf16[256,3456]{1,0:T(8,128)(2,1)S(1)} copy-done((bf16[256,3456]{1,0:T(8,128)(2,1)S(1)}, bf16[256,3456]{1,0:T(8,128)(2,1)}, u32[]{:S(2)}) %copy-start.1) | copy-done | bytes 1769496
  72.5 0.0 copy-start.4
  72.5 1.3 %copy-done.4 = bf16[256,2560]{1,0:T(8,128)(2,1)S(1)} copy-done((bf16[256,2560]{1,0:T(8,128)(2,1)S(1)}, bf16[256,2560]{1,0:T(8,128)(2,1)}, u32[]{:S(2)}) %copy-start.4) | copy-done | bytes 1310744
  73.8 0.0 copy-start.7
  73.8 0.7 copy-done.7
  74.5 1.1 weigh.1
  75.6 0.0 collective-permute-done.8.refs_3_
  75.6 3.9 %collective-permute-start.1 = (bf16[864,128]{1,0:T(8,128)(2,1)}, bf16[864,128]{1,0:T(8,128)(2,1)S(1)}, u32[]{:S(2)}, u32[]{:S(2)}) collective-permute-start(bf16[864,128]{1,0:T(8,128)(2,1)} %get-tuple-element.27), channel_id=1, source_target_pairs={{0,3},{3,0},{4,7},{7,4},{8,11},{11,8},{12,15},{15,12},{16,19},{19,... | collective-permute-start | bytes 663560 | tf_op jit(solution)/shard_map/ppermute | solution.py:541
  79.6 2.1 %collective-permute-done.9.refs_4_ = bf16[864,256]{1,0:T(8,128)(2,1)S(1)} collective-permute-done((bf16[864,256]{1,0:T(8,128)(2,1)}, bf16[864,256]{1,0:T(8,128)(2,1)S(1)}, u32[]{:S(2)}, u32[]{:S(2)}) %collective-permute-start.9) | collective-permute-done | bytes 442400 | tf_op jit(solution)/shard_map/ppermute | solution.py:541
  81.7 0.7 collective-permute-start.3
  82.4 15.5 %collective-permute-done.4.refs_2_ = bf16[864,256]{1,0:T(8,128)(2,1)S(1)} collective-permute-done((bf16[864,256]{1,0:T(8,128)(2,1)}, bf16[864,256]{1,0:T(8,128)(2,1)S(1)}, u32[]{:S(2)}, u32[]{:S(2)}) %collective-permute-start.4) | collective-permute-done | bytes 442400 | tf_op jit(solution)/shard_map/ppermute | solution.py:541
  97.9 1.6 %collective-permute-start = (bf16[864,128]{1,0:T(8,128)(2,1)}, bf16[864,128]{1,0:T(8,128)(2,1)S(1)}, u32[]{:S(2)}, u32[]{:S(2)}) collective-permute-start(bf16[864,128]{1,0:T(8,128)(2,1)} %get-tuple-element.26), channel_id=1, source_target_pairs={{0,1},{3,2},{4,5},{7,6},{8,9},{11,10},{12,13},{15,14},{16,17},{19,... | collective-permute-start | bytes 663560 | tf_op jit(solution)/shard_map/ppermute | solution.py:541
  99.4 0.0 collective-permute-done.5.refs_3_
  99.4 1.3 %collective-permute-start.2 = (bf16[864,128]{1,0:T(8,128)(2,1)}, bf16[864,128]{1,0:T(8,128)(2,1)S(1)}, u32[]{:S(2)}, u32[]{:S(2)}) collective-permute-start(bf16[864,128]{1,0:T(8,128)(2,1)} %get-tuple-element.30), channel_id=1, source_target_pairs={{1,3},{2,0},{5,7},{6,4},{9,11},{10,8},{13,15},{14,12},{17,19},{18,... | collective-permute-start | bytes 663560 | tf_op jit(solution)/shard_map/ppermute | solution.py:541
  100.7 0.0 copy-start
  100.7 3.5 %copy-done = f32[2560,864]{0,1:T(8,128)S(1)} copy-done((f32[2560,864]{0,1:T(8,128)S(1)}, f32[2560,864]{0,1:T(8,128)}, u32[]{:S(2)}) %copy-start) | copy-done | bytes 8847384
  104.2 0.0 copy-start.2
  104.3 0.0 copy-start.3
  104.3 4.9 %update.1 = f32[864,2560]{1,0:T(8,128)} custom-call(f32[864,2560]{1,0:T(8,128)S(1)} %bitcast.4, bf16[864,256]{1,0:T(8,128)(2,1)S(1)} %get-tuple-element.24.right_ref, bf16[256,2560]{1,0:T(8,128)(2,1)S(1)} %get-tuple-element.25.left_ref), custom_call_target="tpu_custom_call" | custom-call | flops 1132462080 | bytes 17694720 | tf_op jit(solution)/shard_map/update/pallas_call | solution.py:447
  109.2 0.0 copy-done.2
  109.2 0.0 copy-done.3
  109.2 3.1 %final.2.refs_8_ = bf16[640,3456]{1,0:T(8,128)(2,1)} custom-call(s32[1]{0:T(128)} %bitcast.2.refs_0_, f32[864,2560]{1,0:T(8,128)S(1)} %bitcast.5, bf16[864,256]{1,0:T(8,128)(2,1)S(1)} %collective-permute-done.7.refs_2_, bf16[864,256]{1,0:T(8,128)(2,1)S(1)} %collective-permute-done.8.refs_3_, bf16[864,256]{1,0:T(8,128)(2,1)S(1)} %collective-permute-done.9.refs_4_, ...), custom_call_target="tpu_custom_call" | custom-call | flops 679477248 | bytes 5308416 | tf_op jit(solution)/shard_map/final/pallas_call | solution.py:364
  112.2 0.0 copy-start.5
  112.2 0.0 copy-start.6
  112.2 2.6 %collective-permute-done.6.refs_4_ = bf16[864,256]{1,0:T(8,128)(2,1)S(1)} collective-permute-done((bf16[864,256]{1,0:T(8,128)(2,1)}, bf16[864,256]{1,0:T(8,128)(2,1)S(1)}, u32[]{:S(2)}, u32[]{:S(2)}) %collective-permute-start.6) | collective-permute-done | bytes 442400 | tf_op jit(solution)/shard_map/ppermute | solution.py:541
  114.8 3.1 %final.3.refs_8_ = bf16[640,3456]{1,0:T(8,128)(2,1)} custom-call(s32[1]{0:T(128)} %bitcast.2.refs_0_, f32[864,2560]{1,0:T(8,128)S(1)} %bitcast.6, bf16[864,256]{1,0:T(8,128)(2,1)S(1)} %collective-permute-done.4.refs_2_, bf16[864,256]{1,0:T(8,128)(2,1)S(1)} %collective-permute-done.5.refs_3_, ...), custom_call_target="tpu_custom_call", output_to_operand_aliasing={{}: (8, {})} | custom-call | flops 679477248 | bytes 5308416 | tf_op jit(solution)/shard_map/final/pallas_call | solution.py:364
  117.9 0.0 collective-permute-done.1.refs_2_
  117.9 0.0 collective-permute-done.3.refs_6_
  117.9 0.0 collective-permute-done.refs_1_
  117.9 4.0 %collective-permute-done.2.refs_5_ = bf16[864,128]{1,0:T(8,128)(2,1)S(1)} collective-permute-done((bf16[864,128]{1,0:T(8,128)(2,1)}, bf16[864,128]{1,0:T(8,128)(2,1)S(1)}, u32[]{:S(2)}, u32[]{:S(2)}) %collective-permute-start.2) | collective-permute-done | bytes 221216 | tf_op jit(solution)/shard_map/ppermute | solution.py:541
  121.9 0.0 copy-done.5
  122.0 0.0 copy-done.6
  122.0 1.3 %last.1 = bf16[640,3456]{1,0:T(8,128)(2,1)} custom-call(f32[864,2560]{1,0:T(8,128)S(1)} %bitcast.7, bf16[864,128]{1,0:T(8,128)(2,1)S(1)} %collective-permute-done.refs_1_, bf16[864,128]{1,0:T(8,128)(2,1)S(1)} %collective-permute-done.1.refs_2_, bf16[864,128]{1,0:T(8,128)(2,1)S(1)} %copy-done.6, ...), custom_call_target="tpu_custom_call", output_to_operand_aliasing={{}: (8, {})} | custom-call | flops 113246208 | bytes 2654208 | tf_op jit(solution)/shard_map/last/pallas_call | solution.py:422
Async XLA Ops:
  39.9 31.1 %collective-permute-start.7 = (bf16[864,256]{1,0:T(8,128)(2,1)}, bf16[864,256]{1,0:T(8,128)(2,1)S(1)}, u32[]{:S(2)}, u32[]{:S(2)}) collective-permute-start(bf16[864,256]{1,0:T(8,128)(2,1)} %get-tuple-element.37), channel_id=1, source_target_pairs={{0,1},{1,0},{2,3},{3,2},{4,5},{5,4},{6,7},{7,6},{8,9},{9,8},{10,11... | collective-permute-start | bytes 1327112 | tf_op jit(solution)/shard_map/ppermute | solution.py:541
  45.1 30.5 %collective-permute-start.8 = (bf16[864,256]{1,0:T(8,128)(2,1)}, bf16[864,256]{1,0:T(8,128)(2,1)S(1)}, u32[]{:S(2)}, u32[]{:S(2)}) collective-permute-start(bf16[864,256]{1,0:T(8,128)(2,1)} %get-tuple-element.38), channel_id=1, source_target_pairs={{0,3},{3,0},{4,7},{7,4},{8,11},{11,8},{12,15},{15,12},{16,19},{19,... | collective-permute-start | bytes 1327112 | tf_op jit(solution)/shard_map/ppermute | solution.py:541
  48.4 33.3 %collective-permute-start.9 = (bf16[864,256]{1,0:T(8,128)(2,1)}, bf16[864,256]{1,0:T(8,128)(2,1)S(1)}, u32[]{:S(2)}, u32[]{:S(2)}) collective-permute-start(bf16[864,256]{1,0:T(8,128)(2,1)} %get-tuple-element.39), channel_id=1, source_target_pairs={{1,3},{2,0},{0,2},{3,1},{5,7},{6,4},{4,6},{7,5},{9,11},{10,8},{8,1... | collective-permute-start | bytes 1327112 | tf_op jit(solution)/shard_map/ppermute | solution.py:541
  48.5 49.4 %collective-permute-start.4 = (bf16[864,256]{1,0:T(8,128)(2,1)}, bf16[864,256]{1,0:T(8,128)(2,1)S(1)}, u32[]{:S(2)}, u32[]{:S(2)}) collective-permute-start(bf16[864,256]{1,0:T(8,128)(2,1)} %get-tuple-element.32), channel_id=1, source_target_pairs={{0,1},{1,0},{2,3},{3,2},{4,5},{5,4},{6,7},{7,6},{8,9},{9,8},{10,11... | collective-permute-start | bytes 1327112 | tf_op jit(solution)/shard_map/ppermute | solution.py:541
  51.5 47.9 %collective-permute-start.5 = (bf16[864,256]{1,0:T(8,128)(2,1)}, bf16[864,256]{1,0:T(8,128)(2,1)S(1)}, u32[]{:S(2)}, u32[]{:S(2)}) collective-permute-start(bf16[864,256]{1,0:T(8,128)(2,1)} %get-tuple-element.33), channel_id=1, source_target_pairs={{0,3},{3,0},{4,7},{7,4},{8,11},{11,8},{12,15},{15,12},{16,19},{19,... | collective-permute-start | bytes 1327112 | tf_op jit(solution)/shard_map/ppermute | solution.py:541
  71.0 43.8 %collective-permute-start.6 = (bf16[864,256]{1,0:T(8,128)(2,1)}, bf16[864,256]{1,0:T(8,128)(2,1)S(1)}, u32[]{:S(2)}, u32[]{:S(2)}) collective-permute-start(bf16[864,256]{1,0:T(8,128)(2,1)} %get-tuple-element.34), channel_id=1, source_target_pairs={{1,3},{2,0},{0,2},{3,1},{5,7},{6,4},{4,6},{7,5},{9,11},{10,8},{8,1... | collective-permute-start | bytes 1327112 | tf_op jit(solution)/shard_map/ppermute | solution.py:541
  71.0 1.5 %copy-start.1 = (bf16[256,3456]{1,0:T(8,128)(2,1)S(1)}, bf16[256,3456]{1,0:T(8,128)(2,1)}, u32[]{:S(2)}) copy-start(bf16[256,3456]{1,0:T(8,128)(2,1)} %get-tuple-element.22.refs_1_.refs_7_) | copy-start | bytes 5308420
  72.5 1.3 %copy-start.4 = (bf16[256,2560]{1,0:T(8,128)(2,1)S(1)}, bf16[256,2560]{1,0:T(8,128)(2,1)}, u32[]{:S(2)}) copy-start(bf16[256,2560]{1,0:T(8,128)(2,1)} %get-tuple-element.21.refs_0_) | copy-start | bytes 3932164
  73.8 0.7 copy-start.7
  75.6 42.3 %collective-permute-start.1 = (bf16[864,128]{1,0:T(8,128)(2,1)}, bf16[864,128]{1,0:T(8,128)(2,1)S(1)}, u32[]{:S(2)}, u32[]{:S(2)}) collective-permute-start(bf16[864,128]{1,0:T(8,128)(2,1)} %get-tuple-element.27), channel_id=1, source_target_pairs={{0,3},{3,0},{4,7},{7,4},{8,11},{11,8},{12,15},{15,12},{16,19},{19,... | collective-permute-start | bytes 663560 | tf_op jit(solution)/shard_map/ppermute | solution.py:541
  81.7 36.2 %collective-permute-start.3 = (bf16[864,128]{1,0:T(8,128)(2,1)}, bf16[864,128]{1,0:T(8,128)(2,1)S(1)}, u32[]{:S(2)}, u32[]{:S(2)}) collective-permute-start(bf16[864,128]{1,0:T(8,128)(2,1)} %get-tuple-element.27), channel_id=1, source_target_pairs={{1,2},{2,1},{5,6},{6,5},{9,10},{10,9},{13,14},{14,13},{17,18},{18,... | collective-permute-start | bytes 663560 | tf_op jit(solution)/shard_map/ppermute | solution.py:541
  97.9 20.1 %collective-permute-start = (bf16[864,128]{1,0:T(8,128)(2,1)}, bf16[864,128]{1,0:T(8,128)(2,1)S(1)}, u32[]{:S(2)}, u32[]{:S(2)}) collective-permute-start(bf16[864,128]{1,0:T(8,128)(2,1)} %get-tuple-element.26), channel_id=1, source_target_pairs={{0,1},{3,2},{4,5},{7,6},{8,9},{11,10},{12,13},{15,14},{16,17},{19,... | collective-permute-start | bytes 663560 | tf_op jit(solution)/shard_map/ppermute | solution.py:541
  99.4 22.5 %collective-permute-start.2 = (bf16[864,128]{1,0:T(8,128)(2,1)}, bf16[864,128]{1,0:T(8,128)(2,1)S(1)}, u32[]{:S(2)}, u32[]{:S(2)}) collective-permute-start(bf16[864,128]{1,0:T(8,128)(2,1)} %get-tuple-element.30), channel_id=1, source_target_pairs={{1,3},{2,0},{5,7},{6,4},{9,11},{10,8},{13,15},{14,12},{17,19},{18,... | collective-permute-start | bytes 663560 | tf_op jit(solution)/shard_map/ppermute | solution.py:541
  100.7 3.5 %copy-start = (f32[2560,864]{0,1:T(8,128)S(1)}, f32[2560,864]{0,1:T(8,128)}, u32[]{:S(2)}) copy-start(f32[2560,864]{0,1:T(8,128)} %param.4) | copy-start | bytes 26542084
  104.2 4.9 %copy-start.2 = (bf16[256,3456]{1,0:T(8,128)(2,1)S(1)}, bf16[256,3456]{1,0:T(8,128)(2,1)}, u32[]{:S(2)}) copy-start(bf16[256,3456]{1,0:T(8,128)(2,1)} %get-tuple-element.22.refs_1_.refs_7_) | copy-start | bytes 5308420
  104.3 4.9 %copy-start.3 = (bf16[864,512]{1,0:T(8,128)(2,1)S(1)}, bf16[864,512]{1,0:T(8,128)(2,1)}, u32[]{:S(2)}) copy-start(bf16[864,512]{1,0:T(8,128)(2,1)} %get-tuple-element.35.refs_5_) | copy-start | bytes 2654212
  112.2 9.7 %copy-start.5 = (bf16[864,128]{1,0:T(8,128)(2,1)S(1)}, bf16[864,128]{1,0:T(8,128)(2,1)}, u32[]{:S(2)}) copy-start(bf16[864,128]{1,0:T(8,128)(2,1)} %get-tuple-element.29.refs_4_) | copy-start | bytes 663556
  112.2 9.7 %copy-start.6 = (bf16[864,128]{1,0:T(8,128)(2,1)S(1)}, bf16[864,128]{1,0:T(8,128)(2,1)}, u32[]{:S(2)}) copy-start(bf16[864,128]{1,0:T(8,128)(2,1)} %get-tuple-element.28.refs_3_) | copy-start | bytes 663556

commit v4 on v3

--- a/solution.py
+++ b/solution.py
@@ -382,9 +382,19 @@
     )(where, transposed, *[block for _, block, _ in sides], left, right, *more)
 
 
-def last_kernel(picks, first, master_ref, *refs):
+def unit_of(rows, dtype):
+    row = lax.broadcasted_iota(jnp.int32, (rows, rows), 0)
+    col = lax.broadcasted_iota(jnp.int32, (rows, rows), 1)
+    return jnp.where(row == col, 1.0, 0.0).astype(dtype)
+
+
+def turn(unit, stack):
+    return lax.dot_general(unit, stack, (((1,), (1,)), ((), ())), preferred_element_type=jnp.float32)
+
+
+def lead_kernel(picks, first, master_ref, *refs):
     sides, refs = refs[:len(picks)], refs[len(picks):]
-    base_ref, _, out_ref, stack, block, sem = refs
+    base_ref, _, out_ref, mix_ref, stack, block, sem = refs
     an = lax.axis_index("answer")
     width, tile = master_ref.shape
     rows = block.shape[0]
@@ -395,19 +405,19 @@
     def place(x, value):
         stack[pl.ds(pl.multiple_of(places[x] * width, 16), width), :] = value.astype(stack.dtype)
 
+    stack[...] = jnp.zeros_like(stack)
     place(0, master_ref[:, pl.ds(pl.multiple_of(an * (tile // 4) + first, 128), rows)])
     for (x, which), ref in zip(picks, sides):
         pl.when(within[which])(lambda x=x, ref=ref: place(x, ref[...]))
-    row = lax.broadcasted_iota(jnp.int32, (rows, rows), 0)
-    col = lax.broadcasted_iota(jnp.int32, (rows, rows), 1)
-    unit = jnp.where(row == col, 1.0, 0.0).astype(stack.dtype)
+    unit = unit_of(rows, stack.dtype)
     total = out_ref.shape[1]
     step = divisor(total, 128, 512)
     copies = []
     for i, at in enumerate(range(0, total, step)):
         cols = slice(at, at + step)
-        old = lax.dot_general(unit, stack[cols, :], (((1,), (1,)), ((), ())), preferred_element_type=jnp.float32)
-        block[:, cols] = (base_ref[:, cols] + old).astype(block.dtype)
+        mixed = base_ref[:, cols] + turn(unit, stack[cols, :])
+        mix_ref[:, cols] = mixed
+        block[:, cols] = mixed.astype(block.dtype)
         copy = pltpu.make_async_copy(block.at[:, cols], out_ref.at[first:first + rows, cols], sem.at[i])
         copy.start()
         copies.append(copy)
@@ -415,25 +425,81 @@
         copy.wait()
 
 
-def finish(transposed, sides, base, first, so_far):
+def lead(transposed, sides, base, first, so_far):
     size, total = base.shape
     vmem, anywhere = pl.BlockSpec(memory_space=pltpu.VMEM), pl.BlockSpec(memory_space=pl.ANY)
-    picks = tuple(key for key, _, _ in sides)
+    picks = tuple(key for key, _ in sides)
     return pl.pallas_call(
-        lambda *refs: last_kernel(picks, first, *refs),
+        lambda *refs: lead_kernel(picks, first, *refs),
         in_specs=[vmem] * (2 + len(sides)) + [anywhere],
-        out_specs=anywhere,
+        out_specs=(anywhere, vmem),
         scratch_shapes=[
             pltpu.VMEM((total, size), so_far.dtype), pltpu.VMEM((size, total), so_far.dtype),
             pltpu.SemaphoreType.DMA((total // divisor(total, 128, 512),)),
         ],
-        out_shape=jax.ShapeDtypeStruct(so_far.shape, so_far.dtype),
+        out_shape=(
+            jax.ShapeDtypeStruct(so_far.shape, so_far.dtype),
+            jax.ShapeDtypeStruct(base.shape, base.dtype),
+        ),
         input_output_aliases={2 + len(sides): 0},
         cost_estimate=pl.CostEstimate(
             flops=2 * size * total * size, bytes_accessed=6 * size * total, transcendentals=0),
         compiler_params=pltpu.CompilerParams(vmem_limit_bytes=24 << 20),
+        name="lead",
+    )(transposed, *[block for _, block in sides], base, so_far)
+
+
+def last_kernel(first, mix_ref, inner_ref, outer_ref, _, out_ref, stack, block, sem):
+    an = lax.axis_index("answer")
+    width, rows = inner_ref.shape
+    inner = lax.div(an + 1, 2) == 1
+    begin = (2 - lax.div(an, 2)) * width
+    low = lax.div(begin, 128) * 128
+    at = pl.ds(pl.multiple_of(begin - low, 16), width)
+    stack[...] = jnp.zeros_like(stack)
+
+    @pl.when(inner)
+    def _():
+        stack[at, :] = inner_ref[...]
+
+    @pl.when(jnp.logical_not(inner))
+    def _():
+        stack[at, :] = outer_ref[...]
+
+    unit = unit_of(rows, stack.dtype)
+    step = block.shape[1] // 2
+    copies = []
+    for i in range(2):
+        cols = pl.ds(pl.multiple_of(low + i * step, 128), step)
+        mixed = mix_ref[:, cols] + turn(unit, stack[i * step:(i + 1) * step, :])
+        block[:, i * step:(i + 1) * step] = mixed.astype(block.dtype)
+        copy = pltpu.make_async_copy(
+            block.at[:, i * step:(i + 1) * step], out_ref.at[first:first + rows, cols], sem.at[i])
+        copy.start()
+        copies.append(copy)
+    for copy in copies:
+        copy.wait()
+
+
+def finish(mix, inner, outer, first, so_far):
+    width, size = inner.shape
+    window = -(-(width + 127) // 256) * 256
+    vmem, anywhere = pl.BlockSpec(memory_space=pltpu.VMEM), pl.BlockSpec(memory_space=pl.ANY)
+    return pl.pallas_call(
+        lambda *refs: last_kernel(first, *refs),
+        in_specs=[vmem] * 3 + [anywhere],
+        out_specs=anywhere,
+        scratch_shapes=[
+            pltpu.VMEM((window, size), so_far.dtype), pltpu.VMEM((size, window), so_far.dtype),
+            pltpu.SemaphoreType.DMA((2,)),
+        ],
+        out_shape=jax.ShapeDtypeStruct(so_far.shape, so_far.dtype),
+        input_output_aliases={3: 0},
+        cost_estimate=pl.CostEstimate(
+            flops=2 * size * window * size, bytes_accessed=6 * size * window, transcendentals=0),
+        compiler_params=pltpu.CompilerParams(vmem_limit_bytes=24 << 20),
         name="last",
-    )(transposed, *[block for _, block, _ in sides], base, so_far)
+    )(mix, inner, outer, so_far)
 
 
 def update_kernel(master_ref, right_ref, left_ref, new_ref):
@@ -543,26 +609,25 @@
     new_master = update(transposed, turned, weighted)
     rollout, at = None, 0
     for c, size in enumerate(chunks):
-        sides = [((1, True if c == last else None), got[c, 1], 0), ((3, False), got[c, 3], 0)]
         if c == last:
-            sides += [((1, False), aside, 0), ((2, True), cross, 0), ((2, False), got[c, 2], 0), ((3, True), got[c, 4], 0)]
+            sides = [((1, True), got[c, 1]), ((1, False), aside), ((2, True), cross), ((3, False), got[c, 3])]
+            rollout, mix = lead(transposed, sides, base, at, rollout)
+            rollout = finish(mix, got[c, 4], got[c, 2], at, rollout)
         else:
-            sides += [((2, None), got[c, 2], 0), ((3, True), early, at // 128)]
-        if c == last:
-            rollout = finish(transposed, sides, base, at, rollout)
-        else:
+            sides = [((1, None), got[c, 1], 0), ((2, None), got[c, 2], 0),
+                     ((3, False), got[c, 3], 0), ((3, True), early, at // 128)]
             rollout = finalize(where, transposed, sides, own, right, at, size, rollout)
         at += size
     return (new_master.T, rollout)
 
 
-def fits(members, tensors, answers, tile, local):
-    return (members, tensors, answers) == (2, 4, 4) and tile % 512 == 0 and tile >= 1024 and local % 32 == 0
+def fits(members, tensors, answers, tile, width, local):
+    return (members, tensors, answers) == (2, 4, 4) and tile % 512 == 0 and tile >= 1024 and width >= 512 and local % 32 == 0
 
 
 def body(master, left_noise, right_noise, returns):
     sizes = [lax.axis_size(n) for n in ("member", "tensor", "answer")]
-    fast = fits(*sizes, master.shape[0], left_noise.shape[0])
+    fast = fits(*sizes, *master.shape, left_noise.shape[0])
     return (fast_body if fast else plain_body)(master, left_noise, right_noise, returns)
 
 

time: 124 us -> 130 us (1.048)
  the two profiles are of different devices: /device:TPU:0 before, /device:TPU:8 now
where the time goes in v4:
time: 130 us; the launch traced here: 129 us
  Pallas kernels  56 us (43%)
  waiting for transfers between devices  47.6 us (37%)
  starting transfers between devices  18 us (14%)
  local copies, waits for them, and re-layouts  6.98 us (5%)
    ppermute x10, waiting for transfers between devices, fast_body(): got[c, x] = lax.ppermute(blocks[min(x, 3) - 1][c], 'answer', some)  47.6 us
    pallas_call x1, Pallas kernels, exchange(): pl.pallas_call(lambda *refs: exchange_kernel(members, chunks, *refs), out...  41.4 us
    ppermute x10, starting transfers between devices, fast_body(): got[c, x] = lax.ppermute(blocks[min(x, 3) - 1][c], 'answer', some)  18 us
    unnamed x16, local copies, waits for them, and re-layouts  6.98 us
    pallas_call x2, Pallas kernels, finalize(): pl.pallas_call(lambda *refs: final_kernel(picks, *refs), grid_spec=pltpu....  6.18 us
    pallas_call x1, Pallas kernels, update(): pl.pallas_call(update_kernel, grid=(width // chunk,), in_specs=[pl.BlockS...  4.9 us
  transfers between devices with their start and end apart: 10, of which 4 were waited for; matrix products, arithmetic and copies ran while one was open for 0% of the time, Pallas kernels for 11%

profile of v4, /device:TPU:8, one launch (start us, length us, event | category | flops | bytes accessed | tf_op | source)
XLA Modules:
  0.0 129.3 jit_solution(12545934892631208097)
XLA Ops:
  0.6 41.4 %exchange.1 = (bf16[256,2560]{1,0:T(8,128)(2,1)}, bf16[256,3456]{1,0:T(8,128)(2,1)}, f32[8,1,128]{2,1,0:T(1,128)}, f32[1,128]{1,0:T(1,128)}, bf16[864,512]{1,0:T...) custom-call(bf16[32,5120]{1,0:T(8,128)(2,1)} %refs_0_.1, ...), custom_call_target="tpu_custom_call" | custom-call | tf_op jit(solution)/shard_map/exchange/pallas_call | solution.py:291
  42.0 0.1 collective-permute-start.5
  42.1 1.9 %collective-permute-start.6 = (bf16[864,256]{1,0:T(8,128)(2,1)}, bf16[864,256]{1,0:T(8,128)(2,1)S(1)}, u32[]{:S(2)}, u32[]{:S(2)}) collective-permute-start(bf16[864,256]{1,0:T(8,128)(2,1)} %get-tuple-element.39), channel_id=1, source_target_pairs={{1,3},{2,0},{0,2},{3,1},{5,7},{6,4},{4,6},{7,5},{9,11},{10,8},{8,1... | collective-permute-start | bytes 1327112 | tf_op jit(solution)/shard_map/ppermute | solution.py:607
  44.0 0.7 collective-permute-start.7
  44.7 3.8 %collective-permute-start.2 = (bf16[864,256]{1,0:T(8,128)(2,1)}, bf16[864,256]{1,0:T(8,128)(2,1)S(1)}, u32[]{:S(2)}, u32[]{:S(2)}) collective-permute-start(bf16[864,256]{1,0:T(8,128)(2,1)} %get-tuple-element.33), channel_id=1, source_target_pairs={{0,1},{1,0},{2,3},{3,2},{4,5},{5,4},{6,7},{7,6},{8,9},{9,8},{10,11... | collective-permute-start | bytes 1327112 | tf_op jit(solution)/shard_map/ppermute | solution.py:607
  48.5 0.0 collective-permute-start.3
  48.5 13.3 %collective-permute-done.5.refs_2_ = bf16[864,256]{1,0:T(8,128)(2,1)S(1)} collective-permute-done((bf16[864,256]{1,0:T(8,128)(2,1)}, bf16[864,256]{1,0:T(8,128)(2,1)S(1)}, u32[]{:S(2)}, u32[]{:S(2)}) %collective-permute-start.5) | collective-permute-done | bytes 442400 | tf_op jit(solution)/shard_map/ppermute | solution.py:607
  61.9 0.7 collective-permute-start.4
  62.6 0.0 copy-start.1
  62.6 1.5 %copy-done.1 = bf16[256,3456]{1,0:T(8,128)(2,1)S(1)} copy-done((bf16[256,3456]{1,0:T(8,128)(2,1)S(1)}, bf16[256,3456]{1,0:T(8,128)(2,1)}, u32[]{:S(2)}) %copy-start.1) | copy-done | bytes 1769496
  64.0 0.0 copy-start.4
  64.0 1.3 %copy-done.4 = bf16[256,2560]{1,0:T(8,128)(2,1)S(1)} copy-done((bf16[256,2560]{1,0:T(8,128)(2,1)S(1)}, bf16[256,2560]{1,0:T(8,128)(2,1)}, u32[]{:S(2)}) %copy-start.4) | copy-done | bytes 1310744
  65.3 0.0 copy-start.7
  65.4 0.7 copy-done.7
  66.0 1.1 weigh.1
  67.1 6.6 %collective-permute-done.6.refs_3_ = bf16[864,256]{1,0:T(8,128)(2,1)S(1)} collective-permute-done((bf16[864,256]{1,0:T(8,128)(2,1)}, bf16[864,256]{1,0:T(8,128)(2,1)S(1)}, u32[]{:S(2)}, u32[]{:S(2)}) %collective-permute-start.6) | collective-permute-done | bytes 442400 | tf_op jit(solution)/shard_map/ppermute | solution.py:607
  73.8 0.7 collective-permute-start.1
  74.4 0.0 collective-permute-done.7.refs_4_
  74.5 3.6 %collective-permute-start.8 = (bf16[864,128]{1,0:T(8,128)(2,1)}, bf16[864,128]{1,0:T(8,128)(2,1)S(1)}, u32[]{:S(2)}, u32[]{:S(2)}) collective-permute-start(bf16[864,128]{1,0:T(8,128)(2,1)} %get-tuple-element.31), channel_id=1, source_target_pairs={{1,2},{2,1},{5,6},{6,5},{9,10},{10,9},{13,14},{14,13},{17,18},{18,... | collective-permute-start | bytes 663560 | tf_op jit(solution)/shard_map/ppermute | solution.py:607
  78.0 9.6 %collective-permute-done.2.refs_2_ = bf16[864,256]{1,0:T(8,128)(2,1)S(1)} collective-permute-done((bf16[864,256]{1,0:T(8,128)(2,1)}, bf16[864,256]{1,0:T(8,128)(2,1)S(1)}, u32[]{:S(2)}, u32[]{:S(2)}) %collective-permute-start.2) | collective-permute-done | bytes 442400 | tf_op jit(solution)/shard_map/ppermute | solution.py:607
  87.6 1.3 collective-permute-start
  88.9 18.0 %collective-permute-done.3.refs_3_ = bf16[864,256]{1,0:T(8,128)(2,1)S(1)} collective-permute-done((bf16[864,256]{1,0:T(8,128)(2,1)}, bf16[864,256]{1,0:T(8,128)(2,1)S(1)}, u32[]{:S(2)}, u32[]{:S(2)}) %collective-permute-start.3) | collective-permute-done | bytes 442400 | tf_op jit(solution)/shard_map/ppermute | solution.py:607
  107.0 5.3 %collective-permute-start.9 = (bf16[864,128]{1,0:T(8,128)(2,1)}, bf16[864,128]{1,0:T(8,128)(2,1)S(1)}, u32[]{:S(2)}, u32[]{:S(2)}) collective-permute-start(bf16[864,128]{1,0:T(8,128)(2,1)} %get-tuple-element.42), channel_id=1, source_target_pairs={{1,3},{2,0},{5,7},{6,4},{9,11},{10,8},{13,15},{14,12},{17,19},{18,... | collective-permute-start | bytes 663560 | tf_op jit(solution)/shard_map/ppermute | solution.py:607
  112.3 0.0 copy-start
  112.3 3.5 %copy-done = f32[2560,864]{0,1:T(8,128)S(1)} copy-done((f32[2560,864]{0,1:T(8,128)S(1)}, f32[2560,864]{0,1:T(8,128)}, u32[]{:S(2)}) %copy-start) | copy-done | bytes 8847384
  115.8 0.0 copy-start.2
  115.8 0.0 copy-start.3
  115.8 4.9 %update.1 = f32[864,2560]{1,0:T(8,128)} custom-call(f32[864,2560]{1,0:T(8,128)S(1)} %bitcast.4, bf16[864,256]{1,0:T(8,128)(2,1)S(1)} %get-tuple-element.26.right_ref, bf16[256,2560]{1,0:T(8,128)(2,1)S(1)} %get-tuple-element.27.left_ref), custom_call_target="tpu_custom_call" | custom-call | flops 1132462080 | bytes 17694720 | tf_op jit(solution)/shard_map/update/pallas_call | solution.py:513
  120.7 0.0 copy-done.2
  120.7 0.0 copy-done.3
  120.7 3.1 %final.2.refs_8_ = bf16[640,3456]{1,0:T(8,128)(2,1)} custom-call(s32[1]{0:T(128)} %bitcast.2.refs_0_, f32[864,2560]{1,0:T(8,128)S(1)} %bitcast.5, bf16[864,256]{1,0:T(8,128)(2,1)S(1)} %collective-permute-done.5.refs_2_, bf16[864,256]{1,0:T(8,128)(2,1)S(1)} %collective-permute-done.6.refs_3_, bf16[864,256]{1,0:T(8,128)(2,1)S(1)} %collective-permute-done.7.refs_4_, ...), custom_call_target="tpu_custom_call" | custom-call | flops 679477248 | bytes 5308416 | tf_op jit(solution)/shard_map/final/pallas_call | solution.py:364
  123.8 0.0 copy-start.5
  123.8 0.0 copy-start.6
  123.8 0.0 collective-permute-done.4.refs_4_
  123.8 3.1 %final.3.refs_6_ = bf16[640,3456]{1,0:T(8,128)(2,1)} custom-call(s32[1]{0:T(128)} %bitcast.2.refs_0_, f32[864,2560]{1,0:T(8,128)S(1)} %bitcast.6, bf16[864,256]{1,0:T(8,128)(2,1)S(1)} %collective-permute-done.2.refs_2_, bf16[864,256]{1,0:T(8,128)(2,1)S(1)} %collective-permute-done.3.refs_3_, ...), custom_call_target="tpu_custom_call", output_to_operand_aliasing={{}: (8, {})} | custom-call | flops 679477248 | bytes 5308416 | tf_op jit(solution)/shard_map/final/pallas_call | solution.py:364
  126.9 0.0 collective-permute-done.1.refs_4_
  126.9 0.0 collective-permute-done.refs_1_
  126.9 0.0 copy-done.5
  126.9 0.0 copy-done.6
  126.9 1.4 %lead.1 = (bf16[640,3456]{1,0:T(8,128)(2,1)}, f32[128,3456]{1,0:T(8,128)S(1)}) custom-call(f32[864,2560]{1,0:T(8,128)S(1)} %bitcast.7, bf16[864,128]{1,0:T(8,128)(2,1)S(1)} %collective-permute-done.refs_1_, bf16[864,128]{1,0:T(8,128)(2,1)S(1)} %copy-done.6, bf16[864,128]{1,0:T(8,128)(2,1)S(1)} %copy-done.5, ...), custom_call_target="tpu_custom_call", output_to_operand_aliasing={{0}: (6, {})} | custom-call | flops 113246208 | bytes 2654208 | tf_op jit(solution)/shard_map/lead/pallas_call | solution.py:432
  128.4 0.0 collective-permute-done.8.refs_1_
  128.4 0.0 collective-permute-done.9.refs_2_
  128.4 1.0 last.1
Async XLA Ops:
  42.0 19.8 %collective-permute-start.5 = (bf16[864,256]{1,0:T(8,128)(2,1)}, bf16[864,256]{1,0:T(8,128)(2,1)S(1)}, u32[]{:S(2)}, u32[]{:S(2)}) collective-permute-start(bf16[864,256]{1,0:T(8,128)(2,1)} %get-tuple-element.38), channel_id=1, source_target_pairs={{0,1},{1,0},{2,3},{3,2},{4,5},{5,4},{6,7},{7,6},{8,9},{9,8},{10,11... | collective-permute-start | bytes 1327112 | tf_op jit(solution)/shard_map/ppermute | solution.py:607
  42.1 31.7 %collective-permute-start.6 = (bf16[864,256]{1,0:T(8,128)(2,1)}, bf16[864,256]{1,0:T(8,128)(2,1)S(1)}, u32[]{:S(2)}, u32[]{:S(2)}) collective-permute-start(bf16[864,256]{1,0:T(8,128)(2,1)} %get-tuple-element.39), channel_id=1, source_target_pairs={{1,3},{2,0},{0,2},{3,1},{5,7},{6,4},{4,6},{7,5},{9,11},{10,8},{8,1... | collective-permute-start | bytes 1327112 | tf_op jit(solution)/shard_map/ppermute | solution.py:607
  44.0 30.4 %collective-permute-start.7 = (bf16[864,256]{1,0:T(8,128)(2,1)}, bf16[864,256]{1,0:T(8,128)(2,1)S(1)}, u32[]{:S(2)}, u32[]{:S(2)}) collective-permute-start(bf16[864,256]{1,0:T(8,128)(2,1)} %get-tuple-element.40), channel_id=1, source_target_pairs={{0,3},{3,0},{4,7},{7,4},{8,11},{11,8},{12,15},{15,12},{16,19},{19,... | collective-permute-start | bytes 1327112 | tf_op jit(solution)/shard_map/ppermute | solution.py:607
  44.7 42.9 %collective-permute-start.2 = (bf16[864,256]{1,0:T(8,128)(2,1)}, bf16[864,256]{1,0:T(8,128)(2,1)S(1)}, u32[]{:S(2)}, u32[]{:S(2)}) collective-permute-start(bf16[864,256]{1,0:T(8,128)(2,1)} %get-tuple-element.33), channel_id=1, source_target_pairs={{0,1},{1,0},{2,3},{3,2},{4,5},{5,4},{6,7},{7,6},{8,9},{9,8},{10,11... | collective-permute-start | bytes 1327112 | tf_op jit(solution)/shard_map/ppermute | solution.py:607
  48.5 58.4 %collective-permute-start.3 = (bf16[864,256]{1,0:T(8,128)(2,1)}, bf16[864,256]{1,0:T(8,128)(2,1)S(1)}, u32[]{:S(2)}, u32[]{:S(2)}) collective-permute-start(bf16[864,256]{1,0:T(8,128)(2,1)} %get-tuple-element.34), channel_id=1, source_target_pairs={{1,3},{2,0},{0,2},{3,1},{5,7},{6,4},{4,6},{7,5},{9,11},{10,8},{8,1... | collective-permute-start | bytes 1327112 | tf_op jit(solution)/shard_map/ppermute | solution.py:607
  61.9 61.9 %collective-permute-start.4 = (bf16[864,256]{1,0:T(8,128)(2,1)}, bf16[864,256]{1,0:T(8,128)(2,1)S(1)}, u32[]{:S(2)}, u32[]{:S(2)}) collective-permute-start(bf16[864,256]{1,0:T(8,128)(2,1)} %get-tuple-element.35), channel_id=1, source_target_pairs={{0,3},{3,0},{4,7},{7,4},{8,11},{11,8},{12,15},{15,12},{16,19},{19,... | collective-permute-start | bytes 1327112 | tf_op jit(solution)/shard_map/ppermute | solution.py:607
  62.6 1.5 %copy-start.1 = (bf16[256,3456]{1,0:T(8,128)(2,1)S(1)}, bf16[256,3456]{1,0:T(8,128)(2,1)}, u32[]{:S(2)}) copy-start(bf16[256,3456]{1,0:T(8,128)(2,1)} %get-tuple-element.24.refs_1_.refs_7_) | copy-start | bytes 5308420
  64.0 1.3 %copy-start.4 = (bf16[256,2560]{1,0:T(8,128)(2,1)S(1)}, bf16[256,2560]{1,0:T(8,128)(2,1)}, u32[]{:S(2)}) copy-start(bf16[256,2560]{1,0:T(8,128)(2,1)} %get-tuple-element.23.refs_0_) | copy-start | bytes 3932164
  65.3 0.7 copy-start.7
  73.8 53.1 %collective-permute-start.1 = (bf16[864,128]{1,0:T(8,128)(2,1)}, bf16[864,128]{1,0:T(8,128)(2,1)S(1)}, u32[]{:S(2)}, u32[]{:S(2)}) collective-permute-start(bf16[864,128]{1,0:T(8,128)(2,1)} %get-tuple-element.31), channel_id=1, source_target_pairs={{0,3},{3,0},{4,7},{7,4},{8,11},{11,8},{12,15},{15,12},{16,19},{19,... | collective-permute-start | bytes 663560 | tf_op jit(solution)/shard_map/ppermute | solution.py:607
  74.5 53.9 %collective-permute-start.8 = (bf16[864,128]{1,0:T(8,128)(2,1)}, bf16[864,128]{1,0:T(8,128)(2,1)S(1)}, u32[]{:S(2)}, u32[]{:S(2)}) collective-permute-start(bf16[864,128]{1,0:T(8,128)(2,1)} %get-tuple-element.31), channel_id=1, source_target_pairs={{1,2},{2,1},{5,6},{6,5},{9,10},{10,9},{13,14},{14,13},{17,18},{18,... | collective-permute-start | bytes 663560 | tf_op jit(solution)/shard_map/ppermute | solution.py:607
  87.6 39.3 %collective-permute-start = (bf16[864,128]{1,0:T(8,128)(2,1)}, bf16[864,128]{1,0:T(8,128)(2,1)S(1)}, u32[]{:S(2)}, u32[]{:S(2)}) collective-permute-start(bf16[864,128]{1,0:T(8,128)(2,1)} %get-tuple-element.28), channel_id=1, source_target_pairs={{0,1},{3,2},{4,5},{7,6},{8,9},{11,10},{12,13},{15,14},{16,17},{19,... | collective-permute-start | bytes 663560 | tf_op jit(solution)/shard_map/ppermute | solution.py:607
  107.0 21.4 %collective-permute-start.9 = (bf16[864,128]{1,0:T(8,128)(2,1)}, bf16[864,128]{1,0:T(8,128)(2,1)S(1)}, u32[]{:S(2)}, u32[]{:S(2)}) collective-permute-start(bf16[864,128]{1,0:T(8,128)(2,1)} %get-tuple-element.42), channel_id=1, source_target_pairs={{1,3},{2,0},{5,7},{6,4},{9,11},{10,8},{13,15},{14,12},{17,19},{18,... | collective-permute-start | bytes 663560 | tf_op jit(solution)/shard_map/ppermute | solution.py:607
  112.3 3.5 %copy-start = (f32[2560,864]{0,1:T(8,128)S(1)}, f32[2560,864]{0,1:T(8,128)}, u32[]{:S(2)}) copy-start(f32[2560,864]{0,1:T(8,128)} %param.4) | copy-start | bytes 26542084
  115.8 4.9 %copy-start.2 = (bf16[256,3456]{1,0:T(8,128)(2,1)S(1)}, bf16[256,3456]{1,0:T(8,128)(2,1)}, u32[]{:S(2)}) copy-start(bf16[256,3456]{1,0:T(8,128)(2,1)} %get-tuple-element.24.refs_1_.refs_7_) | copy-start | bytes 5308420
  115.8 4.9 %copy-start.3 = (bf16[864,512]{1,0:T(8,128)(2,1)S(1)}, bf16[864,512]{1,0:T(8,128)(2,1)}, u32[]{:S(2)}) copy-start(bf16[864,512]{1,0:T(8,128)(2,1)} %get-tuple-element.36.refs_5_) | copy-start | bytes 2654212
  123.8 3.1 %copy-start.5 = (bf16[864,128]{1,0:T(8,128)(2,1)S(1)}, bf16[864,128]{1,0:T(8,128)(2,1)}, u32[]{:S(2)}) copy-start(bf16[864,128]{1,0:T(8,128)(2,1)} %get-tuple-element.30.refs_3_) | copy-start | bytes 663556
  123.8 3.1 %copy-start.6 = (bf16[864,128]{1,0:T(8,128)(2,1)S(1)}, bf16[864,128]{1,0:T(8,128)(2,1)}, u32[]{:S(2)}) copy-start(bf16[864,128]{1,0:T(8,128)(2,1)} %get-tuple-element.29.refs_2_) | copy-start | bytes 663556

commit v5 on v4

--- a/solution.py
+++ b/solution.py
@@ -137,7 +137,7 @@
     pl.semaphore_wait(barrier, 5)
 
     mine = lax.rem(an, 2)
-    halves = 2
+    halves = 4
     count = local // halves
     sources = (an, near, beyond, beyond + 1)
     started = []
@@ -192,7 +192,8 @@
     block = l_slab(an, te)
     start(remote(block, block, q_send.at[0], q_recv.at[1 + mine], {"answer": far}))
     start(remote(block, block, q_send.at[1], q_recv.at[0], {"answer": near}))
-    part_of(1)
+    for h in range(1, halves):
+        part_of(h)
     spread(0)
     for h in range(halves):
         forward(0, h)
@@ -242,7 +243,8 @@
         landed(block, q_recv.at[k - 1])
         relay(block, q_send.at[k], q_recv.at[k - 1])
         spread(k)
-    pass_on(1)
+    for h in range(1, halves):
+        pass_on(h)
     for k in range(answers):
         block = l_slab(sources[k], across)
         landed(block, y_recv.at[k, 0])
@@ -307,8 +309,8 @@
             pltpu.VMEM((2, cols, tile // answers), jnp.float32), pltpu.VMEM((2, cols, tile // answers), half),
             pltpu.VMEM((1, block), jnp.float32),
             dma((4,)), dma((sides,)), dma((sides, len(chunks))), dma((4,)), dma((3,)), dma((4,)), dma((4,)),
-            dma((1,)), dma((1,)), dma((answers, 2)), dma((answers, 2)),
-            dma((4, 2)), dma((3, 2)), dma((4,)), dma((3,)), dma((answers, 3)), dma((answers, 3)),
+            dma((1,)), dma((1,)), dma((answers, 4)), dma((answers, 4)),
+            dma((4, 4)), dma((3, 4)), dma((4,)), dma((3,)), dma((answers, 3)), dma((answers, 3)),
             dma((len(chunks) - 1,)), dma((len(chunks) - 1,)), dma, dma, dma, dma,
         ],
         compiler_params=pltpu.CompilerParams(collective_id=0, has_side_effects=True),
@@ -607,17 +609,15 @@
         got[c, x] = lax.ppermute(blocks[min(x, 3) - 1][c], "answer", some)
     weighted, own, turned, base = weigh(left_tile, right, parts, members, rows, width, chunks[-1])
     new_master = update(transposed, turned, weighted)
-    rollout, at = None, 0
-    for c, size in enumerate(chunks):
-        if c == last:
-            sides = [((1, True), got[c, 1]), ((1, False), aside), ((2, True), cross), ((3, False), got[c, 3])]
-            rollout, mix = lead(transposed, sides, base, at, rollout)
-            rollout = finish(mix, got[c, 4], got[c, 2], at, rollout)
-        else:
-            sides = [((1, None), got[c, 1], 0), ((2, None), got[c, 2], 0),
-                     ((3, False), got[c, 3], 0), ((3, True), early, at // 128)]
-            rollout = finalize(where, transposed, sides, own, right, at, size, rollout)
-        at += size
+    rollout, starts = None, [sum(chunks[:c]) for c in range(len(chunks))]
+    sides = [((1, True), got[last, 1]), ((1, False), aside), ((2, True), cross), ((3, False), got[last, 3])]
+    for c in range(last):
+        picks = [((1, None), got[c, 1], 0), ((2, None), got[c, 2], 0),
+                 ((3, False), got[c, 3], 0), ((3, True), early, starts[c] // 128)]
+        rollout = finalize(where, transposed, picks, own, right, starts[c], chunks[c], rollout)
+        if c == 0:
+            rollout, mix = lead(transposed, sides, base, starts[last], rollout)
+    rollout = finish(mix, got[last, 4], got[last, 2], starts[last], rollout)
     return (new_master.T, rollout)
 
 

time: 130 us -> 126 us (0.969)
  the two profiles are of different devices: /device:TPU:8 before, /device:TPU:0 now
where the time goes in v5:
time: 126 us; the launch traced here: 125 us
  Pallas kernels  52.3 us (42%)
  waiting for transfers between devices  41 us (33%)
  starting transfers between devices  24.4 us (19%)
  local copies, waits for them, and re-layouts  6.98 us (6%)
    ppermute x10, waiting for transfers between devices, fast_body(): got[c, x] = lax.ppermute(blocks[min(x, 3) - 1][c], 'answer', some)  41 us
    pallas_call x1, Pallas kernels, exchange(): pl.pallas_call(lambda *refs: exchange_kernel(members, chunks, *refs), out...  37.7 us
    ppermute x10, starting transfers between devices, fast_body(): got[c, x] = lax.ppermute(blocks[min(x, 3) - 1][c], 'answer', some)  24.4 us
    unnamed x16, local copies, waits for them, and re-layouts  6.98 us
    pallas_call x2, Pallas kernels, finalize(): pl.pallas_call(lambda *refs: final_kernel(picks, *refs), grid_spec=pltpu....  6.16 us
    pallas_call x1, Pallas kernels, update(): pl.pallas_call(update_kernel, grid=(width // chunk,), in_specs=[pl.BlockS...  4.91 us
  transfers between devices with their start and end apart: 10, of which 6 were waited for; matrix products, arithmetic and copies ran while one was open for 0% of the time, Pallas kernels for 11%

profile of v5, /device:TPU:0, one launch (start us, length us, event | category | flops | bytes accessed | tf_op | source)
XLA Modules:
  0.0 125.4 jit_solution(2207401590492809199)
XLA Ops:
  0.6 37.7 %exchange.1 = (bf16[256,2560]{1,0:T(8,128)(2,1)}, bf16[256,3456]{1,0:T(8,128)(2,1)}, f32[8,1,128]{2,1,0:T(1,128)}, f32[1,128]{1,0:T(1,128)}, bf16[864,512]{1,0:T...) custom-call(bf16[32,5120]{1,0:T(8,128)(2,1)} %refs_0_.1, ...), custom_call_target="tpu_custom_call" | custom-call | tf_op jit(solution)/shard_map/exchange/pallas_call | solution.py:293
  38.4 7.9 %collective-permute-start.2 = (bf16[864,256]{1,0:T(8,128)(2,1)}, bf16[864,256]{1,0:T(8,128)(2,1)S(1)}, u32[]{:S(2)}, u32[]{:S(2)}) collective-permute-start(bf16[864,256]{1,0:T(8,128)(2,1)} %get-tuple-element.33), channel_id=1, source_target_pairs={{0,1},{1,0},{2,3},{3,2},{4,5},{5,4},{6,7},{7,6},{8,9},{9,8},{10,11... | collective-permute-start | bytes 1327112 | tf_op jit(solution)/shard_map/ppermute | solution.py:609
  46.2 1.9 %collective-permute-start = (bf16[864,128]{1,0:T(8,128)(2,1)}, bf16[864,128]{1,0:T(8,128)(2,1)S(1)}, u32[]{:S(2)}, u32[]{:S(2)}) collective-permute-start(bf16[864,128]{1,0:T(8,128)(2,1)} %get-tuple-element.28), channel_id=1, source_target_pairs={{0,1},{3,2},{4,5},{7,6},{8,9},{11,10},{12,13},{15,14},{16,17},{19,... | collective-permute-start | bytes 663560 | tf_op jit(solution)/shard_map/ppermute | solution.py:609
  48.2 3.0 %collective-permute-start.1 = (bf16[864,128]{1,0:T(8,128)(2,1)}, bf16[864,128]{1,0:T(8,128)(2,1)S(1)}, u32[]{:S(2)}, u32[]{:S(2)}) collective-permute-start(bf16[864,128]{1,0:T(8,128)(2,1)} %get-tuple-element.31), channel_id=1, source_target_pairs={{0,3},{3,0},{4,7},{7,4},{8,11},{11,8},{12,15},{15,12},{16,19},{19,... | collective-permute-start | bytes 663560 | tf_op jit(solution)/shard_map/ppermute | solution.py:609
  51.2 0.1 collective-permute-start.3
  51.3 4.6 %collective-permute-start.4 = (bf16[864,256]{1,0:T(8,128)(2,1)}, bf16[864,256]{1,0:T(8,128)(2,1)S(1)}, u32[]{:S(2)}, u32[]{:S(2)}) collective-permute-start(bf16[864,256]{1,0:T(8,128)(2,1)} %get-tuple-element.35), channel_id=1, source_target_pairs={{0,3},{3,0},{4,7},{7,4},{8,11},{11,8},{12,15},{15,12},{16,19},{19,... | collective-permute-start | bytes 1327112 | tf_op jit(solution)/shard_map/ppermute | solution.py:609
  55.9 5.9 %collective-permute-done.refs_1_ = bf16[864,128]{1,0:T(8,128)(2,1)S(1)} collective-permute-done((bf16[864,128]{1,0:T(8,128)(2,1)}, bf16[864,128]{1,0:T(8,128)(2,1)S(1)}, u32[]{:S(2)}, u32[]{:S(2)}) %collective-permute-start) | collective-permute-done | bytes 221216 | tf_op jit(solution)/shard_map/ppermute | solution.py:609
  61.8 2.4 %collective-permute-start.7 = (bf16[864,256]{1,0:T(8,128)(2,1)}, bf16[864,256]{1,0:T(8,128)(2,1)S(1)}, u32[]{:S(2)}, u32[]{:S(2)}) collective-permute-start(bf16[864,256]{1,0:T(8,128)(2,1)} %get-tuple-element.40), channel_id=1, source_target_pairs={{0,1},{1,0},{2,3},{3,2},{4,5},{5,4},{6,7},{7,6},{8,9},{9,8},{10,11... | collective-permute-start | bytes 1327112 | tf_op jit(solution)/shard_map/ppermute | solution.py:609
  64.2 3.9 %collective-permute-done.1.refs_4_ = bf16[864,128]{1,0:T(8,128)(2,1)S(1)} collective-permute-done((bf16[864,128]{1,0:T(8,128)(2,1)}, bf16[864,128]{1,0:T(8,128)(2,1)S(1)}, u32[]{:S(2)}, u32[]{:S(2)}) %collective-permute-start.1) | collective-permute-done | bytes 221216 | tf_op jit(solution)/shard_map/ppermute | solution.py:609
  68.1 0.0 collective-permute-start.8
  68.1 2.1 %collective-permute-done.2.refs_2_ = bf16[864,256]{1,0:T(8,128)(2,1)S(1)} collective-permute-done((bf16[864,256]{1,0:T(8,128)(2,1)}, bf16[864,256]{1,0:T(8,128)(2,1)S(1)}, u32[]{:S(2)}, u32[]{:S(2)}) %collective-permute-start.2) | collective-permute-done | bytes 442400 | tf_op jit(solution)/shard_map/ppermute | solution.py:609
  70.2 2.6 %collective-permute-start.9 = (bf16[864,256]{1,0:T(8,128)(2,1)}, bf16[864,256]{1,0:T(8,128)(2,1)S(1)}, u32[]{:S(2)}, u32[]{:S(2)}) collective-permute-start(bf16[864,256]{1,0:T(8,128)(2,1)} %get-tuple-element.42), channel_id=1, source_target_pairs={{0,3},{3,0},{4,7},{7,4},{8,11},{11,8},{12,15},{15,12},{16,19},{19,... | collective-permute-start | bytes 1327112 | tf_op jit(solution)/shard_map/ppermute | solution.py:609
  72.8 0.0 copy-start.1
  72.8 1.5 %copy-done.1 = bf16[256,3456]{1,0:T(8,128)(2,1)S(1)} copy-done((bf16[256,3456]{1,0:T(8,128)(2,1)S(1)}, bf16[256,3456]{1,0:T(8,128)(2,1)}, u32[]{:S(2)}) %copy-start.1) | copy-done | bytes 1769496
  74.2 0.0 copy-start.4
  74.3 1.3 %copy-done.4 = bf16[256,2560]{1,0:T(8,128)(2,1)S(1)} copy-done((bf16[256,2560]{1,0:T(8,128)(2,1)S(1)}, bf16[256,2560]{1,0:T(8,128)(2,1)}, u32[]{:S(2)}) %copy-start.4) | copy-done | bytes 1310744
  75.6 0.0 copy-start.7
  75.6 0.7 copy-done.7
  76.2 1.1 weigh.1
  77.3 10.7 %collective-permute-done.3.refs_3_ = bf16[864,256]{1,0:T(8,128)(2,1)S(1)} collective-permute-done((bf16[864,256]{1,0:T(8,128)(2,1)}, bf16[864,256]{1,0:T(8,128)(2,1)S(1)}, u32[]{:S(2)}, u32[]{:S(2)}) %collective-permute-start.3) | collective-permute-done | bytes 442400 | tf_op jit(solution)/shard_map/ppermute | solution.py:609
  88.0 0.7 collective-permute-start.5
  88.7 0.0 collective-permute-done.4.refs_4_
  88.7 1.3 %collective-permute-start.6 = (bf16[864,128]{1,0:T(8,128)(2,1)}, bf16[864,128]{1,0:T(8,128)(2,1)S(1)}, u32[]{:S(2)}, u32[]{:S(2)}) collective-permute-start(bf16[864,128]{1,0:T(8,128)(2,1)} %get-tuple-element.39), channel_id=1, source_target_pairs={{1,3},{2,0},{5,7},{6,4},{9,11},{10,8},{13,15},{14,12},{17,19},{18,... | collective-permute-start | bytes 663560 | tf_op jit(solution)/shard_map/ppermute | solution.py:609
  90.0 0.0 copy-start
  90.0 3.5 %copy-done = f32[2560,864]{0,1:T(8,128)S(1)} copy-done((f32[2560,864]{0,1:T(8,128)S(1)}, f32[2560,864]{0,1:T(8,128)}, u32[]{:S(2)}) %copy-start) | copy-done | bytes 8847384
  93.5 0.0 copy-start.2
  93.5 0.0 copy-start.3
  93.5 4.9 %update.1 = f32[864,2560]{1,0:T(8,128)} custom-call(f32[864,2560]{1,0:T(8,128)S(1)} %bitcast.4, bf16[864,256]{1,0:T(8,128)(2,1)S(1)} %get-tuple-element.26.right_ref, bf16[256,2560]{1,0:T(8,128)(2,1)S(1)} %get-tuple-element.27.left_ref), custom_call_target="tpu_custom_call" | custom-call | flops 1132462080 | bytes 17694720 | tf_op jit(solution)/shard_map/update/pallas_call | solution.py:515
  98.5 0.0 copy-done.2
  98.5 0.0 copy-done.3
  98.5 0.0 copy-start.5
  98.5 0.0 copy-start.6
  98.5 3.1 %final.2.refs_6_ = bf16[640,3456]{1,0:T(8,128)(2,1)} custom-call(s32[1]{0:T(128)} %bitcast.2.refs_0_, f32[864,2560]{1,0:T(8,128)S(1)} %bitcast.5, bf16[864,256]{1,0:T(8,128)(2,1)S(1)} %collective-permute-done.2.refs_2_, bf16[864,256]{1,0:T(8,128)(2,1)S(1)} %collective-permute-done.3.refs_3_, bf16[864,256]{1,0:T(8,128)(2,1)S(1)} %collective-permute-done.4.refs_4_, ...), custom_call_target="tpu_custom_call" | custom-call | flops 679477248 | bytes 5308416 | tf_op jit(solution)/shard_map/final/pallas_call | solution.py:366
  101.5 0.0 copy-done.5
  101.5 0.0 copy-done.6
  101.5 1.4 %lead.1 = (bf16[640,3456]{1,0:T(8,128)(2,1)}, f32[128,3456]{1,0:T(8,128)S(1)}) custom-call(f32[864,2560]{1,0:T(8,128)S(1)} %bitcast.6, bf16[864,128]{1,0:T(8,128)(2,1)S(1)} %collective-permute-done.refs_1_, bf16[864,128]{1,0:T(8,128)(2,1)S(1)} %copy-done.6, bf16[864,128]{1,0:T(8,128)(2,1)S(1)} %copy-done.5, ...), custom_call_target="tpu_custom_call", output_to_operand_aliasing={{0}: (6, {})} | custom-call | flops 113246208 | bytes 2654208 | tf_op jit(solution)/shard_map/lead/pallas_call | solution.py:434
  103.0 0.0 collective-permute-done.7.refs_2_
  103.0 13.4 %collective-permute-done.8.refs_3_ = bf16[864,256]{1,0:T(8,128)(2,1)S(1)} collective-permute-done((bf16[864,256]{1,0:T(8,128)(2,1)}, bf16[864,256]{1,0:T(8,128)(2,1)S(1)}, u32[]{:S(2)}, u32[]{:S(2)}) %collective-permute-start.8) | collective-permute-done | bytes 442400 | tf_op jit(solution)/shard_map/ppermute | solution.py:609
  116.4 0.0 collective-permute-done.9.refs_4_
  116.4 3.1 %final.3.refs_3_ = bf16[640,3456]{1,0:T(8,128)(2,1)} custom-call(s32[1]{0:T(128)} %bitcast.2.refs_0_, f32[864,2560]{1,0:T(8,128)S(1)} %bitcast.7, bf16[864,256]{1,0:T(8,128)(2,1)S(1)} %collective-permute-done.7.refs_2_, bf16[864,256]{1,0:T(8,128)(2,1)S(1)} %collective-permute-done.8.refs_3_, ...), custom_call_target="tpu_custom_call", output_to_operand_aliasing={{}: (8, {})} | custom-call | flops 679477248 | bytes 5308416 | tf_op jit(solution)/shard_map/final/pallas_call | solution.py:366
  119.5 4.9 %collective-permute-done.6.refs_2_ = bf16[864,128]{1,0:T(8,128)(2,1)S(1)} collective-permute-done((bf16[864,128]{1,0:T(8,128)(2,1)}, bf16[864,128]{1,0:T(8,128)(2,1)S(1)}, u32[]{:S(2)}, u32[]{:S(2)}) %collective-permute-start.6) | collective-permute-done | bytes 221216 | tf_op jit(solution)/shard_map/ppermute | solution.py:609
  124.4 0.0 collective-permute-done.5.refs_1_
  124.4 1.0 last.1
Async XLA Ops:
  38.4 31.8 %collective-permute-start.2 = (bf16[864,256]{1,0:T(8,128)(2,1)}, bf16[864,256]{1,0:T(8,128)(2,1)S(1)}, u32[]{:S(2)}, u32[]{:S(2)}) collective-permute-start(bf16[864,256]{1,0:T(8,128)(2,1)} %get-tuple-element.33), channel_id=1, source_target_pairs={{0,1},{1,0},{2,3},{3,2},{4,5},{5,4},{6,7},{7,6},{8,9},{9,8},{10,11... | collective-permute-start | bytes 1327112 | tf_op jit(solution)/shard_map/ppermute | solution.py:609
  46.2 15.6 %collective-permute-start = (bf16[864,128]{1,0:T(8,128)(2,1)}, bf16[864,128]{1,0:T(8,128)(2,1)S(1)}, u32[]{:S(2)}, u32[]{:S(2)}) collective-permute-start(bf16[864,128]{1,0:T(8,128)(2,1)} %get-tuple-element.28), channel_id=1, source_target_pairs={{0,1},{3,2},{4,5},{7,6},{8,9},{11,10},{12,13},{15,14},{16,17},{19,... | collective-permute-start | bytes 663560 | tf_op jit(solution)/shard_map/ppermute | solution.py:609
  48.2 20.0 %collective-permute-start.1 = (bf16[864,128]{1,0:T(8,128)(2,1)}, bf16[864,128]{1,0:T(8,128)(2,1)S(1)}, u32[]{:S(2)}, u32[]{:S(2)}) collective-permute-start(bf16[864,128]{1,0:T(8,128)(2,1)} %get-tuple-element.31), channel_id=1, source_target_pairs={{0,3},{3,0},{4,7},{7,4},{8,11},{11,8},{12,15},{15,12},{16,19},{19,... | collective-permute-start | bytes 663560 | tf_op jit(solution)/shard_map/ppermute | solution.py:609
  51.2 36.9 %collective-permute-start.3 = (bf16[864,256]{1,0:T(8,128)(2,1)}, bf16[864,256]{1,0:T(8,128)(2,1)S(1)}, u32[]{:S(2)}, u32[]{:S(2)}) collective-permute-start(bf16[864,256]{1,0:T(8,128)(2,1)} %get-tuple-element.34), channel_id=1, source_target_pairs={{1,3},{2,0},{0,2},{3,1},{5,7},{6,4},{4,6},{7,5},{9,11},{10,8},{8,1... | collective-permute-start | bytes 1327112 | tf_op jit(solution)/shard_map/ppermute | solution.py:609
  51.3 37.5 %collective-permute-start.4 = (bf16[864,256]{1,0:T(8,128)(2,1)}, bf16[864,256]{1,0:T(8,128)(2,1)S(1)}, u32[]{:S(2)}, u32[]{:S(2)}) collective-permute-start(bf16[864,256]{1,0:T(8,128)(2,1)} %get-tuple-element.35), channel_id=1, source_target_pairs={{0,3},{3,0},{4,7},{7,4},{8,11},{11,8},{12,15},{15,12},{16,19},{19,... | collective-permute-start | bytes 1327112 | tf_op jit(solution)/shard_map/ppermute | solution.py:609
  61.8 41.1 %collective-permute-start.7 = (bf16[864,256]{1,0:T(8,128)(2,1)}, bf16[864,256]{1,0:T(8,128)(2,1)S(1)}, u32[]{:S(2)}, u32[]{:S(2)}) collective-permute-start(bf16[864,256]{1,0:T(8,128)(2,1)} %get-tuple-element.40), channel_id=1, source_target_pairs={{0,1},{1,0},{2,3},{3,2},{4,5},{5,4},{6,7},{7,6},{8,9},{9,8},{10,11... | collective-permute-start | bytes 1327112 | tf_op jit(solution)/shard_map/ppermute | solution.py:609
  68.1 48.3 %collective-permute-start.8 = (bf16[864,256]{1,0:T(8,128)(2,1)}, bf16[864,256]{1,0:T(8,128)(2,1)S(1)}, u32[]{:S(2)}, u32[]{:S(2)}) collective-permute-start(bf16[864,256]{1,0:T(8,128)(2,1)} %get-tuple-element.41), channel_id=1, source_target_pairs={{1,3},{2,0},{0,2},{3,1},{5,7},{6,4},{4,6},{7,5},{9,11},{10,8},{8,1... | collective-permute-start | bytes 1327112 | tf_op jit(solution)/shard_map/ppermute | solution.py:609
  70.2 46.2 %collective-permute-start.9 = (bf16[864,256]{1,0:T(8,128)(2,1)}, bf16[864,256]{1,0:T(8,128)(2,1)S(1)}, u32[]{:S(2)}, u32[]{:S(2)}) collective-permute-start(bf16[864,256]{1,0:T(8,128)(2,1)} %get-tuple-element.42), channel_id=1, source_target_pairs={{0,3},{3,0},{4,7},{7,4},{8,11},{11,8},{12,15},{15,12},{16,19},{19,... | collective-permute-start | bytes 1327112 | tf_op jit(solution)/shard_map/ppermute | solution.py:609
  72.8 1.5 %copy-start.1 = (bf16[256,3456]{1,0:T(8,128)(2,1)S(1)}, bf16[256,3456]{1,0:T(8,128)(2,1)}, u32[]{:S(2)}) copy-start(bf16[256,3456]{1,0:T(8,128)(2,1)} %get-tuple-element.24.refs_1_.refs_7_) | copy-start | bytes 5308420
  74.2 1.3 %copy-start.4 = (bf16[256,2560]{1,0:T(8,128)(2,1)S(1)}, bf16[256,2560]{1,0:T(8,128)(2,1)}, u32[]{:S(2)}) copy-start(bf16[256,2560]{1,0:T(8,128)(2,1)} %get-tuple-element.23.refs_0_) | copy-start | bytes 3932164
  75.6 0.7 copy-start.7
  88.0 36.4 %collective-permute-start.5 = (bf16[864,128]{1,0:T(8,128)(2,1)}, bf16[864,128]{1,0:T(8,128)(2,1)S(1)}, u32[]{:S(2)}, u32[]{:S(2)}) collective-permute-start(bf16[864,128]{1,0:T(8,128)(2,1)} %get-tuple-element.31), channel_id=1, source_target_pairs={{1,2},{2,1},{5,6},{6,5},{9,10},{10,9},{13,14},{14,13},{17,18},{18,... | collective-permute-start | bytes 663560 | tf_op jit(solution)/shard_map/ppermute | solution.py:609
  88.7 35.7 %collective-permute-start.6 = (bf16[864,128]{1,0:T(8,128)(2,1)}, bf16[864,128]{1,0:T(8,128)(2,1)S(1)}, u32[]{:S(2)}, u32[]{:S(2)}) collective-permute-start(bf16[864,128]{1,0:T(8,128)(2,1)} %get-tuple-element.39), channel_id=1, source_target_pairs={{1,3},{2,0},{5,7},{6,4},{9,11},{10,8},{13,15},{14,12},{17,19},{18,... | collective-permute-start | bytes 663560 | tf_op jit(solution)/shard_map/ppermute | solution.py:609
  90.0 3.5 %copy-start = (f32[2560,864]{0,1:T(8,128)S(1)}, f32[2560,864]{0,1:T(8,128)}, u32[]{:S(2)}) copy-start(f32[2560,864]{0,1:T(8,128)} %param.4) | copy-start | bytes 26542084
  93.5 4.9 %copy-start.2 = (bf16[256,3456]{1,0:T(8,128)(2,1)S(1)}, bf16[256,3456]{1,0:T(8,128)(2,1)}, u32[]{:S(2)}) copy-start(bf16[256,3456]{1,0:T(8,128)(2,1)} %get-tuple-element.24.refs_1_.refs_7_) | copy-start | bytes 5308420
  93.5 4.9 %copy-start.3 = (bf16[864,512]{1,0:T(8,128)(2,1)S(1)}, bf16[864,512]{1,0:T(8,128)(2,1)}, u32[]{:S(2)}) copy-start(bf16[864,512]{1,0:T(8,128)(2,1)} %get-tuple-element.36.refs_5_) | copy-start | bytes 2654212
  98.5 3.1 %copy-start.5 = (bf16[864,128]{1,0:T(8,128)(2,1)S(1)}, bf16[864,128]{1,0:T(8,128)(2,1)}, u32[]{:S(2)}) copy-start(bf16[864,128]{1,0:T(8,128)(2,1)} %get-tuple-element.30.refs_3_) | copy-start | bytes 663556
  98.5 3.1 %copy-start.6 = (bf16[864,128]{1,0:T(8,128)(2,1)S(1)}, bf16[864,128]{1,0:T(8,128)(2,1)}, u32[]{:S(2)}) copy-start(bf16[864,128]{1,0:T(8,128)(2,1)} %get-tuple-element.29.refs_2_) | copy-start | bytes 663556
